TPU v7x, 32 devices: a whole 2x2x4 slice. The times are simulated.
32 devices in a mesh: groups: 2 (over y), space: 16 (over z, x, core).
Axes of the slice: x: 2, y: 2, z: 4, core: 2. Of those that a mesh axis runs over, the one named last changes fastest.
Arguments:
- wavefield: bfloat16 [8192, 1024], P(('groups', 'space')), parts along dimension 0, may hold values from -6 to 6
- redatum_taps: float32 [512, 65], P('groups'), parts along dimension 0, may hold values from -0.75 to 0.75
- cell_x: int32 [5, 16384], replicated, may hold values from 0 to 4095
- cell_depth: int32 [16384], replicated, may hold values from 1 to 511
- slowness: float32 [4], replicated, may hold values from 0.02 to 0.2
- illumination: float32 [32768], P('groups'), parts along dimension 0, may hold values from 0.3 to 3
- aperture: int32 [8192, 1024], P(('groups', 'space')), parts along dimension 0, may hold values 0 or 1
Outputs:
- image: float32 [32, 1024], P(('groups', 'space')), parts along dimension 0
There are 2 independent parts, one for each index of `groups`. A program takes and returns all parts, laid end to end along the dimension named above; an argument that names none is the same for every part. Nothing has to cross between parts.
All inputs are finite; a program needn't handle non-finite values. No bound on the sum of `aperture` on one device may be relied on, other than what follows from the above.
Results may differ from a plain program's by a relative error of at most 0.0075.
Values may be sent and summed in bfloat16 or wider, within the bound.
No kernel may reach another device: no remote copies, remote signals or barrier semaphores. Data moves between devices by JAX's collectives and lax.ppermute only.
A program may use at most 64 MiB of HBM per device.

v0:
```python
import functools
import math

import jax
import jax.numpy as jnp
from jax import lax
from jax.experimental import pallas as pl
from jax.experimental.pallas import tpu as pltpu
from jax.sharding import PartitionSpec as P


LEVELS = 4
BOXES = 16
LANES = 128

POLY_A = -0.55846636
POLY_B = 0.08535978
SCALE = -73.58594804
VMEM = pl.BlockSpec(memory_space=pltpu.VMEM)
GRANT = 56 << 20
ANY = pl.BlockSpec(memory_space=pl.ANY)
HBM = pl.BlockSpec(memory_space=pltpu.HBM)
SMEM = pl.BlockSpec(memory_space=pltpu.SMEM)


def params(mib):
    return pltpu.CompilerParams(vmem_limit_bytes=mib << 20)


def cost(flops, moved, transcendentals=0):
    return pl.CostEstimate(flops=flops, bytes_accessed=moved, transcendentals=transcendentals)


def across(shard, axis, blocks):
    devices = lax.axis_size(axis)
    shift = [blocks if i // blocks % 2 else -blocks for i in range(devices)]
    pairs = [(i, i + by) for i, by in enumerate(shift) if 0 <= i + by < devices]
    return lax.ppermute(shard, axis, pairs)


def partner(shard, axis, bit):
    return lax.ppermute(shard, axis, [(i, i ^ 1 << bit) for i in range(lax.axis_size(axis))])


def cosine(squared):
    u = squared * lax.rsqrt(squared)
    r = u - jnp.round(u)
    w = jnp.abs(r) - 0.25
    q = w * w
    return w * ((q + POLY_A) * q + POLY_B)


def boxes_of(level, blocks):
    box = lax.axis_index("space") // blocks
    bit = 1 << level
    upper = (box // bit) % 2
    return box, box + bit - 2 * bit * upper


ROW, OTHER_ROW, COLUMN, BELOW, OTHER_COLUMN, OTHER_BELOW, WEIGHT, OTHER_WEIGHT = range(8)


def prepare_kernel(blocks, wave, cell_x, depth, illumination, slowness, *refs):
    near_edge, far_edge, coords, cells, depths, lights, slow, sems = refs
    width = wave.shape[1]
    tall = width // LANES
    box = boxes_of(0, blocks)[0]
    others = [boxes_of(level, blocks)[1] for level in range(LEVELS)]
    copies = [pltpu.make_async_copy(slowness, slow, sems.at[0])]
    for k, which in enumerate([box] + others):
        at = pl.ds(pl.multiple_of(which * width, width), width)
        copies.append(pltpu.make_async_copy(cell_x.at[:, at], cells.at[k], sems.at[1 + k]))
    for k, which in enumerate((box, others[-1])):
        at = pl.ds(pl.multiple_of(which * tall, tall), tall)
        copies.append(pltpu.make_async_copy(depth.at[at, :], depths.at[k], sems.at[6 + k]))
        light = illumination.at[at, :]
        copies.append(pltpu.make_async_copy(light, lights.at[k], sems.at[10 + k]))
    end = width - LANES
    even = 1 - box % 2
    first = pl.ds(pl.multiple_of(even * end, LANES), LANES)
    second = pl.ds(pl.multiple_of((1 - even) * end, LANES), LANES)
    late = [
        pltpu.make_async_copy(wave.at[:, first], near_edge, sems.at[8]),
        pltpu.make_async_copy(wave.at[:, second], far_edge, sems.at[9]),
    ]
    for copy in copies + late:
        copy.start()
    for copy in copies:
        copy.wait()
    coords[...] = jnp.zeros_like(coords)
    for level in range(LEVELS):
        turns = slow[level] * (0.5 / math.pi)
        base = 8 * level

        def put(kind, source, row):
            coords[base + kind : base + kind + 1, :] = (
                cells[source, row : row + 1, :].astype(jnp.float32) * turns
            )

        def put_below(kind, source):
            for k in range(tall):
                part = depths[source, k : k + 1, :].astype(jnp.float32) * turns
                coords[base + kind : base + kind + 1, k * LANES : (k + 1) * LANES] = part * part

        put(ROW, 0, level)
        put(OTHER_ROW, 1 + level, level)
        put(COLUMN, 0, level + 1)
        put_below(BELOW, 0)
        if level + 1 == LEVELS:
            put(OTHER_COLUMN, LEVELS, level + 1)
            put_below(OTHER_BELOW, 1)
    share = 1.0 / math.sqrt(wave.shape[0] * blocks)
    base = 8 * (LEVELS - 1)
    for source, kind in enumerate((WEIGHT, OTHER_WEIGHT)):
        for k in range(tall):
            coords[base + kind : base + kind + 1, k * LANES : (k + 1) * LANES] = (
                lights[source, k : k + 1, :] * share
            )
    for copy in late:
        copy.wait()


def mark_kernel(aperture, mask):
    mask[...] = (aperture[...] > 0).astype(jnp.float32).astype(jnp.bfloat16)


def mark(aperture):
    return pl.pallas_call(
        mark_kernel,
        out_shape=jax.ShapeDtypeStruct(aperture.shape, jnp.bfloat16),
        in_specs=[VMEM],
        out_specs=VMEM,
        compiler_params=params(4),
        cost_estimate=cost(aperture.size * 200, aperture.size * 6),
        name="mark",
    )(aperture)


def prepare(blocks, wave, cell_x, depth, illumination, slowness):
    count, width = wave.shape
    levels = cell_x.shape[0]
    edge = jax.ShapeDtypeStruct((count, LANES), wave.dtype)
    return pl.pallas_call(
        functools.partial(prepare_kernel, blocks),
        out_shape=(
            edge,
            edge,
            jax.ShapeDtypeStruct((8 * LEVELS, width), jnp.float32),
        ),
        in_specs=[HBM] * 5,
        out_specs=(VMEM,) * 3,
        scratch_shapes=[
            pltpu.VMEM((1 + LEVELS, levels, width), jnp.int32),
            pltpu.VMEM((2, width // LANES, LANES), jnp.int32),
            pltpu.VMEM((2, width // LANES, LANES), jnp.float32),
            pltpu.SMEM((LEVELS,), jnp.float32),
            pltpu.SemaphoreType.DMA((12,)),
        ],
        compiler_params=pltpu.CompilerParams(vmem_limit_bytes=GRANT),
        cost_estimate=cost(24 * 2 * width * width * 15, count * width * 8),
        name="prepare",
    )(wave, cell_x, depth, illumination, slowness)


def tables_kernel(jobs, step, coords, *refs):
    outs, rows = refs[-1 - len(jobs) : -1], refs[-1]
    width = outs[0].shape[0]
    steps = width // step

    def fill(slot, row, i):
        at = pl.ds(pl.multiple_of(i * step, step), step)
        rows[slot] = jnp.broadcast_to(coords[row : row + 1, at], (LANES, step)).T

    for (row, column, below), out in zip(jobs, outs):
        fill(0, row, 0)

        @pl.loop(0, steps)
        def _(i):
            at = pl.ds(pl.multiple_of(i * step, step), step)
            part = rows[i % 2]
            part = jnp.concatenate([part, part], 1)
            for c in range(0, width, 2 * LANES):
                columns = slice(c, c + 2 * LANES)
                across = part - coords[column : column + 1, columns]
                squared = across * across + coords[below : below + 1, columns]
                out[at, columns] = cosine(squared).astype(jnp.bfloat16)
            fill((i + 1) % 2, row, jnp.minimum(i + 1, steps - 1))


def tables(level, which, coords, *after):
    width = coords.shape[1]
    base = 8 * level
    near = (base + ROW, base + COLUMN, base + BELOW)
    far = (base + OTHER_ROW, base + COLUMN, base + BELOW)
    if level + 1 == LEVELS:
        far = (base + ROW, base + OTHER_COLUMN, base + OTHER_BELOW)
    jobs = [(near, far)[k] for k in which]
    shape = jax.ShapeDtypeStruct((width, width), jnp.bfloat16)
    step = LANES
    return pl.pallas_call(
        functools.partial(tables_kernel, jobs, step),
        out_shape=(shape,) * len(jobs),
        in_specs=[VMEM] + [ANY] * len(after),
        out_specs=(VMEM,) * len(jobs),
        scratch_shapes=[pltpu.VMEM((2, step, LANES), jnp.float32)],
        compiler_params=params(6),
        cost_estimate=cost(24 * len(jobs) * width * width * 40, 2 * len(jobs) * width * width),
    )(coords, *after)


def redatum_kernel(reach, blocks, near_edge, wave, far_edge, taps, *refs):
    out, padded = refs[-2:]
    count, width = wave.shape
    edge = near_edge.shape[1]
    even = 1 - boxes_of(0, blocks)[0] % 2
    after = edge + width
    starts = (pl.multiple_of(even * after, LANES), pl.multiple_of((1 - even) * after, LANES))
    for lane in range(count // LANES):
        held = slice(lane * LANES, (lane + 1) * LANES)
        for source, start in ((near_edge, starts[0]), (far_edge, starts[1]), (wave, edge)):
            for x in range(0, source.shape[1], LANES):
                block = source[held, x : x + LANES].astype(jnp.float32)
                padded[lane, pl.ds(start + x, LANES), :] = block.T

        @pl.loop(0, width // LANES)
        def _(block):
            base = pl.multiple_of(block * LANES, LANES)
            total = None
            for j in range(taps.shape[0]):
                weight = jnp.broadcast_to(taps[j : j + 1, held], (LANES, LANES))
                term = weight * padded[lane, pl.ds(base + edge - reach + j, LANES), :]
                total = term if total is None else total + term
            out[held, pl.ds(base, LANES)] = total.T.astype(out.dtype)


def redatum(blocks, near_edge, wave, far_edge, taps, *after):
    count, width = wave.shape
    reach = (taps.shape[0] - 1) // 2
    long = width + 2 * near_edge.shape[1]
    return pl.pallas_call(
        functools.partial(redatum_kernel, reach, blocks),
        out_shape=jax.ShapeDtypeStruct((count, width), jnp.bfloat16),
        in_specs=[VMEM] * 4 + [ANY] * len(after),
        out_specs=VMEM,
        scratch_shapes=[pltpu.VMEM((count // LANES, long, LANES), jnp.float32)],
        compiler_params=params(6),
        cost_estimate=cost(24 * 2 * width * width * 60, count * width * 4),
        name="redatum",
    )(near_edge, wave, far_edge, taps, *after)


def mix_kernel(held, mine, theirs, near, far, *refs):
    out = refs[-1]
    width = near.shape[1]
    scale = SCALE / math.sqrt(width)
    step = min(width, 256)
    for c in range(0, width, step):
        columns = slice(c, c + step)
        total = jnp.dot(mine[held, :], near[:, columns], preferred_element_type=jnp.float32)
        total += jnp.dot(theirs[held, :], far[:, columns], preferred_element_type=jnp.float32)
        out[:, columns] = (total * scale).astype(out.dtype)


def mix(part, mine, theirs, near, far, *after):
    count, width = mine.shape
    held = slice(part * LANES, (part + 1) * LANES) if count > LANES else slice(0, LANES)
    return pl.pallas_call(
        functools.partial(mix_kernel, held),
        out_shape=jax.ShapeDtypeStruct((LANES, width), jnp.bfloat16),
        in_specs=[VMEM] * 4 + [ANY] * len(after),
        out_specs=VMEM,
        compiler_params=params(7),
        cost_estimate=cost(24 * width * width * 15, 4 * width * width),
        name="mix",
    )(mine, theirs, near, far, *after)


def last_kernel(part, weights, added, state, coords, *refs):
    count = len(weights)
    tables, masks, sums = refs[:count], refs[count : 2 * count], refs[2 * count : 2 * count + added]
    width = tables[0].shape[1]
    scale = SCALE / math.sqrt(width)
    step = min(width, 256)
    held = slice(part * LANES, (part + 1) * LANES)
    for k, out in enumerate(refs[-count:]):
        for c in range(0, width, step):
            columns = slice(c, c + step)
            mixed = jnp.dot(state[...], tables[k][:, columns], preferred_element_type=jnp.float32)
            kept = jnp.where(masks[k][held, columns].astype(jnp.float32) > 0, mixed, 0.0)
            total = jnp.sum(kept, 0, keepdims=True) * scale
            total = total * coords[weights[k] : weights[k] + 1, columns]
            if added:
                total = total + sums[k][:, columns]
            out[:, columns] = total


def last(part, which, state, coords, tables, masks, sums, *after):
    width = state.shape[1]
    count = len(which)
    base = 8 * (LEVELS - 1)
    weights = [base + (WEIGHT, OTHER_WEIGHT)[k] for k in which]
    tables, masks = [tables[k] for k in which], [masks[k] for k in which]
    shape = jax.ShapeDtypeStruct((1, width), jnp.float32)
    return pl.pallas_call(
        functools.partial(last_kernel, part, weights, len(sums)),
        out_shape=(shape,) * count,
        in_specs=[VMEM] * (2 + 2 * count + len(sums)) + [ANY] * len(after),
        out_specs=(VMEM,) * count,
        compiler_params=params(7),
        cost_estimate=cost(24 * count * width * width * 8, 2 * count * width * width),
    )(state, coords, *tables, *masks, *sums, *after)


def on_device(wavefield, redatum_taps, cell_x, cell_depth, slowness, illumination, aperture):
    index = lax.axis_index("space")
    blocks = lax.axis_size("space") // BOXES
    block_bits = blocks.bit_length() - 1
    block = index % blocks
    count, width = wavefield.shape
    depth = cell_depth.reshape(BOXES * width // LANES, LANES)
    light = illumination.reshape(BOXES * width // LANES, LANES)
    near_edge, far_edge, coords = prepare(blocks, wavefield, cell_x, depth, light, slowness)
    mask = mark(aperture)
    near_edge = partner(near_edge, "space", block_bits)
    far_edge = across(far_edge, "space", blocks)
    taps = redatum_taps
    if blocks > 1:
        taps = lax.dynamic_slice_in_dim(redatum_taps, block * count, count, 0)
    taps = taps.T
    parts = range(count // LANES)

    (near,) = tables(0, (0,), coords, mask)
    near_edge, far_edge, held_mask = lax.optimization_barrier((near_edge, far_edge, mask))
    masks = partner(held_mask, "space", LEVELS - 1 + block_bits)
    state = redatum(blocks, near_edge, wavefield, far_edge, taps, near)
    received = partner(state, "space", block_bits)
    (far,) = tables(0, (1,), coords, state)
    states = [state for _ in parts]
    theirs = [received for _ in parts]
    table, ahead = (near, far), far
    both, sums = (mask, masks), ()
    for level in range(LEVELS - 1):
        for part in parts:
            states[part] = mix(part, states[part], theirs[part], *table, ahead)
            ahead = states[part]
            if level + 2 == LEVELS and part + 1 < len(parts):
                sums = last(part, (0, 1), states[part], coords, later, both, sums)
                ahead = sums[0]
            if level + 2 == LEVELS and part + 1 == len(parts):
                final = (states[part], coords, later, both)
                (other,) = last(part, (1,), *final, sums[1:])
                (own,) = last(part, (0,), *final, sums[:1], other)
            if level + 2 < LEVELS:
                theirs[part] = partner(states[part], "space", level + 1 + block_bits)
            if part == (0 if level == 1 else len(parts) - 1) and level < 2:
                following = tables(level + 1, (0, 1), coords, ahead)
                ahead = following[0]
            if part == len(parts) - 1 and level == 1:
                later = tables(level + 2, (0, 1), coords, ahead)
                ahead = later[0]
        table = following
    image = own + partner(other, "space", LEVELS - 1 + block_bits)
    for level in range(block_bits):
        image = image + partner(image, "space", level)
    share = width // blocks
    return lax.dynamic_slice_in_dim(image, block * share, share, 1)


def solution(mesh):
    placed = (
        P(("groups", "space"), None),
        P("groups", None),
        P(),
        P(),
        P(),
        P("groups"),
        P(("groups", "space"), None),
    )
    return jax.shard_map(
        on_device,
        mesh=mesh,
        in_specs=placed,
        out_specs=P(("groups", "space"), None),
        check_vma=False,
    )
```

profile of v0, /device:TPU:0, one launch (start us, length us, event | category | flops | bytes accessed | tf_op | source)
XLA Modules:
  0.0 59.9 jit_solution(14541939179334933771)
XLA Ops:
  0.0 1.9 %prepare.1 = (bf16[256,128]{1,0:T(8,128)(2,1)}, bf16[256,128]{1,0:T(8,128)(2,1)}, f32[32,1024]{1,0:T(8,128)}) custom-call(bf16[256,1024]{1,0:T(8,128)(2,1)} %wave.3, s32[5,16384]{1,0:T(8,128)} %cell_x.1, s32[128,128]{1,0:T(8,128)} %bitcast.4, f32[128,128]{1,0:T(8,128)} %bitcast.5, f32[4]{0:T(128)} %slowness.1), custom_call_target="tpu_custom_call" | custom-call | flops 754974720 | bytes 2097152 | tf_op jit(solution)/shard_map/prepare/pallas_call | solution.py:143
  1.9 0.6 collective-permute-start
  2.5 0.7 %collective-permute-start.1 = (bf16[256,128]{1,0:T(8,128)(2,1)}, bf16[256,128]{1,0:T(8,128)(2,1)S(1)}, u32[]{:S(2)}, u32[]{:S(2)}) collective-permute-start(bf16[256,128]{1,0:T(8,128)(2,1)} %get-tuple-element.20), channel_id=1, source_target_pairs={{1,2},{2,1},{3,4},{4,3},{5,6},{6,5},{7,8},{8,7},{9,10},{10,9},{11,... | collective-permute-start | bytes 196616 | tf_op jit(solution)/shard_map/ppermute | solution.py:38
  3.2 0.1 mark.1.refs_0_.refs_2_.refs_1_
  3.3 0.9 %copy-done = f32[32,1024]{1,0:T(8,128)S(1)} copy-done((f32[32,1024]{1,0:T(8,128)S(1)}, f32[32,1024]{1,0:T(8,128)}, u32[]{:S(2)}) %copy-start) | copy-done | bytes 131096
  4.2 2.2 %shard_map.73.refs_0_.near = bf16[1024,1024]{1,0:T(8,128)(2,1)S(1)} custom-call(f32[32,1024]{1,0:T(8,128)S(1)} %copy-done, bf16[256,1024]{1,0:T(8,128)(2,1)S(1)} %mark.1.refs_0_.refs_2_.refs_1_), custom_call_target="tpu_custom_call" | custom-call | flops 1006632960 | bytes 2097152 | tf_op jit(solution)/shard_map/pallas_call | solution.py:200
  6.3 0.0 collective-permute-done.1.far_edge
  6.4 6.0 %redatum.1.refs_0_.mine = bf16[256,1024]{1,0:T(8,128)(2,1)S(1)} custom-call(bf16[256,128]{1,0:T(8,128)(2,1)S(1)} %collective-permute-done.near_edge, bf16[256,1024]{1,0:T(8,128)(2,1)S(1)} %copy-done.3, bf16[256,128]{1,0:T(8,128)(2,1)S(1)} %collective-permute-done.1.far_edge, f32[65,256]{1,0:T(8,128)S(1)} %bitcast.3, ...), custom_call_target="tpu_custom_call" | custom-call | flops 3019898880 | bytes 1048576 | tf_op jit(solution)/shard_map/redatum/pallas_call | solution.py:240
  12.3 3.9 %collective-permute-start.2 = (bf16[256,1024]{1,0:T(8,128)(2,1)S(1)}, bf16[256,1024]{1,0:T(8,128)(2,1)S(1)}, u32[]{:S(2)}, u32[]{:S(2)}) collective-permute-start(bf16[256,1024]{1,0:T(8,128)(2,1)S(1)} %redatum.1.refs_0_.mine), channel_id=1, source_target_pairs={{0,1},{1,0},{2,3},{3,2},{4,5},{5,4},{6,7},{7,6},{8,9},{9,8},{10,11... | collective-permute-start | bytes 1572872 | tf_op jit(solution)/shard_map/ppermute | solution.py:42
  16.3 2.2 %shard_map.74.far.refs_0_ = bf16[1024,1024]{1,0:T(8,128)(2,1)S(1)} custom-call(f32[32,1024]{1,0:T(8,128)S(1)} %copy-done, bf16[256,1024]{1,0:T(8,128)(2,1)S(1)} %redatum.1.refs_0_.mine), custom_call_target="tpu_custom_call" | custom-call | flops 1006632960 | bytes 2097152 | tf_op jit(solution)/shard_map/pallas_call | solution.py:200
  18.4 0.7 %mix.6.refs_0_.mine = bf16[128,1024]{1,0:T(8,128)(2,1)S(1)} custom-call(bf16[256,1024]{1,0:T(8,128)(2,1)S(1)} %redatum.1.refs_0_.mine, bf16[256,1024]{1,0:T(8,128)(2,1)S(1)} %collective-permute-done.2.theirs, bf16[1024,1024]{1,0:T(8,128)(2,1)S(1)} %shard_map.73.refs_0_.near, bf16[1024,1024]{1,0:T(8,128)(2,1)S(1)} %shard_map.74.far.refs_0_, ...), custom_call_target="tpu_custom_call" | custom-call | flops 377487360 | bytes 4194304 | tf_op jit(solution)/shard_map/mix/pallas_call | solution.py:267
  19.2 2.0 %collective-permute-start.4 = (bf16[128,1024]{1,0:T(8,128)(2,1)S(1)}, bf16[128,1024]{1,0:T(8,128)(2,1)S(1)}, u32[]{:S(2)}, u32[]{:S(2)}) collective-permute-start(bf16[128,1024]{1,0:T(8,128)(2,1)S(1)} %mix.6.refs_0_.mine), channel_id=1, source_target_pairs={{0,2},{1,3},{2,0},{3,1},{4,6},{5,7},{6,4},{7,5},{8,10},{9,11},{10,... | collective-permute-start | bytes 786440 | tf_op jit(solution)/shard_map/ppermute | solution.py:42
  21.2 2.6 %collective-permute-start.7 = (bf16[256,1024]{1,0:T(8,128)(2,1)S(1)}, bf16[256,1024]{1,0:T(8,128)(2,1)S(1)}, u32[]{:S(2)}, u32[]{:S(2)}) collective-permute-start(bf16[256,1024]{1,0:T(8,128)(2,1)S(1)} %mark.1.refs_0_.refs_2_.refs_1_), channel_id=1, source_target_pairs={{0,8},{1,9},{2,10},{3,11},{4,12},{5,13},{6,14},{7,15},{8,0},{9,1},... | collective-permute-start | bytes 1572872 | tf_op jit(solution)/shard_map/ppermute | solution.py:42
  23.8 0.7 %mix.7.refs_0_.mine = bf16[128,1024]{1,0:T(8,128)(2,1)S(1)} custom-call(bf16[256,1024]{1,0:T(8,128)(2,1)S(1)} %redatum.1.refs_0_.mine, bf16[256,1024]{1,0:T(8,128)(2,1)S(1)} %collective-permute-done.2.theirs, bf16[1024,1024]{1,0:T(8,128)(2,1)S(1)} %shard_map.73.refs_0_.near, bf16[1024,1024]{1,0:T(8,128)(2,1)S(1)} %shard_map.74.far.refs_0_, ...), custom_call_target="tpu_custom_call" | custom-call | flops 377487360 | bytes 4194304 | tf_op jit(solution)/shard_map/mix/pallas_call | solution.py:267
  24.5 0.4 collective-permute-start.3
  24.9 4.3 %shard_map.75 = (bf16[1024,1024]{1,0:T(8,128)(2,1)S(1)}, bf16[1024,1024]{1,0:T(8,128)(2,1)S(1)}) custom-call(f32[32,1024]{1,0:T(8,128)S(1)} %copy-done.1, bf16[128,1024]{1,0:T(8,128)(2,1)S(1)} %mix.7.refs_0_.mine), custom_call_target="tpu_custom_call" | custom-call | flops 2013265920 | bytes 4194304 | tf_op jit(solution)/shard_map/pallas_call | solution.py:200
  29.2 0.7 %mix.8.refs_0_.mine = bf16[128,1024]{1,0:T(8,128)(2,1)S(1)} custom-call(bf16[128,1024]{1,0:T(8,128)(2,1)S(1)} %mix.6.refs_0_.mine, bf16[128,1024]{1,0:T(8,128)(2,1)S(1)} %collective-permute-done.4.theirs, bf16[1024,1024]{1,0:T(8,128)(2,1)S(1)} %get-tuple-element.24.near.refs_0_, bf16[1024,1024]{1,0:T(8,128)(2,1)S(1)} %get-tuple-element.25.far, ...), custom_call_target="tpu_custom_call" | custom-call | flops 377487360 | bytes 4194304 | tf_op jit(solution)/shard_map/mix/pallas_call | solution.py:267
  30.0 1.6 %collective-permute-start.6 = (bf16[128,1024]{1,0:T(8,128)(2,1)S(1)}, bf16[128,1024]{1,0:T(8,128)(2,1)S(1)}, u32[]{:S(2)}, u32[]{:S(2)}) collective-permute-start(bf16[128,1024]{1,0:T(8,128)(2,1)S(1)} %mix.8.refs_0_.mine), channel_id=1, source_target_pairs={{0,4},{1,5},{2,6},{3,7},{4,0},{5,1},{6,2},{7,3},{8,12},{9,13},{10,... | collective-permute-start | bytes 786440 | tf_op jit(solution)/shard_map/ppermute | solution.py:42
  31.6 4.3 %shard_map.76 = (bf16[1024,1024]{1,0:T(8,128)(2,1)S(1)}, bf16[1024,1024]{1,0:T(8,128)(2,1)S(1)}) custom-call(f32[32,1024]{1,0:T(8,128)S(1)} %copy-done.1, bf16[128,1024]{1,0:T(8,128)(2,1)S(1)} %mix.8.refs_0_.mine), custom_call_target="tpu_custom_call" | custom-call | flops 2013265920 | bytes 4194304 | tf_op jit(solution)/shard_map/pallas_call | solution.py:200
  36.0 0.7 %mix.9.refs_0_.mine = bf16[128,1024]{1,0:T(8,128)(2,1)S(1)} custom-call(bf16[128,1024]{1,0:T(8,128)(2,1)S(1)} %mix.7.refs_0_.mine, bf16[128,1024]{1,0:T(8,128)(2,1)S(1)} %collective-permute-done.3.theirs, bf16[1024,1024]{1,0:T(8,128)(2,1)S(1)} %get-tuple-element.24.near.refs_0_, bf16[1024,1024]{1,0:T(8,128)(2,1)S(1)} %get-tuple-element.25.far, ...), custom_call_target="tpu_custom_call" | custom-call | flops 377487360 | bytes 4194304 | tf_op jit(solution)/shard_map/mix/pallas_call | solution.py:267
  36.7 0.5 collective-permute-start.5
  37.2 4.3 %shard_map.77 = (bf16[1024,1024]{1,0:T(8,128)(2,1)S(1)}, bf16[1024,1024]{1,0:T(8,128)(2,1)S(1)}) custom-call(f32[32,1024]{1,0:T(8,128)S(1)} %copy-done.1, bf16[128,1024]{1,0:T(8,128)(2,1)S(1)} %mix.9.refs_0_.mine), custom_call_target="tpu_custom_call" | custom-call | flops 2013265920 | bytes 4194304 | tf_op jit(solution)/shard_map/pallas_call | solution.py:200
  41.5 7.2 %collective-permute-done.6.theirs = bf16[128,1024]{1,0:T(8,128)(2,1)S(1)} collective-permute-done((bf16[128,1024]{1,0:T(8,128)(2,1)S(1)}, bf16[128,1024]{1,0:T(8,128)(2,1)S(1)}, u32[]{:S(2)}, u32[]{:S(2)}) %collective-permute-start.6) | collective-permute-done | bytes 262176 | tf_op jit(solution)/shard_map/ppermute | solution.py:42
  48.7 0.7 %mix.10.state = bf16[128,1024]{1,0:T(8,128)(2,1)S(1)} custom-call(bf16[128,1024]{1,0:T(8,128)(2,1)S(1)} %mix.8.refs_0_.mine, bf16[128,1024]{1,0:T(8,128)(2,1)S(1)} %collective-permute-done.6.theirs, bf16[1024,1024]{1,0:T(8,128)(2,1)S(1)} %get-tuple-element.26.refs_0_.near, bf16[1024,1024]{1,0:T(8,128)(2,1)S(1)} %get-tuple-element.27.far, ...), custom_call_target="tpu_custom_call" | custom-call | flops 377487360 | bytes 4194304 | tf_op jit(solution)/shard_map/mix/pallas_call | solution.py:267
  49.5 0.8 %shard_map.78 = (f32[1,1024]{1,0:T(1,128)S(1)}, f32[1,1024]{1,0:T(1,128)S(1)}) custom-call(bf16[128,1024]{1,0:T(8,128)(2,1)S(1)} %mix.10.state, f32[32,1024]{1,0:T(8,128)S(1)} %copy-done.1, bf16[1024,1024]{1,0:T(8,128)(2,1)S(1)} %get-tuple-element.28.refs_0_, bf16[1024,1024]{1,0:T(8,128)(2,1)S(1)} %get-tuple-element.29.refs_1_.refs_0_, ...), custom_call_target="tpu_custom_call" | custom-call | flops 402653184 | bytes 4194304 | tf_op jit(solution)/shard_map/pallas_call | solution.py:304
  50.2 3.2 %collective-permute-done.5.theirs = bf16[128,1024]{1,0:T(8,128)(2,1)S(1)} collective-permute-done((bf16[128,1024]{1,0:T(8,128)(2,1)S(1)}, bf16[128,1024]{1,0:T(8,128)(2,1)S(1)}, u32[]{:S(2)}, u32[]{:S(2)}) %collective-permute-start.5) | collective-permute-done | bytes 262176 | tf_op jit(solution)/shard_map/ppermute | solution.py:42
  53.5 0.7 %mix.11.state = bf16[128,1024]{1,0:T(8,128)(2,1)S(1)} custom-call(bf16[128,1024]{1,0:T(8,128)(2,1)S(1)} %mix.9.refs_0_.mine, bf16[128,1024]{1,0:T(8,128)(2,1)S(1)} %collective-permute-done.5.theirs, bf16[1024,1024]{1,0:T(8,128)(2,1)S(1)} %get-tuple-element.26.refs_0_.near, bf16[1024,1024]{1,0:T(8,128)(2,1)S(1)} %get-tuple-element.27.far, ...), custom_call_target="tpu_custom_call" | custom-call | flops 377487360 | bytes 4194304 | tf_op jit(solution)/shard_map/mix/pallas_call | solution.py:267
  54.2 0.5 shard_map.79.refs_3_
  54.7 0.7 %collective-permute-start.8 = (f32[1,1024]{1,0:T(1,128)S(1)}, f32[1,1024]{1,0:T(1,128)S(1)}, u32[]{:S(2)}, u32[]{:S(2)}) collective-permute-start(f32[1,1024]{1,0:T(1,128)S(1)} %shard_map.79.refs_3_), channel_id=1, source_target_pairs={{0,8},{1,9},{2,10},{3,11},{4,12},{5,13},{6,14},{7,15},{8,0},{9,1},... | collective-permute-start | bytes 12296 | tf_op jit(solution)/shard_map/ppermute | solution.py:42
  55.4 0.5 shard_map.80
  55.9 3.4 %collective-permute-done.8 = f32[1,1024]{1,0:T(1,128)S(1)} collective-permute-done((f32[1,1024]{1,0:T(1,128)S(1)}, f32[1,1024]{1,0:T(1,128)S(1)}, u32[]{:S(2)}, u32[]{:S(2)}) %collective-permute-start.8) | collective-permute-done | bytes 4128 | tf_op jit(solution)/shard_map/ppermute | solution.py:42
  59.3 0.6 add.6
  (14 shorter events, 0.0 us)
Async XLA Ops:
  0.0 3.1 %copy-start.2 = (s32[256,1024]{1,0:T(8,128)S(1)}, s32[256,1024]{1,0:T(8,128)}, u32[]{:S(2)}) copy-start(s32[256,1024]{1,0:T(8,128)} %aperture.1) | copy-start | bytes 3145732
  1.9 4.4 %collective-permute-start = (bf16[256,128]{1,0:T(8,128)(2,1)}, bf16[256,128]{1,0:T(8,128)(2,1)S(1)}, u32[]{:S(2)}, u32[]{:S(2)}) collective-permute-start(bf16[256,128]{1,0:T(8,128)(2,1)} %get-tuple-element.19), channel_id=1, source_target_pairs={{0,1},{1,0},{2,3},{3,2},{4,5},{5,4},{6,7},{7,6},{8,9},{9,8},{10,11... | collective-permute-start | bytes 196616 | tf_op jit(solution)/shard_map/ppermute | solution.py:42
  2.5 3.9 %collective-permute-start.1 = (bf16[256,128]{1,0:T(8,128)(2,1)}, bf16[256,128]{1,0:T(8,128)(2,1)S(1)}, u32[]{:S(2)}, u32[]{:S(2)}) collective-permute-start(bf16[256,128]{1,0:T(8,128)(2,1)} %get-tuple-element.20), channel_id=1, source_target_pairs={{1,2},{2,1},{3,4},{4,3},{5,6},{6,5},{7,8},{8,7},{9,10},{10,9},{11,... | collective-permute-start | bytes 196616 | tf_op jit(solution)/shard_map/ppermute | solution.py:38
  3.2 0.9 %copy-start = (f32[32,1024]{1,0:T(8,128)S(1)}, f32[32,1024]{1,0:T(8,128)}, u32[]{:S(2)}) copy-start(f32[32,1024]{1,0:T(8,128)} %get-tuple-element.23.coords) | copy-start | bytes 393220
  4.2 2.2 %copy-start.3 = (bf16[256,1024]{1,0:T(8,128)(2,1)S(1)}, bf16[256,1024]{1,0:T(8,128)(2,1)}, u32[]{:S(2)}) copy-start(bf16[256,1024]{1,0:T(8,128)(2,1)} %wave.3) | copy-start | bytes 1572868
  4.2 2.2 %copy-start.4 = (f32[256,65]{0,1:T(8,128)S(1)}, f32[256,65]{0,1:T(8,128)}, u32[]{:S(2)}) copy-start(f32[256,65]{0,1:T(8,128)} %param.8) | copy-start | bytes 199684
  12.3 6.1 %collective-permute-start.2 = (bf16[256,1024]{1,0:T(8,128)(2,1)S(1)}, bf16[256,1024]{1,0:T(8,128)(2,1)S(1)}, u32[]{:S(2)}, u32[]{:S(2)}) collective-permute-start(bf16[256,1024]{1,0:T(8,128)(2,1)S(1)} %redatum.1.refs_0_.mine), channel_id=1, source_target_pairs={{0,1},{1,0},{2,3},{3,2},{4,5},{5,4},{6,7},{7,6},{8,9},{9,8},{10,11... | collective-permute-start | bytes 1572872 | tf_op jit(solution)/shard_map/ppermute | solution.py:42
  19.2 5.7 %copy-start.1 = (f32[32,1024]{1,0:T(8,128)S(1)}, f32[32,1024]{1,0:T(8,128)}, u32[]{:S(2)}) copy-start(f32[32,1024]{1,0:T(8,128)} %get-tuple-element.23.coords) | copy-start | bytes 393220
  19.2 10.0 %collective-permute-start.4 = (bf16[128,1024]{1,0:T(8,128)(2,1)S(1)}, bf16[128,1024]{1,0:T(8,128)(2,1)S(1)}, u32[]{:S(2)}, u32[]{:S(2)}) collective-permute-start(bf16[128,1024]{1,0:T(8,128)(2,1)S(1)} %mix.6.refs_0_.mine), channel_id=1, source_target_pairs={{0,2},{1,3},{2,0},{3,1},{4,6},{5,7},{6,4},{7,5},{8,10},{9,11},{10,... | collective-permute-start | bytes 786440 | tf_op jit(solution)/shard_map/ppermute | solution.py:42
  21.2 28.3 %collective-permute-start.7 = (bf16[256,1024]{1,0:T(8,128)(2,1)S(1)}, bf16[256,1024]{1,0:T(8,128)(2,1)S(1)}, u32[]{:S(2)}, u32[]{:S(2)}) collective-permute-start(bf16[256,1024]{1,0:T(8,128)(2,1)S(1)} %mark.1.refs_0_.refs_2_.refs_1_), channel_id=1, source_target_pairs={{0,8},{1,9},{2,10},{3,11},{4,12},{5,13},{6,14},{7,15},{8,0},{9,1},... | collective-permute-start | bytes 1572872 | tf_op jit(solution)/shard_map/ppermute | solution.py:42
  24.5 11.5 %collective-permute-start.3 = (bf16[128,1024]{1,0:T(8,128)(2,1)S(1)}, bf16[128,1024]{1,0:T(8,128)(2,1)S(1)}, u32[]{:S(2)}, u32[]{:S(2)}) collective-permute-start(bf16[128,1024]{1,0:T(8,128)(2,1)S(1)} %mix.7.refs_0_.mine), channel_id=1, source_target_pairs={{0,2},{1,3},{2,0},{3,1},{4,6},{5,7},{6,4},{7,5},{8,10},{9,11},{10,... | collective-permute-start | bytes 786440 | tf_op jit(solution)/shard_map/ppermute | solution.py:42
  30.0 18.7 %collective-permute-start.6 = (bf16[128,1024]{1,0:T(8,128)(2,1)S(1)}, bf16[128,1024]{1,0:T(8,128)(2,1)S(1)}, u32[]{:S(2)}, u32[]{:S(2)}) collective-permute-start(bf16[128,1024]{1,0:T(8,128)(2,1)S(1)} %mix.8.refs_0_.mine), channel_id=1, source_target_pairs={{0,4},{1,5},{2,6},{3,7},{4,0},{5,1},{6,2},{7,3},{8,12},{9,13},{10,... | collective-permute-start | bytes 786440 | tf_op jit(solution)/shard_map/ppermute | solution.py:42
  36.7 16.8 %collective-permute-start.5 = (bf16[128,1024]{1,0:T(8,128)(2,1)S(1)}, bf16[128,1024]{1,0:T(8,128)(2,1)S(1)}, u32[]{:S(2)}, u32[]{:S(2)}) collective-permute-start(bf16[128,1024]{1,0:T(8,128)(2,1)S(1)} %mix.9.refs_0_.mine), channel_id=1, source_target_pairs={{0,4},{1,5},{2,6},{3,7},{4,0},{5,1},{6,2},{7,3},{8,12},{9,13},{10,... | collective-permute-start | bytes 786440 | tf_op jit(solution)/shard_map/ppermute | solution.py:42
  54.7 4.6 %collective-permute-start.8 = (f32[1,1024]{1,0:T(1,128)S(1)}, f32[1,1024]{1,0:T(1,128)S(1)}, u32[]{:S(2)}, u32[]{:S(2)}) collective-permute-start(f32[1,1024]{1,0:T(1,128)S(1)} %shard_map.79.refs_3_), channel_id=1, source_target_pairs={{0,8},{1,9},{2,10},{3,11},{4,12},{5,13},{6,14},{7,15},{8,0},{9,1},... | collective-permute-start | bytes 12296 | tf_op jit(solution)/shard_map/ppermute | solution.py:42
where the time goes:
time: 60 us; the launch traced here: 59.9 us
  Pallas kernels  31.3 us (52%)
  waiting for transfers between devices  13.8 us (23%)
  starting transfers between devices  13 us (22%)
  local copies, waits for them, and re-layouts  0.91 us (2%)
  other arithmetic  0.6 us (1%)
    pallas_call x5, Pallas kernels, tables(): pl.pallas_call(functools.partial(tables_kernel, jobs, step), out_shape=(s...  17.3 us
    ppermute x8, waiting for transfers between devices, partner(): lax.ppermute(shard, axis, [(i, i ^ 1 << bit) for i in range(lax.axis_size...  13.8 us
    ppermute x8, starting transfers between devices, partner(): lax.ppermute(shard, axis, [(i, i ^ 1 << bit) for i in range(lax.axis_size...  12.4 us
    pallas_call x1, Pallas kernels, redatum(): pl.pallas_call(functools.partial(redatum_kernel, reach, blocks), out_shap...  5.96 us
    pallas_call x6, Pallas kernels, mix(): pl.pallas_call(functools.partial(mix_kernel, held), out_shape=jax.ShapeDt...  4.35 us
    pallas_call x1, Pallas kernels, prepare(): pl.pallas_call(functools.partial(prepare_kernel, blocks), out_shape=(edge...  1.91 us
    pallas_call x3, Pallas kernels, last(): pl.pallas_call(functools.partial(last_kernel, part, weights, len(sums)),...  1.71 us
  transfers between devices with their start and end apart: 9, of which 3 were waited for; matrix products, arithmetic and copies ran while one was open for 0% of the time, Pallas kernels for 36%

commit v1 on v0

--- a/solution.py
+++ b/solution.py
@@ -60,9 +60,8 @@
 ROW, OTHER_ROW, COLUMN, BELOW, OTHER_COLUMN, OTHER_BELOW, WEIGHT, OTHER_WEIGHT = range(8)
 
 
-def prepare_kernel(blocks, wave, cell_x, depth, illumination, slowness, *refs):
-    near_edge, far_edge, coords, cells, depths, lights, slow, sems = refs
-    width = wave.shape[1]
+def prepare_kernel(blocks, count, width, cell_x, depth, illumination, slowness, *refs):
+    coords, cells, depths, lights, slow, sems = refs[-6:]
     tall = width // LANES
     box = boxes_of(0, blocks)[0]
     others = [boxes_of(level, blocks)[1] for level in range(LEVELS)]
@@ -75,15 +74,7 @@
         copies.append(pltpu.make_async_copy(depth.at[at, :], depths.at[k], sems.at[6 + k]))
         light = illumination.at[at, :]
         copies.append(pltpu.make_async_copy(light, lights.at[k], sems.at[10 + k]))
-    end = width - LANES
-    even = 1 - box % 2
-    first = pl.ds(pl.multiple_of(even * end, LANES), LANES)
-    second = pl.ds(pl.multiple_of((1 - even) * end, LANES), LANES)
-    late = [
-        pltpu.make_async_copy(wave.at[:, first], near_edge, sems.at[8]),
-        pltpu.make_async_copy(wave.at[:, second], far_edge, sems.at[9]),
-    ]
-    for copy in copies + late:
+    for copy in copies:
         copy.start()
     for copy in copies:
         copy.wait()
@@ -109,46 +100,39 @@
         if level + 1 == LEVELS:
             put(OTHER_COLUMN, LEVELS, level + 1)
             put_below(OTHER_BELOW, 1)
-    share = 1.0 / math.sqrt(wave.shape[0] * blocks)
+    share = 1.0 / math.sqrt(count * blocks)
     base = 8 * (LEVELS - 1)
     for source, kind in enumerate((WEIGHT, OTHER_WEIGHT)):
         for k in range(tall):
             coords[base + kind : base + kind + 1, k * LANES : (k + 1) * LANES] = (
                 lights[source, k : k + 1, :] * share
             )
-    for copy in late:
-        copy.wait()
-
-
-def mark_kernel(aperture, mask):
+
+
+def mark_kernel(aperture, *refs):
+    mask = refs[-1]
     mask[...] = (aperture[...] > 0).astype(jnp.float32).astype(jnp.bfloat16)
 
 
-def mark(aperture):
+def mark(aperture, *after):
     return pl.pallas_call(
         mark_kernel,
         out_shape=jax.ShapeDtypeStruct(aperture.shape, jnp.bfloat16),
-        in_specs=[VMEM],
+        in_specs=[VMEM] + [ANY] * len(after),
         out_specs=VMEM,
         compiler_params=params(4),
         cost_estimate=cost(aperture.size * 200, aperture.size * 6),
         name="mark",
-    )(aperture)
-
-
-def prepare(blocks, wave, cell_x, depth, illumination, slowness):
-    count, width = wave.shape
+    )(aperture, *after)
+
+
+def prepare(blocks, count, width, cell_x, depth, illumination, slowness, *after):
     levels = cell_x.shape[0]
-    edge = jax.ShapeDtypeStruct((count, LANES), wave.dtype)
-    return pl.pallas_call(
-        functools.partial(prepare_kernel, blocks),
-        out_shape=(
-            edge,
-            edge,
-            jax.ShapeDtypeStruct((8 * LEVELS, width), jnp.float32),
-        ),
-        in_specs=[HBM] * 5,
-        out_specs=(VMEM,) * 3,
+    return pl.pallas_call(
+        functools.partial(prepare_kernel, blocks, count, width),
+        out_shape=jax.ShapeDtypeStruct((8 * LEVELS, width), jnp.float32),
+        in_specs=[HBM] * 4 + [ANY] * len(after),
+        out_specs=VMEM,
         scratch_shapes=[
             pltpu.VMEM((1 + LEVELS, levels, width), jnp.int32),
             pltpu.VMEM((2, width // LANES, LANES), jnp.int32),
@@ -159,7 +143,7 @@
         compiler_params=pltpu.CompilerParams(vmem_limit_bytes=GRANT),
         cost_estimate=cost(24 * 2 * width * width * 15, count * width * 8),
         name="prepare",
-    )(wave, cell_x, depth, illumination, slowness)
+    )(cell_x, depth, illumination, slowness, *after)
 
 
 def tables_kernel(jobs, step, coords, *refs):
@@ -319,19 +303,21 @@
     count, width = wavefield.shape
     depth = cell_depth.reshape(BOXES * width // LANES, LANES)
     light = illumination.reshape(BOXES * width // LANES, LANES)
-    near_edge, far_edge, coords = prepare(blocks, wavefield, cell_x, depth, light, slowness)
+    even = index // blocks % 2 == 0
+    head, tail = wavefield[:, :LANES], wavefield[:, width - LANES :]
+    far_edge = across(jnp.where(even, head, tail), "space", blocks)
+    near_edge = partner(jnp.where(even, tail, head), "space", block_bits)
+    coords = prepare(blocks, count, width, cell_x, depth, light, slowness)
     mask = mark(aperture)
-    near_edge = partner(near_edge, "space", block_bits)
-    far_edge = across(far_edge, "space", blocks)
     taps = redatum_taps
     if blocks > 1:
         taps = lax.dynamic_slice_in_dim(redatum_taps, block * count, count, 0)
     taps = taps.T
     parts = range(count // LANES)
 
-    (near,) = tables(0, (0,), coords, mask)
     near_edge, far_edge, held_mask = lax.optimization_barrier((near_edge, far_edge, mask))
     masks = partner(held_mask, "space", LEVELS - 1 + block_bits)
+    (near,) = tables(0, (0,), coords, near_edge)
     state = redatum(blocks, near_edge, wavefield, far_edge, taps, near)
     received = partner(state, "space", block_bits)
     (far,) = tables(0, (1,), coords, state)

time: 60 us -> 62 us (1.033)
  local copies, waits for them, and re-layouts: 0.91 us -> 2.13 us
  other arithmetic: 0.6 us -> 1.48 us
    unnamed x10, local copies, waits for them, and re-layouts: 0.91 us -> 2.13 us
    select_n x0 -> x1, other arithmetic: none -> 0.89 us  [on_device(): far_edge = across(jnp.where(even, head, tail), 'space', blocks)]
  transfers between devices with their start and end apart: 9 -> 9, of which waited for: 3 -> 3; matrix products, arithmetic and copies ran while one was open for 0% -> 0% of each run, Pallas kernels for 36% -> 34%
where the time goes in v1:
time: 62 us; the launch traced here: 61.7 us
  Pallas kernels  31.1 us (50%)
  waiting for transfers between devices  13.7 us (22%)
  starting transfers between devices  13 us (21%)
  local copies, waits for them, and re-layouts  2.13 us (3%)
  other arithmetic  1.48 us (2%)
    pallas_call x5, Pallas kernels, tables(): pl.pallas_call(functools.partial(tables_kernel, jobs, step), out_shape=(s...  17.3 us
    ppermute x8, waiting for transfers between devices, partner(): lax.ppermute(shard, axis, [(i, i ^ 1 << bit) for i in range(lax.axis_size...  13.7 us
    ppermute x8, starting transfers between devices, partner(): lax.ppermute(shard, axis, [(i, i ^ 1 << bit) for i in range(lax.axis_size...  12.3 us
    pallas_call x1, Pallas kernels, redatum(): pl.pallas_call(functools.partial(redatum_kernel, reach, blocks), out_shap...  5.96 us
    pallas_call x6, Pallas kernels, mix(): pl.pallas_call(functools.partial(mix_kernel, held), out_shape=jax.ShapeDt...  4.34 us
    unnamed x10, local copies, waits for them, and re-layouts  2.13 us
    pallas_call x3, Pallas kernels, last(): pl.pallas_call(functools.partial(last_kernel, part, weights, len(sums)),...  1.73 us
    pallas_call x1, Pallas kernels, prepare(): pl.pallas_call(functools.partial(prepare_kernel, blocks, count, width), o...  1.71 us
  transfers between devices with their start and end apart: 9, of which 3 were waited for; matrix products, arithmetic and copies ran while one was open for 0% of the time, Pallas kernels for 34%

profile of v1, /device:TPU:0, one launch (start us, length us, event | category | flops | bytes accessed | tf_op | source)
XLA Modules:
  0.0 61.7 jit_solution(9532826208773493326)
XLA Ops:
  0.0 0.9 %broadcast_select_fusion = (bf16[256,128]{1,0:T(8,128)(2,1)S(1)}, bf16[256,128]{1,0:T(8,128)(2,1)S(1)}) fusion(pred[]{:T(512)S(6)} %eq.6, bf16[256,1024]{1,0:T(8,128)(2,1)} %wave.1), kind=kLoop, calls=%fused_computation | loop fusion | flops 65536 | bytes 262145 | tf_op jit(solution)/shard_map/jit(_where)/select_n | solution.py:308
  0.9 0.6 collective-permute-start
  1.4 0.7 %collective-permute-start.1 = (bf16[256,128]{1,0:T(8,128)(2,1)S(1)}, bf16[256,128]{1,0:T(8,128)(2,1)S(1)}, u32[]{:S(2)}, u32[]{:S(2)}) collective-permute-start(bf16[256,128]{1,0:T(8,128)(2,1)S(1)} %get-tuple-element.27), channel_id=1, source_target_pairs={{1,2},{2,1},{3,4},{4,3},{5,6},{6,5},{7,8},{8,7},{9,10},{10,9},{11,... | collective-permute-start | bytes 196616 | tf_op jit(solution)/shard_map/ppermute | solution.py:38
  2.1 1.2 %copy-done.2 = s32[256,1024]{1,0:T(8,128)S(1)} copy-done((s32[256,1024]{1,0:T(8,128)S(1)}, s32[256,1024]{1,0:T(8,128)}, u32[]{:S(2)}) %copy-start.2) | copy-done | bytes 1048600
  3.5 1.7 %prepare.1.coords = f32[32,1024]{1,0:T(8,128)} custom-call(s32[5,16384]{1,0:T(8,128)} %cell_x.1, s32[128,128]{1,0:T(8,128)} %bitcast.4, f32[128,128]{1,0:T(8,128)} %bitcast.5, f32[4]{0:T(128)} %slowness.1), custom_call_target="tpu_custom_call" | custom-call | flops 754974720 | bytes 2097152 | tf_op jit(solution)/shard_map/prepare/pallas_call | solution.py:131
  5.2 0.9 %copy-done = f32[32,1024]{1,0:T(8,128)S(1)} copy-done((f32[32,1024]{1,0:T(8,128)S(1)}, f32[32,1024]{1,0:T(8,128)}, u32[]{:S(2)}) %copy-start) | copy-done | bytes 131096
  6.1 2.2 %shard_map.73.refs_0_.near = bf16[1024,1024]{1,0:T(8,128)(2,1)S(1)} custom-call(f32[32,1024]{1,0:T(8,128)S(1)} %copy-done, bf16[256,128]{1,0:T(8,128)(2,1)S(1)} %collective-permute-done.refs_0_.near_edge), custom_call_target="tpu_custom_call" | custom-call | flops 1006632960 | bytes 2097152 | tf_op jit(solution)/shard_map/pallas_call | solution.py:184
  8.3 6.0 %redatum.1.refs_0_.mine = bf16[256,1024]{1,0:T(8,128)(2,1)S(1)} custom-call(bf16[256,128]{1,0:T(8,128)(2,1)S(1)} %collective-permute-done.refs_0_.near_edge, bf16[256,1024]{1,0:T(8,128)(2,1)S(1)} %copy-done.3, bf16[256,128]{1,0:T(8,128)(2,1)S(1)} %collective-permute-done.1.far_edge, f32[65,256]{1,0:T(8,128)S(1)} %bitcast.3, ...), custom_call_target="tpu_custom_call" | custom-call | flops 3019898880 | bytes 1048576 | tf_op jit(solution)/shard_map/redatum/pallas_call | solution.py:224
  14.3 3.9 %collective-permute-start.2 = (bf16[256,1024]{1,0:T(8,128)(2,1)S(1)}, bf16[256,1024]{1,0:T(8,128)(2,1)S(1)}, u32[]{:S(2)}, u32[]{:S(2)}) collective-permute-start(bf16[256,1024]{1,0:T(8,128)(2,1)S(1)} %redatum.1.refs_0_.mine), channel_id=1, source_target_pairs={{0,1},{1,0},{2,3},{3,2},{4,5},{5,4},{6,7},{7,6},{8,9},{9,8},{10,11... | collective-permute-start | bytes 1572872 | tf_op jit(solution)/shard_map/ppermute | solution.py:42
  18.2 2.2 %shard_map.74.far.refs_0_ = bf16[1024,1024]{1,0:T(8,128)(2,1)S(1)} custom-call(f32[32,1024]{1,0:T(8,128)S(1)} %copy-done.1, bf16[256,1024]{1,0:T(8,128)(2,1)S(1)} %redatum.1.refs_0_.mine), custom_call_target="tpu_custom_call" | custom-call | flops 1006632960 | bytes 2097152 | tf_op jit(solution)/shard_map/pallas_call | solution.py:184
  20.4 0.7 %mix.6.refs_0_.mine = bf16[128,1024]{1,0:T(8,128)(2,1)S(1)} custom-call(bf16[256,1024]{1,0:T(8,128)(2,1)S(1)} %redatum.1.refs_0_.mine, bf16[256,1024]{1,0:T(8,128)(2,1)S(1)} %collective-permute-done.2.theirs, bf16[1024,1024]{1,0:T(8,128)(2,1)S(1)} %shard_map.73.refs_0_.near, bf16[1024,1024]{1,0:T(8,128)(2,1)S(1)} %shard_map.74.far.refs_0_, ...), custom_call_target="tpu_custom_call" | custom-call | flops 377487360 | bytes 4194304 | tf_op jit(solution)/shard_map/mix/pallas_call | solution.py:251
  21.1 1.9 %collective-permute-start.4 = (bf16[128,1024]{1,0:T(8,128)(2,1)S(1)}, bf16[128,1024]{1,0:T(8,128)(2,1)S(1)}, u32[]{:S(2)}, u32[]{:S(2)}) collective-permute-start(bf16[128,1024]{1,0:T(8,128)(2,1)S(1)} %mix.6.refs_0_.mine), channel_id=1, source_target_pairs={{0,2},{1,3},{2,0},{3,1},{4,6},{5,7},{6,4},{7,5},{8,10},{9,11},{10,... | collective-permute-start | bytes 786440 | tf_op jit(solution)/shard_map/ppermute | solution.py:42
  23.0 2.6 %collective-permute-start.7 = (bf16[256,1024]{1,0:T(8,128)(2,1)S(1)}, bf16[256,1024]{1,0:T(8,128)(2,1)S(1)}, u32[]{:S(2)}, u32[]{:S(2)}) collective-permute-start(bf16[256,1024]{1,0:T(8,128)(2,1)S(1)} %mark.1.refs_2_.refs_1_), channel_id=1, source_target_pairs={{0,8},{1,9},{2,10},{3,11},{4,12},{5,13},{6,14},{7,15},{8,0},{9,1},... | collective-permute-start | bytes 1572872 | tf_op jit(solution)/shard_map/ppermute | solution.py:42
  25.6 0.7 %mix.7.refs_0_.mine = bf16[128,1024]{1,0:T(8,128)(2,1)S(1)} custom-call(bf16[256,1024]{1,0:T(8,128)(2,1)S(1)} %redatum.1.refs_0_.mine, bf16[256,1024]{1,0:T(8,128)(2,1)S(1)} %collective-permute-done.2.theirs, bf16[1024,1024]{1,0:T(8,128)(2,1)S(1)} %shard_map.73.refs_0_.near, bf16[1024,1024]{1,0:T(8,128)(2,1)S(1)} %shard_map.74.far.refs_0_, ...), custom_call_target="tpu_custom_call" | custom-call | flops 377487360 | bytes 4194304 | tf_op jit(solution)/shard_map/mix/pallas_call | solution.py:251
  26.4 0.4 collective-permute-start.3
  26.8 4.3 %shard_map.75 = (bf16[1024,1024]{1,0:T(8,128)(2,1)S(1)}, bf16[1024,1024]{1,0:T(8,128)(2,1)S(1)}) custom-call(f32[32,1024]{1,0:T(8,128)S(1)} %copy-done.1, bf16[128,1024]{1,0:T(8,128)(2,1)S(1)} %mix.7.refs_0_.mine), custom_call_target="tpu_custom_call" | custom-call | flops 2013265920 | bytes 4194304 | tf_op jit(solution)/shard_map/pallas_call | solution.py:184
  31.1 0.7 %mix.8.refs_0_.mine = bf16[128,1024]{1,0:T(8,128)(2,1)S(1)} custom-call(bf16[128,1024]{1,0:T(8,128)(2,1)S(1)} %mix.6.refs_0_.mine, bf16[128,1024]{1,0:T(8,128)(2,1)S(1)} %collective-permute-done.4.theirs, bf16[1024,1024]{1,0:T(8,128)(2,1)S(1)} %get-tuple-element.18.near.refs_0_, bf16[1024,1024]{1,0:T(8,128)(2,1)S(1)} %get-tuple-element.19.far, ...), custom_call_target="tpu_custom_call" | custom-call | flops 377487360 | bytes 4194304 | tf_op jit(solution)/shard_map/mix/pallas_call | solution.py:251
  31.8 1.6 %collective-permute-start.6 = (bf16[128,1024]{1,0:T(8,128)(2,1)S(1)}, bf16[128,1024]{1,0:T(8,128)(2,1)S(1)}, u32[]{:S(2)}, u32[]{:S(2)}) collective-permute-start(bf16[128,1024]{1,0:T(8,128)(2,1)S(1)} %mix.8.refs_0_.mine), channel_id=1, source_target_pairs={{0,4},{1,5},{2,6},{3,7},{4,0},{5,1},{6,2},{7,3},{8,12},{9,13},{10,... | collective-permute-start | bytes 786440 | tf_op jit(solution)/shard_map/ppermute | solution.py:42
  33.5 4.3 %shard_map.76 = (bf16[1024,1024]{1,0:T(8,128)(2,1)S(1)}, bf16[1024,1024]{1,0:T(8,128)(2,1)S(1)}) custom-call(f32[32,1024]{1,0:T(8,128)S(1)} %copy-done.1, bf16[128,1024]{1,0:T(8,128)(2,1)S(1)} %mix.8.refs_0_.mine), custom_call_target="tpu_custom_call" | custom-call | flops 2013265920 | bytes 4194304 | tf_op jit(solution)/shard_map/pallas_call | solution.py:184
  37.8 0.7 %mix.9.refs_0_.mine = bf16[128,1024]{1,0:T(8,128)(2,1)S(1)} custom-call(bf16[128,1024]{1,0:T(8,128)(2,1)S(1)} %mix.7.refs_0_.mine, bf16[128,1024]{1,0:T(8,128)(2,1)S(1)} %collective-permute-done.3.theirs, bf16[1024,1024]{1,0:T(8,128)(2,1)S(1)} %get-tuple-element.18.near.refs_0_, bf16[1024,1024]{1,0:T(8,128)(2,1)S(1)} %get-tuple-element.19.far, ...), custom_call_target="tpu_custom_call" | custom-call | flops 377487360 | bytes 4194304 | tf_op jit(solution)/shard_map/mix/pallas_call | solution.py:251
  38.5 0.5 collective-permute-start.5
  39.1 4.3 %shard_map.77 = (bf16[1024,1024]{1,0:T(8,128)(2,1)S(1)}, bf16[1024,1024]{1,0:T(8,128)(2,1)S(1)}) custom-call(f32[32,1024]{1,0:T(8,128)S(1)} %copy-done.1, bf16[128,1024]{1,0:T(8,128)(2,1)S(1)} %mix.9.refs_0_.mine), custom_call_target="tpu_custom_call" | custom-call | flops 2013265920 | bytes 4194304 | tf_op jit(solution)/shard_map/pallas_call | solution.py:184
  43.4 7.2 %collective-permute-done.6.theirs = bf16[128,1024]{1,0:T(8,128)(2,1)S(1)} collective-permute-done((bf16[128,1024]{1,0:T(8,128)(2,1)S(1)}, bf16[128,1024]{1,0:T(8,128)(2,1)S(1)}, u32[]{:S(2)}, u32[]{:S(2)}) %collective-permute-start.6) | collective-permute-done | bytes 262176 | tf_op jit(solution)/shard_map/ppermute | solution.py:42
  50.6 0.7 %mix.10.state = bf16[128,1024]{1,0:T(8,128)(2,1)S(1)} custom-call(bf16[128,1024]{1,0:T(8,128)(2,1)S(1)} %mix.8.refs_0_.mine, bf16[128,1024]{1,0:T(8,128)(2,1)S(1)} %collective-permute-done.6.theirs, bf16[1024,1024]{1,0:T(8,128)(2,1)S(1)} %get-tuple-element.20.refs_0_.near, bf16[1024,1024]{1,0:T(8,128)(2,1)S(1)} %get-tuple-element.21.far, ...), custom_call_target="tpu_custom_call" | custom-call | flops 377487360 | bytes 4194304 | tf_op jit(solution)/shard_map/mix/pallas_call | solution.py:251
  51.3 0.8 %shard_map.78 = (f32[1,1024]{1,0:T(1,128)S(1)}, f32[1,1024]{1,0:T(1,128)S(1)}) custom-call(bf16[128,1024]{1,0:T(8,128)(2,1)S(1)} %mix.10.state, f32[32,1024]{1,0:T(8,128)S(1)} %copy-done.1, bf16[1024,1024]{1,0:T(8,128)(2,1)S(1)} %get-tuple-element.22.refs_0_, bf16[1024,1024]{1,0:T(8,128)(2,1)S(1)} %get-tuple-element.23.refs_1_.refs_0_, ...), custom_call_target="tpu_custom_call" | custom-call | flops 402653184 | bytes 4194304 | tf_op jit(solution)/shard_map/pallas_call | solution.py:288
  52.1 3.2 %collective-permute-done.5.theirs = bf16[128,1024]{1,0:T(8,128)(2,1)S(1)} collective-permute-done((bf16[128,1024]{1,0:T(8,128)(2,1)S(1)}, bf16[128,1024]{1,0:T(8,128)(2,1)S(1)}, u32[]{:S(2)}, u32[]{:S(2)}) %collective-permute-start.5) | collective-permute-done | bytes 262176 | tf_op jit(solution)/shard_map/ppermute | solution.py:42
  55.3 0.7 %mix.11.state = bf16[128,1024]{1,0:T(8,128)(2,1)S(1)} custom-call(bf16[128,1024]{1,0:T(8,128)(2,1)S(1)} %mix.9.refs_0_.mine, bf16[128,1024]{1,0:T(8,128)(2,1)S(1)} %collective-permute-done.5.theirs, bf16[1024,1024]{1,0:T(8,128)(2,1)S(1)} %get-tuple-element.20.refs_0_.near, bf16[1024,1024]{1,0:T(8,128)(2,1)S(1)} %get-tuple-element.21.far, ...), custom_call_target="tpu_custom_call" | custom-call | flops 377487360 | bytes 4194304 | tf_op jit(solution)/shard_map/mix/pallas_call | solution.py:251
  56.1 0.5 shard_map.79.refs_3_
  56.5 0.8 %collective-permute-start.8 = (f32[1,1024]{1,0:T(1,128)S(1)}, f32[1,1024]{1,0:T(1,128)S(1)}, u32[]{:S(2)}, u32[]{:S(2)}) collective-permute-start(f32[1,1024]{1,0:T(1,128)S(1)} %shard_map.79.refs_3_), channel_id=1, source_target_pairs={{0,8},{1,9},{2,10},{3,11},{4,12},{5,13},{6,14},{7,15},{8,0},{9,1},... | collective-permute-start | bytes 12296 | tf_op jit(solution)/shard_map/ppermute | solution.py:42
  57.3 0.5 shard_map.80
  57.8 3.3 %collective-permute-done.8 = f32[1,1024]{1,0:T(1,128)S(1)} collective-permute-done((f32[1,1024]{1,0:T(1,128)S(1)}, f32[1,1024]{1,0:T(1,128)S(1)}, u32[]{:S(2)}, u32[]{:S(2)}) %collective-permute-start.8) | collective-permute-done | bytes 4128 | tf_op jit(solution)/shard_map/ppermute | solution.py:42
  61.1 0.6 add.11
  (15 shorter events, 0.1 us)
Async XLA Ops:
  0.9 4.3 %collective-permute-start = (bf16[256,128]{1,0:T(8,128)(2,1)S(1)}, bf16[256,128]{1,0:T(8,128)(2,1)S(1)}, u32[]{:S(2)}, u32[]{:S(2)}) collective-permute-start(bf16[256,128]{1,0:T(8,128)(2,1)S(1)} %get-tuple-element.28), channel_id=1, source_target_pairs={{0,1},{1,0},{2,3},{3,2},{4,5},{5,4},{6,7},{7,6},{8,9},{9,8},{10,11... | collective-permute-start | bytes 196616 | tf_op jit(solution)/shard_map/ppermute | solution.py:42
  1.4 3.7 %collective-permute-start.1 = (bf16[256,128]{1,0:T(8,128)(2,1)S(1)}, bf16[256,128]{1,0:T(8,128)(2,1)S(1)}, u32[]{:S(2)}, u32[]{:S(2)}) collective-permute-start(bf16[256,128]{1,0:T(8,128)(2,1)S(1)} %get-tuple-element.27), channel_id=1, source_target_pairs={{1,2},{2,1},{3,4},{4,3},{5,6},{6,5},{7,8},{8,7},{9,10},{10,9},{11,... | collective-permute-start | bytes 196616 | tf_op jit(solution)/shard_map/ppermute | solution.py:38
  2.1 1.2 %copy-start.2 = (s32[256,1024]{1,0:T(8,128)S(1)}, s32[256,1024]{1,0:T(8,128)}, u32[]{:S(2)}) copy-start(s32[256,1024]{1,0:T(8,128)} %aperture.1) | copy-start | bytes 3145732
  3.4 4.8 %copy-start.3 = (bf16[256,1024]{1,0:T(8,128)(2,1)S(1)}, bf16[256,1024]{1,0:T(8,128)(2,1)}, u32[]{:S(2)}) copy-start(bf16[256,1024]{1,0:T(8,128)(2,1)} %wave.1) | copy-start | bytes 1572868
  3.4 4.8 %copy-start.4 = (f32[256,65]{0,1:T(8,128)S(1)}, f32[256,65]{0,1:T(8,128)}, u32[]{:S(2)}) copy-start(f32[256,65]{0,1:T(8,128)} %param.8) | copy-start | bytes 199684
  5.2 0.9 %copy-start = (f32[32,1024]{1,0:T(8,128)S(1)}, f32[32,1024]{1,0:T(8,128)}, u32[]{:S(2)}) copy-start(f32[32,1024]{1,0:T(8,128)} %prepare.1.coords) | copy-start | bytes 393220
  8.3 9.9 %copy-start.1 = (f32[32,1024]{1,0:T(8,128)S(1)}, f32[32,1024]{1,0:T(8,128)}, u32[]{:S(2)}) copy-start(f32[32,1024]{1,0:T(8,128)} %prepare.1.coords) | copy-start | bytes 393220
  14.3 6.1 %collective-permute-start.2 = (bf16[256,1024]{1,0:T(8,128)(2,1)S(1)}, bf16[256,1024]{1,0:T(8,128)(2,1)S(1)}, u32[]{:S(2)}, u32[]{:S(2)}) collective-permute-start(bf16[256,1024]{1,0:T(8,128)(2,1)S(1)} %redatum.1.refs_0_.mine), channel_id=1, source_target_pairs={{0,1},{1,0},{2,3},{3,2},{4,5},{5,4},{6,7},{7,6},{8,9},{9,8},{10,11... | collective-permute-start | bytes 1572872 | tf_op jit(solution)/shard_map/ppermute | solution.py:42
  21.1 10.0 %collective-permute-start.4 = (bf16[128,1024]{1,0:T(8,128)(2,1)S(1)}, bf16[128,1024]{1,0:T(8,128)(2,1)S(1)}, u32[]{:S(2)}, u32[]{:S(2)}) collective-permute-start(bf16[128,1024]{1,0:T(8,128)(2,1)S(1)} %mix.6.refs_0_.mine), channel_id=1, source_target_pairs={{0,2},{1,3},{2,0},{3,1},{4,6},{5,7},{6,4},{7,5},{8,10},{9,11},{10,... | collective-permute-start | bytes 786440 | tf_op jit(solution)/shard_map/ppermute | solution.py:42
  23.0 28.3 %collective-permute-start.7 = (bf16[256,1024]{1,0:T(8,128)(2,1)S(1)}, bf16[256,1024]{1,0:T(8,128)(2,1)S(1)}, u32[]{:S(2)}, u32[]{:S(2)}) collective-permute-start(bf16[256,1024]{1,0:T(8,128)(2,1)S(1)} %mark.1.refs_2_.refs_1_), channel_id=1, source_target_pairs={{0,8},{1,9},{2,10},{3,11},{4,12},{5,13},{6,14},{7,15},{8,0},{9,1},... | collective-permute-start | bytes 1572872 | tf_op jit(solution)/shard_map/ppermute | solution.py:42
  26.4 11.5 %collective-permute-start.3 = (bf16[128,1024]{1,0:T(8,128)(2,1)S(1)}, bf16[128,1024]{1,0:T(8,128)(2,1)S(1)}, u32[]{:S(2)}, u32[]{:S(2)}) collective-permute-start(bf16[128,1024]{1,0:T(8,128)(2,1)S(1)} %mix.7.refs_0_.mine), channel_id=1, source_target_pairs={{0,2},{1,3},{2,0},{3,1},{4,6},{5,7},{6,4},{7,5},{8,10},{9,11},{10,... | collective-permute-start | bytes 786440 | tf_op jit(solution)/shard_map/ppermute | solution.py:42
  31.8 18.7 %collective-permute-start.6 = (bf16[128,1024]{1,0:T(8,128)(2,1)S(1)}, bf16[128,1024]{1,0:T(8,128)(2,1)S(1)}, u32[]{:S(2)}, u32[]{:S(2)}) collective-permute-start(bf16[128,1024]{1,0:T(8,128)(2,1)S(1)} %mix.8.refs_0_.mine), channel_id=1, source_target_pairs={{0,4},{1,5},{2,6},{3,7},{4,0},{5,1},{6,2},{7,3},{8,12},{9,13},{10,... | collective-permute-start | bytes 786440 | tf_op jit(solution)/shard_map/ppermute | solution.py:42
  38.5 16.8 %collective-permute-start.5 = (bf16[128,1024]{1,0:T(8,128)(2,1)S(1)}, bf16[128,1024]{1,0:T(8,128)(2,1)S(1)}, u32[]{:S(2)}, u32[]{:S(2)}) collective-permute-start(bf16[128,1024]{1,0:T(8,128)(2,1)S(1)} %mix.9.refs_0_.mine), channel_id=1, source_target_pairs={{0,4},{1,5},{2,6},{3,7},{4,0},{5,1},{6,2},{7,3},{8,12},{9,13},{10,... | collective-permute-start | bytes 786440 | tf_op jit(solution)/shard_map/ppermute | solution.py:42
  56.5 4.6 %collective-permute-start.8 = (f32[1,1024]{1,0:T(1,128)S(1)}, f32[1,1024]{1,0:T(1,128)S(1)}, u32[]{:S(2)}, u32[]{:S(2)}) collective-permute-start(f32[1,1024]{1,0:T(1,128)S(1)} %shard_map.79.refs_3_), channel_id=1, source_target_pairs={{0,8},{1,9},{2,10},{3,11},{4,12},{5,13},{6,14},{7,15},{8,0},{9,1},... | collective-permute-start | bytes 12296 | tf_op jit(solution)/shard_map/ppermute | solution.py:42

commit v2 on v1

--- a/solution.py
+++ b/solution.py
@@ -60,8 +60,8 @@
 ROW, OTHER_ROW, COLUMN, BELOW, OTHER_COLUMN, OTHER_BELOW, WEIGHT, OTHER_WEIGHT = range(8)
 
 
-def prepare_kernel(blocks, count, width, cell_x, depth, illumination, slowness, *refs):
-    coords, cells, depths, lights, slow, sems = refs[-6:]
+def prepare_kernel(blocks, count, width, aperture, cell_x, depth, illumination, slowness, *refs):
+    mask, coords, cells, depths, lights, slow, marks, sems = refs[-8:]
     tall = width // LANES
     box = boxes_of(0, blocks)[0]
     others = [boxes_of(level, blocks)[1] for level in range(LEVELS)]
@@ -74,7 +74,8 @@
         copies.append(pltpu.make_async_copy(depth.at[at, :], depths.at[k], sems.at[6 + k]))
         light = illumination.at[at, :]
         copies.append(pltpu.make_async_copy(light, lights.at[k], sems.at[10 + k]))
-    for copy in copies:
+    marking = pltpu.make_async_copy(aperture, marks, sems.at[8])
+    for copy in copies + [marking]:
         copy.start()
     for copy in copies:
         copy.wait()
@@ -107,43 +108,33 @@
             coords[base + kind : base + kind + 1, k * LANES : (k + 1) * LANES] = (
                 lights[source, k : k + 1, :] * share
             )
-
-
-def mark_kernel(aperture, *refs):
-    mask = refs[-1]
-    mask[...] = (aperture[...] > 0).astype(jnp.float32).astype(jnp.bfloat16)
-
-
-def mark(aperture, *after):
-    return pl.pallas_call(
-        mark_kernel,
-        out_shape=jax.ShapeDtypeStruct(aperture.shape, jnp.bfloat16),
-        in_specs=[VMEM] + [ANY] * len(after),
-        out_specs=VMEM,
-        compiler_params=params(4),
-        cost_estimate=cost(aperture.size * 200, aperture.size * 6),
-        name="mark",
-    )(aperture, *after)
-
-
-def prepare(blocks, count, width, cell_x, depth, illumination, slowness, *after):
+    marking.wait()
+    mask[...] = (marks[...] > 0).astype(jnp.float32).astype(jnp.bfloat16)
+
+
+def prepare(blocks, aperture, cell_x, depth, illumination, slowness):
+    count, width = aperture.shape
     levels = cell_x.shape[0]
     return pl.pallas_call(
         functools.partial(prepare_kernel, blocks, count, width),
-        out_shape=jax.ShapeDtypeStruct((8 * LEVELS, width), jnp.float32),
-        in_specs=[HBM] * 4 + [ANY] * len(after),
-        out_specs=VMEM,
+        out_shape=(
+            jax.ShapeDtypeStruct((count, width), jnp.bfloat16),
+            jax.ShapeDtypeStruct((8 * LEVELS, width), jnp.float32),
+        ),
+        in_specs=[HBM] * 5,
+        out_specs=(VMEM, VMEM),
         scratch_shapes=[
             pltpu.VMEM((1 + LEVELS, levels, width), jnp.int32),
             pltpu.VMEM((2, width // LANES, LANES), jnp.int32),
             pltpu.VMEM((2, width // LANES, LANES), jnp.float32),
             pltpu.SMEM((LEVELS,), jnp.float32),
+            pltpu.VMEM((count, width), jnp.int32),
             pltpu.SemaphoreType.DMA((12,)),
         ],
         compiler_params=pltpu.CompilerParams(vmem_limit_bytes=GRANT),
         cost_estimate=cost(24 * 2 * width * width * 15, count * width * 8),
         name="prepare",
-    )(cell_x, depth, illumination, slowness, *after)
+    )(aperture, cell_x, depth, illumination, slowness)
 
 
 def tables_kernel(jobs, step, coords, *refs):
@@ -307,8 +298,7 @@
     head, tail = wavefield[:, :LANES], wavefield[:, width - LANES :]
     far_edge = across(jnp.where(even, head, tail), "space", blocks)
     near_edge = partner(jnp.where(even, tail, head), "space", block_bits)
-    coords = prepare(blocks, count, width, cell_x, depth, light, slowness)
-    mask = mark(aperture)
+    mask, coords = prepare(blocks, aperture, cell_x, depth, light, slowness)
     taps = redatum_taps
     if blocks > 1:
         taps = lax.dynamic_slice_in_dim(redatum_taps, block * count, count, 0)
@@ -325,26 +315,32 @@
     theirs = [received for _ in parts]
     table, ahead = (near, far), far
     both, sums = (mask, masks), ()
-    for level in range(LEVELS - 1):
-        for part in parts:
-            states[part] = mix(part, states[part], theirs[part], *table, ahead)
-            ahead = states[part]
-            if level + 2 == LEVELS and part + 1 < len(parts):
-                sums = last(part, (0, 1), states[part], coords, later, both, sums)
-                ahead = sums[0]
-            if level + 2 == LEVELS and part + 1 == len(parts):
-                final = (states[part], coords, later, both)
-                (other,) = last(part, (1,), *final, sums[1:])
-                (own,) = last(part, (0,), *final, sums[:1], other)
-            if level + 2 < LEVELS:
-                theirs[part] = partner(states[part], "space", level + 1 + block_bits)
-            if part == (0 if level == 1 else len(parts) - 1) and level < 2:
-                following = tables(level + 1, (0, 1), coords, ahead)
-                ahead = following[0]
-            if part == len(parts) - 1 and level == 1:
-                later = tables(level + 2, (0, 1), coords, ahead)
-                ahead = later[0]
-        table = following
+    end = len(parts) - 1
+    for part in parts:
+        states[part] = mix(part, states[part], theirs[part], *table, ahead)
+        ahead = states[part]
+        theirs[part] = partner(states[part], "space", 1 + block_bits)
+    second = tables(1, (0, 1), coords, ahead)
+    (near,) = tables(2, (0,), coords, second[0])
+    ahead = near
+    for part in parts:
+        states[part] = mix(part, states[part], theirs[part], *second, ahead)
+        ahead = states[part]
+        theirs[part] = partner(states[part], "space", 2 + block_bits)
+        if part == 0:
+            (far,) = tables(2, (1,), coords, ahead)
+            ahead = far
+    later = tables(3, (0, 1), coords, ahead)
+    ahead = later[0]
+    for part in parts:
+        states[part] = mix(part, states[part], theirs[part], near, far, ahead)
+        final = (states[part], coords, later, both)
+        if part < end:
+            sums = last(part, (0, 1), *final, sums)
+            ahead = sums[0]
+        else:
+            (other,) = last(part, (1,), *final, sums[1:])
+            (own,) = last(part, (0,), *final, sums[:1], other)
     image = own + partner(other, "space", LEVELS - 1 + block_bits)
     for level in range(block_bits):
         image = image + partner(image, "space", level)

time: 62 us -> 62.4 us (level)
  starting transfers between devices: 13 us -> 15.6 us
  waiting for transfers between devices: 13.7 us -> 12.2 us
  local copies, waits for them, and re-layouts: 2.13 us -> 0.92 us
  Pallas kernels: 31.1 us -> 31.8 us
    ppermute x8, starting transfers between devices: 12.3 us -> 14.9 us  [partner(): lax.ppermute(shard, axis, [(i, i ^ 1 << bit) for i in range(lax.axis_size...]
    ppermute x8, waiting for transfers between devices: 13.7 us -> 12.2 us  [partner(): lax.ppermute(shard, axis, [(i, i ^ 1 << bit) for i in range(lax.axis_size...]
    unnamed x10, local copies, waits for them, and re-layouts: 2.13 us -> 0.92 us
    pallas_call x1, Pallas kernels: 1.71 us -> 2.42 us  [prepare(): pl.pallas_call(functools.partial(prepare_kernel, blocks, count, width), o...]
    pallas_call x5 -> x6, Pallas kernels: 17.3 us -> 17.3 us  [tables(): pl.pallas_call(functools.partial(tables_kernel, jobs, step), out_shape=(s...]
  transfers between devices with their start and end apart: 9 -> 9, of which waited for: 3 -> 3; matrix products, arithmetic and copies ran while one was open for 0% -> 0% of each run, Pallas kernels for 34% -> 36%
where the time goes in v2:
time: 62.4 us; the launch traced here: 62.2 us
  Pallas kernels  31.8 us (51%)
  starting transfers between devices  15.6 us (25%)
  waiting for transfers between devices  12.2 us (20%)
  other arithmetic  1.48 us (2%)
  local copies, waits for them, and re-layouts  0.92 us (1%)
    pallas_call x6, Pallas kernels, tables(): pl.pallas_call(functools.partial(tables_kernel, jobs, step), out_shape=(s...  17.3 us
    ppermute x8, starting transfers between devices, partner(): lax.ppermute(shard, axis, [(i, i ^ 1 << bit) for i in range(lax.axis_size...  14.9 us
    ppermute x8, waiting for transfers between devices, partner(): lax.ppermute(shard, axis, [(i, i ^ 1 << bit) for i in range(lax.axis_size...  12.2 us
    pallas_call x1, Pallas kernels, redatum(): pl.pallas_call(functools.partial(redatum_kernel, reach, blocks), out_shap...  5.96 us
    pallas_call x6, Pallas kernels, mix(): pl.pallas_call(functools.partial(mix_kernel, held), out_shape=jax.ShapeDt...  4.34 us
    pallas_call x1, Pallas kernels, prepare(): pl.pallas_call(functools.partial(prepare_kernel, blocks, count, width), o...  2.42 us
    pallas_call x3, Pallas kernels, last(): pl.pallas_call(functools.partial(last_kernel, part, weights, len(sums)),...  1.72 us
  transfers between devices with their start and end apart: 9, of which 3 were waited for; matrix products, arithmetic and copies ran while one was open for 0% of the time, Pallas kernels for 36%

profile of v2, /device:TPU:0, one launch (start us, length us, event | category | flops | bytes accessed | tf_op | source)
XLA Modules:
  0.0 62.2 jit_solution(4688817925706464927)
XLA Ops:
  0.0 0.9 %broadcast_select_fusion = (bf16[256,128]{1,0:T(8,128)(2,1)S(1)}, bf16[256,128]{1,0:T(8,128)(2,1)S(1)}) fusion(pred[]{:T(512)S(6)} %eq.6, bf16[256,1024]{1,0:T(8,128)(2,1)} %wave.1), kind=kLoop, calls=%fused_computation | loop fusion | flops 65536 | bytes 262145 | tf_op jit(solution)/shard_map/jit(_where)/select_n | solution.py:299
  0.9 0.6 collective-permute-start
  1.4 0.7 %collective-permute-start.1 = (bf16[256,128]{1,0:T(8,128)(2,1)S(1)}, bf16[256,128]{1,0:T(8,128)(2,1)S(1)}, u32[]{:S(2)}, u32[]{:S(2)}) collective-permute-start(bf16[256,128]{1,0:T(8,128)(2,1)S(1)} %get-tuple-element.27), channel_id=1, source_target_pairs={{1,2},{2,1},{3,4},{4,3},{5,6},{6,5},{7,8},{8,7},{9,10},{10,9},{11,... | collective-permute-start | bytes 196616 | tf_op jit(solution)/shard_map/ppermute | solution.py:38
  2.1 2.4 %prepare.1 = (bf16[256,1024]{1,0:T(8,128)(2,1)}, f32[32,1024]{1,0:T(8,128)}) custom-call(s32[256,1024]{1,0:T(8,128)} %aperture.1, s32[5,16384]{1,0:T(8,128)} %cell_x.1, s32[128,128]{1,0:T(8,128)} %bitcast.4, f32[128,128]{1,0:T(8,128)} %bitcast.5, f32[4]{0:T(128)} %slowness.1), custom_call_target="tpu_custom_call" | custom-call | flops 754974720 | bytes 2097152 | tf_op jit(solution)/shard_map/prepare/pallas_call | solution.py:118
  4.6 0.9 %copy-done = f32[32,1024]{1,0:T(8,128)S(1)} copy-done((f32[32,1024]{1,0:T(8,128)S(1)}, f32[32,1024]{1,0:T(8,128)}, u32[]{:S(2)}) %copy-start) | copy-done | bytes 131096
  5.5 2.2 %shard_map.73.refs_0_.near = bf16[1024,1024]{1,0:T(8,128)(2,1)S(1)} custom-call(f32[32,1024]{1,0:T(8,128)S(1)} %copy-done, bf16[256,128]{1,0:T(8,128)(2,1)S(1)} %collective-permute-done.refs_0_.near_edge), custom_call_target="tpu_custom_call" | custom-call | flops 1006632960 | bytes 2097152 | tf_op jit(solution)/shard_map/pallas_call | solution.py:175
  7.7 6.0 %redatum.1.refs_0_.mine = bf16[256,1024]{1,0:T(8,128)(2,1)S(1)} custom-call(bf16[256,128]{1,0:T(8,128)(2,1)S(1)} %collective-permute-done.refs_0_.near_edge, bf16[256,1024]{1,0:T(8,128)(2,1)S(1)} %copy-done.3, bf16[256,128]{1,0:T(8,128)(2,1)S(1)} %collective-permute-done.1.far_edge, f32[65,256]{1,0:T(8,128)S(1)} %bitcast.3, ...), custom_call_target="tpu_custom_call" | custom-call | flops 3019898880 | bytes 1048576 | tf_op jit(solution)/shard_map/redatum/pallas_call | solution.py:215
  13.7 3.9 %collective-permute-start.2 = (bf16[256,1024]{1,0:T(8,128)(2,1)S(1)}, bf16[256,1024]{1,0:T(8,128)(2,1)S(1)}, u32[]{:S(2)}, u32[]{:S(2)}) collective-permute-start(bf16[256,1024]{1,0:T(8,128)(2,1)S(1)} %redatum.1.refs_0_.mine), channel_id=1, source_target_pairs={{0,1},{1,0},{2,3},{3,2},{4,5},{5,4},{6,7},{7,6},{8,9},{9,8},{10,11... | collective-permute-start | bytes 1572872 | tf_op jit(solution)/shard_map/ppermute | solution.py:42
  17.6 3.4 %collective-permute-start.7 = (bf16[256,1024]{1,0:T(8,128)(2,1)S(1)}, bf16[256,1024]{1,0:T(8,128)(2,1)S(1)}, u32[]{:S(2)}, u32[]{:S(2)}) collective-permute-start(bf16[256,1024]{1,0:T(8,128)(2,1)S(1)} %copy-done.2), channel_id=1, source_target_pairs={{0,8},{1,9},{2,10},{3,11},{4,12},{5,13},{6,14},{7,15},{8,0},{9,1},... | collective-permute-start | bytes 1572872 | tf_op jit(solution)/shard_map/ppermute | solution.py:42
  21.0 2.2 %shard_map.74.far.refs_0_ = bf16[1024,1024]{1,0:T(8,128)(2,1)S(1)} custom-call(f32[32,1024]{1,0:T(8,128)S(1)} %copy-done.1, bf16[256,1024]{1,0:T(8,128)(2,1)S(1)} %redatum.1.refs_0_.mine), custom_call_target="tpu_custom_call" | custom-call | flops 1006632960 | bytes 2097152 | tf_op jit(solution)/shard_map/pallas_call | solution.py:175
  23.1 0.7 %mix.6.refs_0_.mine = bf16[128,1024]{1,0:T(8,128)(2,1)S(1)} custom-call(bf16[256,1024]{1,0:T(8,128)(2,1)S(1)} %redatum.1.refs_0_.mine, bf16[256,1024]{1,0:T(8,128)(2,1)S(1)} %collective-permute-done.2.theirs, bf16[1024,1024]{1,0:T(8,128)(2,1)S(1)} %shard_map.73.refs_0_.near, bf16[1024,1024]{1,0:T(8,128)(2,1)S(1)} %shard_map.74.far.refs_0_, ...), custom_call_target="tpu_custom_call" | custom-call | flops 377487360 | bytes 4194304 | tf_op jit(solution)/shard_map/mix/pallas_call | solution.py:242
  23.9 1.8 %collective-permute-start.4 = (bf16[128,1024]{1,0:T(8,128)(2,1)S(1)}, bf16[128,1024]{1,0:T(8,128)(2,1)S(1)}, u32[]{:S(2)}, u32[]{:S(2)}) collective-permute-start(bf16[128,1024]{1,0:T(8,128)(2,1)S(1)} %mix.6.refs_0_.mine), channel_id=1, source_target_pairs={{0,2},{1,3},{2,0},{3,1},{4,6},{5,7},{6,4},{7,5},{8,10},{9,11},{10,... | collective-permute-start | bytes 786440 | tf_op jit(solution)/shard_map/ppermute | solution.py:42
  25.6 0.7 %mix.7.refs_0_.mine = bf16[128,1024]{1,0:T(8,128)(2,1)S(1)} custom-call(bf16[256,1024]{1,0:T(8,128)(2,1)S(1)} %redatum.1.refs_0_.mine, bf16[256,1024]{1,0:T(8,128)(2,1)S(1)} %collective-permute-done.2.theirs, bf16[1024,1024]{1,0:T(8,128)(2,1)S(1)} %shard_map.73.refs_0_.near, bf16[1024,1024]{1,0:T(8,128)(2,1)S(1)} %shard_map.74.far.refs_0_, ...), custom_call_target="tpu_custom_call" | custom-call | flops 377487360 | bytes 4194304 | tf_op jit(solution)/shard_map/mix/pallas_call | solution.py:242
  26.4 0.4 collective-permute-start.3
  26.8 4.3 %shard_map.75 = (bf16[1024,1024]{1,0:T(8,128)(2,1)S(1)}, bf16[1024,1024]{1,0:T(8,128)(2,1)S(1)}) custom-call(f32[32,1024]{1,0:T(8,128)S(1)} %copy-done.1, bf16[128,1024]{1,0:T(8,128)(2,1)S(1)} %mix.7.refs_0_.mine), custom_call_target="tpu_custom_call" | custom-call | flops 2013265920 | bytes 4194304 | tf_op jit(solution)/shard_map/pallas_call | solution.py:175
  31.1 2.2 %shard_map.76.refs_0_.near = bf16[1024,1024]{1,0:T(8,128)(2,1)S(1)} custom-call(f32[32,1024]{1,0:T(8,128)S(1)} %copy-done.1, bf16[1024,1024]{1,0:T(8,128)(2,1)S(1)} %get-tuple-element.20.refs_0_.near), custom_call_target="tpu_custom_call" | custom-call | flops 1006632960 | bytes 2097152 | tf_op jit(solution)/shard_map/pallas_call | solution.py:175
  33.3 0.7 %mix.8.refs_0_.mine = bf16[128,1024]{1,0:T(8,128)(2,1)S(1)} custom-call(bf16[128,1024]{1,0:T(8,128)(2,1)S(1)} %mix.6.refs_0_.mine, bf16[128,1024]{1,0:T(8,128)(2,1)S(1)} %collective-permute-done.4.theirs, bf16[1024,1024]{1,0:T(8,128)(2,1)S(1)} %get-tuple-element.20.refs_0_.near, bf16[1024,1024]{1,0:T(8,128)(2,1)S(1)} %get-tuple-element.21.far, ...), custom_call_target="tpu_custom_call" | custom-call | flops 377487360 | bytes 4194304 | tf_op jit(solution)/shard_map/mix/pallas_call | solution.py:242
  34.0 1.6 %collective-permute-start.6 = (bf16[128,1024]{1,0:T(8,128)(2,1)S(1)}, bf16[128,1024]{1,0:T(8,128)(2,1)S(1)}, u32[]{:S(2)}, u32[]{:S(2)}) collective-permute-start(bf16[128,1024]{1,0:T(8,128)(2,1)S(1)} %mix.8.refs_0_.mine), channel_id=1, source_target_pairs={{0,4},{1,5},{2,6},{3,7},{4,0},{5,1},{6,2},{7,3},{8,12},{9,13},{10,... | collective-permute-start | bytes 786440 | tf_op jit(solution)/shard_map/ppermute | solution.py:42
  35.7 2.2 %shard_map.77.refs_0_.far = bf16[1024,1024]{1,0:T(8,128)(2,1)S(1)} custom-call(f32[32,1024]{1,0:T(8,128)S(1)} %copy-done.1, bf16[128,1024]{1,0:T(8,128)(2,1)S(1)} %mix.8.refs_0_.mine), custom_call_target="tpu_custom_call" | custom-call | flops 1006632960 | bytes 2097152 | tf_op jit(solution)/shard_map/pallas_call | solution.py:175
  37.8 0.7 %mix.9.refs_0_.mine = bf16[128,1024]{1,0:T(8,128)(2,1)S(1)} custom-call(bf16[128,1024]{1,0:T(8,128)(2,1)S(1)} %mix.7.refs_0_.mine, bf16[128,1024]{1,0:T(8,128)(2,1)S(1)} %collective-permute-done.3.theirs, bf16[1024,1024]{1,0:T(8,128)(2,1)S(1)} %get-tuple-element.20.refs_0_.near, bf16[1024,1024]{1,0:T(8,128)(2,1)S(1)} %get-tuple-element.21.far, ...), custom_call_target="tpu_custom_call" | custom-call | flops 377487360 | bytes 4194304 | tf_op jit(solution)/shard_map/mix/pallas_call | solution.py:242
  38.6 1.6 %collective-permute-start.5 = (bf16[128,1024]{1,0:T(8,128)(2,1)S(1)}, bf16[128,1024]{1,0:T(8,128)(2,1)S(1)}, u32[]{:S(2)}, u32[]{:S(2)}) collective-permute-start(bf16[128,1024]{1,0:T(8,128)(2,1)S(1)} %mix.9.refs_0_.mine), channel_id=1, source_target_pairs={{0,4},{1,5},{2,6},{3,7},{4,0},{5,1},{6,2},{7,3},{8,12},{9,13},{10,... | collective-permute-start | bytes 786440 | tf_op jit(solution)/shard_map/ppermute | solution.py:42
  40.2 4.3 %shard_map.78 = (bf16[1024,1024]{1,0:T(8,128)(2,1)S(1)}, bf16[1024,1024]{1,0:T(8,128)(2,1)S(1)}) custom-call(f32[32,1024]{1,0:T(8,128)S(1)} %copy-done.1, bf16[128,1024]{1,0:T(8,128)(2,1)S(1)} %mix.9.refs_0_.mine), custom_call_target="tpu_custom_call" | custom-call | flops 2013265920 | bytes 4194304 | tf_op jit(solution)/shard_map/pallas_call | solution.py:175
  44.5 5.8 %collective-permute-done.6.theirs = bf16[128,1024]{1,0:T(8,128)(2,1)S(1)} collective-permute-done((bf16[128,1024]{1,0:T(8,128)(2,1)S(1)}, bf16[128,1024]{1,0:T(8,128)(2,1)S(1)}, u32[]{:S(2)}, u32[]{:S(2)}) %collective-permute-start.6) | collective-permute-done | bytes 262176 | tf_op jit(solution)/shard_map/ppermute | solution.py:42
  50.3 0.7 %mix.10.state = bf16[128,1024]{1,0:T(8,128)(2,1)S(1)} custom-call(bf16[128,1024]{1,0:T(8,128)(2,1)S(1)} %mix.8.refs_0_.mine, bf16[128,1024]{1,0:T(8,128)(2,1)S(1)} %collective-permute-done.6.theirs, bf16[1024,1024]{1,0:T(8,128)(2,1)S(1)} %shard_map.76.refs_0_.near, bf16[1024,1024]{1,0:T(8,128)(2,1)S(1)} %shard_map.77.refs_0_.far, ...), custom_call_target="tpu_custom_call" | custom-call | flops 377487360 | bytes 4194304 | tf_op jit(solution)/shard_map/mix/pallas_call | solution.py:242
  51.0 0.8 %shard_map.79 = (f32[1,1024]{1,0:T(1,128)S(1)}, f32[1,1024]{1,0:T(1,128)S(1)}) custom-call(bf16[128,1024]{1,0:T(8,128)(2,1)S(1)} %mix.10.state, f32[32,1024]{1,0:T(8,128)S(1)} %copy-done.1, bf16[1024,1024]{1,0:T(8,128)(2,1)S(1)} %get-tuple-element.22.refs_0_, bf16[1024,1024]{1,0:T(8,128)(2,1)S(1)} %get-tuple-element.23.refs_1_.refs_0_, ...), custom_call_target="tpu_custom_call" | custom-call | flops 402653184 | bytes 4194304 | tf_op jit(solution)/shard_map/pallas_call | solution.py:279
  51.8 4.0 %collective-permute-done.5.theirs = bf16[128,1024]{1,0:T(8,128)(2,1)S(1)} collective-permute-done((bf16[128,1024]{1,0:T(8,128)(2,1)S(1)}, bf16[128,1024]{1,0:T(8,128)(2,1)S(1)}, u32[]{:S(2)}, u32[]{:S(2)}) %collective-permute-start.5) | collective-permute-done | bytes 262176 | tf_op jit(solution)/shard_map/ppermute | solution.py:42
  55.8 0.7 %mix.11.state = bf16[128,1024]{1,0:T(8,128)(2,1)S(1)} custom-call(bf16[128,1024]{1,0:T(8,128)(2,1)S(1)} %mix.9.refs_0_.mine, bf16[128,1024]{1,0:T(8,128)(2,1)S(1)} %collective-permute-done.5.theirs, bf16[1024,1024]{1,0:T(8,128)(2,1)S(1)} %shard_map.76.refs_0_.near, bf16[1024,1024]{1,0:T(8,128)(2,1)S(1)} %shard_map.77.refs_0_.far, ...), custom_call_target="tpu_custom_call" | custom-call | flops 377487360 | bytes 4194304 | tf_op jit(solution)/shard_map/mix/pallas_call | solution.py:242
  56.6 0.5 shard_map.80.refs_3_
  57.1 1.7 %collective-permute-start.8 = (f32[1,1024]{1,0:T(1,128)S(1)}, f32[1,1024]{1,0:T(1,128)S(1)}, u32[]{:S(2)}, u32[]{:S(2)}) collective-permute-start(f32[1,1024]{1,0:T(1,128)S(1)} %shard_map.80.refs_3_), channel_id=1, source_target_pairs={{0,8},{1,9},{2,10},{3,11},{4,12},{5,13},{6,14},{7,15},{8,0},{9,1},... | collective-permute-start | bytes 12296 | tf_op jit(solution)/shard_map/ppermute | solution.py:42
  58.7 0.5 shard_map.81
  59.2 2.4 %collective-permute-done.8 = f32[1,1024]{1,0:T(1,128)S(1)} collective-permute-done((f32[1,1024]{1,0:T(1,128)S(1)}, f32[1,1024]{1,0:T(1,128)S(1)}, u32[]{:S(2)}, u32[]{:S(2)}) %collective-permute-start.8) | collective-permute-done | bytes 4128 | tf_op jit(solution)/shard_map/ppermute | solution.py:42
  61.6 0.6 add.11
  (15 shorter events, 0.0 us)
Async XLA Ops:
  0.9 3.7 %collective-permute-start = (bf16[256,128]{1,0:T(8,128)(2,1)S(1)}, bf16[256,128]{1,0:T(8,128)(2,1)S(1)}, u32[]{:S(2)}, u32[]{:S(2)}) collective-permute-start(bf16[256,128]{1,0:T(8,128)(2,1)S(1)} %get-tuple-element.28), channel_id=1, source_target_pairs={{0,1},{1,0},{2,3},{3,2},{4,5},{5,4},{6,7},{7,6},{8,9},{9,8},{10,11... | collective-permute-start | bytes 196616 | tf_op jit(solution)/shard_map/ppermute | solution.py:42
  1.4 3.1 %collective-permute-start.1 = (bf16[256,128]{1,0:T(8,128)(2,1)S(1)}, bf16[256,128]{1,0:T(8,128)(2,1)S(1)}, u32[]{:S(2)}, u32[]{:S(2)}) collective-permute-start(bf16[256,128]{1,0:T(8,128)(2,1)S(1)} %get-tuple-element.27), channel_id=1, source_target_pairs={{1,2},{2,1},{3,4},{4,3},{5,6},{6,5},{7,8},{8,7},{9,10},{10,9},{11,... | collective-permute-start | bytes 196616 | tf_op jit(solution)/shard_map/ppermute | solution.py:38
  2.1 5.6 %copy-start.3 = (bf16[256,1024]{1,0:T(8,128)(2,1)S(1)}, bf16[256,1024]{1,0:T(8,128)(2,1)}, u32[]{:S(2)}) copy-start(bf16[256,1024]{1,0:T(8,128)(2,1)} %wave.1) | copy-start | bytes 1572868
  2.1 5.6 %copy-start.4 = (f32[256,65]{0,1:T(8,128)S(1)}, f32[256,65]{0,1:T(8,128)}, u32[]{:S(2)}) copy-start(f32[256,65]{0,1:T(8,128)} %param.8) | copy-start | bytes 199684
  4.6 0.9 %copy-start = (f32[32,1024]{1,0:T(8,128)S(1)}, f32[32,1024]{1,0:T(8,128)}, u32[]{:S(2)}) copy-start(f32[32,1024]{1,0:T(8,128)} %get-tuple-element.19.coords) | copy-start | bytes 393220
  7.7 9.9 %copy-start.2 = (bf16[256,1024]{1,0:T(8,128)(2,1)S(1)}, bf16[256,1024]{1,0:T(8,128)(2,1)}, u32[]{:S(2)}) copy-start(bf16[256,1024]{1,0:T(8,128)(2,1)} %get-tuple-element.24.refs_2_.refs_1_) | copy-start | bytes 1572868
  7.7 13.3 %copy-start.1 = (f32[32,1024]{1,0:T(8,128)S(1)}, f32[32,1024]{1,0:T(8,128)}, u32[]{:S(2)}) copy-start(f32[32,1024]{1,0:T(8,128)} %get-tuple-element.19.coords) | copy-start | bytes 393220
  13.7 9.5 %collective-permute-start.2 = (bf16[256,1024]{1,0:T(8,128)(2,1)S(1)}, bf16[256,1024]{1,0:T(8,128)(2,1)S(1)}, u32[]{:S(2)}, u32[]{:S(2)}) collective-permute-start(bf16[256,1024]{1,0:T(8,128)(2,1)S(1)} %redatum.1.refs_0_.mine), channel_id=1, source_target_pairs={{0,1},{1,0},{2,3},{3,2},{4,5},{5,4},{6,7},{7,6},{8,9},{9,8},{10,11... | collective-permute-start | bytes 1572872 | tf_op jit(solution)/shard_map/ppermute | solution.py:42
  17.6 33.4 %collective-permute-start.7 = (bf16[256,1024]{1,0:T(8,128)(2,1)S(1)}, bf16[256,1024]{1,0:T(8,128)(2,1)S(1)}, u32[]{:S(2)}, u32[]{:S(2)}) collective-permute-start(bf16[256,1024]{1,0:T(8,128)(2,1)S(1)} %copy-done.2), channel_id=1, source_target_pairs={{0,8},{1,9},{2,10},{3,11},{4,12},{5,13},{6,14},{7,15},{8,0},{9,1},... | collective-permute-start | bytes 1572872 | tf_op jit(solution)/shard_map/ppermute | solution.py:42
  23.9 9.4 %collective-permute-start.4 = (bf16[128,1024]{1,0:T(8,128)(2,1)S(1)}, bf16[128,1024]{1,0:T(8,128)(2,1)S(1)}, u32[]{:S(2)}, u32[]{:S(2)}) collective-permute-start(bf16[128,1024]{1,0:T(8,128)(2,1)S(1)} %mix.6.refs_0_.mine), channel_id=1, source_target_pairs={{0,2},{1,3},{2,0},{3,1},{4,6},{5,7},{6,4},{7,5},{8,10},{9,11},{10,... | collective-permute-start | bytes 786440 | tf_op jit(solution)/shard_map/ppermute | solution.py:42
  26.4 11.5 %collective-permute-start.3 = (bf16[128,1024]{1,0:T(8,128)(2,1)S(1)}, bf16[128,1024]{1,0:T(8,128)(2,1)S(1)}, u32[]{:S(2)}, u32[]{:S(2)}) collective-permute-start(bf16[128,1024]{1,0:T(8,128)(2,1)S(1)} %mix.7.refs_0_.mine), channel_id=1, source_target_pairs={{0,2},{1,3},{2,0},{3,1},{4,6},{5,7},{6,4},{7,5},{8,10},{9,11},{10,... | collective-permute-start | bytes 786440 | tf_op jit(solution)/shard_map/ppermute | solution.py:42
  34.0 16.3 %collective-permute-start.6 = (bf16[128,1024]{1,0:T(8,128)(2,1)S(1)}, bf16[128,1024]{1,0:T(8,128)(2,1)S(1)}, u32[]{:S(2)}, u32[]{:S(2)}) collective-permute-start(bf16[128,1024]{1,0:T(8,128)(2,1)S(1)} %mix.8.refs_0_.mine), channel_id=1, source_target_pairs={{0,4},{1,5},{2,6},{3,7},{4,0},{5,1},{6,2},{7,3},{8,12},{9,13},{10,... | collective-permute-start | bytes 786440 | tf_op jit(solution)/shard_map/ppermute | solution.py:42
  38.6 17.3 %collective-permute-start.5 = (bf16[128,1024]{1,0:T(8,128)(2,1)S(1)}, bf16[128,1024]{1,0:T(8,128)(2,1)S(1)}, u32[]{:S(2)}, u32[]{:S(2)}) collective-permute-start(bf16[128,1024]{1,0:T(8,128)(2,1)S(1)} %mix.9.refs_0_.mine), channel_id=1, source_target_pairs={{0,4},{1,5},{2,6},{3,7},{4,0},{5,1},{6,2},{7,3},{8,12},{9,13},{10,... | collective-permute-start | bytes 786440 | tf_op jit(solution)/shard_map/ppermute | solution.py:42
  57.1 4.6 %collective-permute-start.8 = (f32[1,1024]{1,0:T(1,128)S(1)}, f32[1,1024]{1,0:T(1,128)S(1)}, u32[]{:S(2)}, u32[]{:S(2)}) collective-permute-start(f32[1,1024]{1,0:T(1,128)S(1)} %shard_map.80.refs_3_), channel_id=1, source_target_pairs={{0,8},{1,9},{2,10},{3,11},{4,12},{5,13},{6,14},{7,15},{8,0},{9,1},... | collective-permute-start | bytes 12296 | tf_op jit(solution)/shard_map/ppermute | solution.py:42

commit v3 on v2

--- a/solution.py
+++ b/solution.py
@@ -183,65 +183,62 @@
     )(coords, *after)
 
 
-def redatum_kernel(reach, blocks, near_edge, wave, far_edge, taps, *refs):
+def redatum_kernel(reach, blocks, lane, near_edge, wave, far_edge, taps, *refs):
     out, padded = refs[-2:]
-    count, width = wave.shape
+    width = wave.shape[1]
     edge = near_edge.shape[1]
     even = 1 - boxes_of(0, blocks)[0] % 2
     after = edge + width
     starts = (pl.multiple_of(even * after, LANES), pl.multiple_of((1 - even) * after, LANES))
-    for lane in range(count // LANES):
-        held = slice(lane * LANES, (lane + 1) * LANES)
-        for source, start in ((near_edge, starts[0]), (far_edge, starts[1]), (wave, edge)):
-            for x in range(0, source.shape[1], LANES):
-                block = source[held, x : x + LANES].astype(jnp.float32)
-                padded[lane, pl.ds(start + x, LANES), :] = block.T
-
-        @pl.loop(0, width // LANES)
-        def _(block):
-            base = pl.multiple_of(block * LANES, LANES)
-            total = None
-            for j in range(taps.shape[0]):
-                weight = jnp.broadcast_to(taps[j : j + 1, held], (LANES, LANES))
-                term = weight * padded[lane, pl.ds(base + edge - reach + j, LANES), :]
-                total = term if total is None else total + term
-            out[held, pl.ds(base, LANES)] = total.T.astype(out.dtype)
-
-
-def redatum(blocks, near_edge, wave, far_edge, taps, *after):
-    count, width = wave.shape
+    held = slice(lane * LANES, (lane + 1) * LANES)
+    for source, start in ((near_edge, starts[0]), (far_edge, starts[1]), (wave, edge)):
+        for x in range(0, source.shape[1], LANES):
+            block = source[held, x : x + LANES].astype(jnp.float32)
+            padded[pl.ds(start + x, LANES), :] = block.T
+
+    @pl.loop(0, width // LANES)
+    def _(block):
+        base = pl.multiple_of(block * LANES, LANES)
+        total = None
+        for j in range(taps.shape[0]):
+            weight = jnp.broadcast_to(taps[j : j + 1, held], (LANES, LANES))
+            term = weight * padded[pl.ds(base + edge - reach + j, LANES), :]
+            total = term if total is None else total + term
+        out[:, pl.ds(base, LANES)] = total.T.astype(out.dtype)
+
+
+def redatum(blocks, part, near_edge, wave, far_edge, taps, *after):
+    width = wave.shape[1]
     reach = (taps.shape[0] - 1) // 2
     long = width + 2 * near_edge.shape[1]
     return pl.pallas_call(
-        functools.partial(redatum_kernel, reach, blocks),
-        out_shape=jax.ShapeDtypeStruct((count, width), jnp.bfloat16),
+        functools.partial(redatum_kernel, reach, blocks, part),
+        out_shape=jax.ShapeDtypeStruct((LANES, width), jnp.bfloat16),
         in_specs=[VMEM] * 4 + [ANY] * len(after),
         out_specs=VMEM,
-        scratch_shapes=[pltpu.VMEM((count // LANES, long, LANES), jnp.float32)],
+        scratch_shapes=[pltpu.VMEM((long, LANES), jnp.float32)],
         compiler_params=params(6),
-        cost_estimate=cost(24 * 2 * width * width * 60, count * width * 4),
-        name="redatum",
+        cost_estimate=cost(24 * 2 * width * width * 30, LANES * width * 4),
     )(near_edge, wave, far_edge, taps, *after)
 
 
-def mix_kernel(held, mine, theirs, near, far, *refs):
+def mix_kernel(mine, theirs, near, far, *refs):
     out = refs[-1]
     width = near.shape[1]
     scale = SCALE / math.sqrt(width)
     step = min(width, 256)
     for c in range(0, width, step):
         columns = slice(c, c + step)
-        total = jnp.dot(mine[held, :], near[:, columns], preferred_element_type=jnp.float32)
-        total += jnp.dot(theirs[held, :], far[:, columns], preferred_element_type=jnp.float32)
+        total = jnp.dot(mine[...], near[:, columns], preferred_element_type=jnp.float32)
+        total += jnp.dot(theirs[...], far[:, columns], preferred_element_type=jnp.float32)
         out[:, columns] = (total * scale).astype(out.dtype)
 
 
-def mix(part, mine, theirs, near, far, *after):
+def mix(mine, theirs, near, far, *after):
     count, width = mine.shape
-    held = slice(part * LANES, (part + 1) * LANES) if count > LANES else slice(0, LANES)
-    return pl.pallas_call(
-        functools.partial(mix_kernel, held),
-        out_shape=jax.ShapeDtypeStruct((LANES, width), jnp.bfloat16),
+    return pl.pallas_call(
+        mix_kernel,
+        out_shape=jax.ShapeDtypeStruct((count, width), jnp.bfloat16),
         in_specs=[VMEM] * 4 + [ANY] * len(after),
         out_specs=VMEM,
         compiler_params=params(7),
@@ -308,32 +305,37 @@
     near_edge, far_edge, held_mask = lax.optimization_barrier((near_edge, far_edge, mask))
     masks = partner(held_mask, "space", LEVELS - 1 + block_bits)
     (near,) = tables(0, (0,), coords, near_edge)
-    state = redatum(blocks, near_edge, wavefield, far_edge, taps, near)
-    received = partner(state, "space", block_bits)
-    (far,) = tables(0, (1,), coords, state)
-    states = [state for _ in parts]
-    theirs = [received for _ in parts]
-    table, ahead = (near, far), far
     both, sums = (mask, masks), ()
     end = len(parts) - 1
-    for part in parts:
-        states[part] = mix(part, states[part], theirs[part], *table, ahead)
-        ahead = states[part]
-        theirs[part] = partner(states[part], "space", 1 + block_bits)
-    second = tables(1, (0, 1), coords, ahead)
-    (near,) = tables(2, (0,), coords, second[0])
+    states, theirs, far = [], [], None
     ahead = near
     for part in parts:
-        states[part] = mix(part, states[part], theirs[part], *second, ahead)
+        state = redatum(blocks, part, near_edge, wavefield, far_edge, taps, ahead)
+        received = partner(state, "space", block_bits)
+        ahead = state
+        if part == 0:
+            (far,) = tables(0, (1,), coords, ahead)
+            ahead = far
+        states.append(mix(state, received, near, far, ahead))
         ahead = states[part]
-        theirs[part] = partner(states[part], "space", 2 + block_bits)
+        theirs.append(partner(ahead, "space", 1 + block_bits))
+    second = tables(1, (0, 1), coords, ahead)
+    ahead = second[0]
+    third = []
+    for part in parts:
+        states[part] = mix(states[part], theirs[part], *second, ahead)
+        ahead = states[part]
+        theirs[part] = partner(ahead, "space", 2 + block_bits)
         if part == 0:
-            (far,) = tables(2, (1,), coords, ahead)
-            ahead = far
+            third += tables(2, (0,), coords, ahead)
+            ahead = third[-1]
+        if part == end:
+            third += tables(2, (1,), coords, ahead)
+            ahead = third[-1]
     later = tables(3, (0, 1), coords, ahead)
     ahead = later[0]
     for part in parts:
-        states[part] = mix(part, states[part], theirs[part], near, far, ahead)
+        states[part] = mix(states[part], theirs[part], *third, ahead)
         final = (states[part], coords, later, both)
         if part < end:
             sums = last(part, (0, 1), *final, sums)

time: 62.4 us -> 62.2 us (level)
  starting transfers between devices: 15.6 us -> 14.1 us
  waiting for transfers between devices: 12.2 us -> 13.4 us
    ppermute x8 -> x9, starting transfers between devices: 14.9 us -> 13.4 us  [partner(): lax.ppermute(shard, axis, [(i, i ^ 1 << bit) for i in range(lax.axis_size...]
    ppermute x8 -> x9, waiting for transfers between devices: 12.2 us -> 13.4 us  [partner(): lax.ppermute(shard, axis, [(i, i ^ 1 << bit) for i in range(lax.axis_size...]
    pallas_call x7 -> x8, Pallas kernels: 10.3 us -> 10.4 us  [the longest x2 5.97 us: redatum(): pl.pallas_call(functools.partial(redatum_kernel, reach, blocks, part), ou...]
  transfers between devices with their start and end apart: 9 -> 10, of which waited for: 3 -> 3; matrix products, arithmetic and copies ran while one was open for 0% -> 0% of each run, Pallas kernels for 36% -> 35%
where the time goes in v3:
time: 62.2 us; the launch traced here: 62 us
  Pallas kernels  31.9 us (51%)
  starting transfers between devices  14.1 us (23%)
  waiting for transfers between devices  13.4 us (22%)
  other arithmetic  1.48 us (2%)
  local copies, waits for them, and re-layouts  0.92 us (1%)
    pallas_call x6, Pallas kernels, tables(): pl.pallas_call(functools.partial(tables_kernel, jobs, step), out_shape=(s...  17.3 us
    ppermute x9, starting transfers between devices, partner(): lax.ppermute(shard, axis, [(i, i ^ 1 << bit) for i in range(lax.axis_size...  13.4 us
    ppermute x9, waiting for transfers between devices, partner(): lax.ppermute(shard, axis, [(i, i ^ 1 << bit) for i in range(lax.axis_size...  13.4 us
    pallas_call x2, Pallas kernels, redatum(): pl.pallas_call(functools.partial(redatum_kernel, reach, blocks, part), ou...  5.97 us
    pallas_call x6, Pallas kernels, mix(): pl.pallas_call(mix_kernel, out_shape=jax.ShapeDtypeStruct((count, width),...  4.43 us
    pallas_call x1, Pallas kernels, prepare(): pl.pallas_call(functools.partial(prepare_kernel, blocks, count, width), o...  2.41 us
    pallas_call x3, Pallas kernels, last(): pl.pallas_call(functools.partial(last_kernel, part, weights, len(sums)),...  1.74 us
  transfers between devices with their start and end apart: 10, of which 3 were waited for; matrix products, arithmetic and copies ran while one was open for 0% of the time, Pallas kernels for 35%

profile of v3, /device:TPU:0, one launch (start us, length us, event | category | flops | bytes accessed | tf_op | source)
XLA Modules:
  0.0 62.0 jit_solution(9929880257488948762)
XLA Ops:
  0.0 0.9 %broadcast_select_fusion = (bf16[256,128]{1,0:T(8,128)(2,1)S(1)}, bf16[256,128]{1,0:T(8,128)(2,1)S(1)}) fusion(pred[]{:T(512)S(6)} %eq.6, bf16[256,1024]{1,0:T(8,128)(2,1)} %wave.3), kind=kLoop, calls=%fused_computation | loop fusion | flops 65536 | bytes 262145 | tf_op jit(solution)/shard_map/jit(_where)/select_n | solution.py:296
  0.9 0.6 collective-permute-start
  1.4 0.7 %collective-permute-start.1 = (bf16[256,128]{1,0:T(8,128)(2,1)S(1)}, bf16[256,128]{1,0:T(8,128)(2,1)S(1)}, u32[]{:S(2)}, u32[]{:S(2)}) collective-permute-start(bf16[256,128]{1,0:T(8,128)(2,1)S(1)} %get-tuple-element.27), channel_id=1, source_target_pairs={{1,2},{2,1},{3,4},{4,3},{5,6},{6,5},{7,8},{8,7},{9,10},{10,9},{11,... | collective-permute-start | bytes 196616 | tf_op jit(solution)/shard_map/ppermute | solution.py:38
  2.1 2.4 %prepare.1 = (bf16[256,1024]{1,0:T(8,128)(2,1)}, f32[32,1024]{1,0:T(8,128)}) custom-call(s32[256,1024]{1,0:T(8,128)} %aperture.1, s32[5,16384]{1,0:T(8,128)} %cell_x.1, s32[128,128]{1,0:T(8,128)} %bitcast.5, f32[128,128]{1,0:T(8,128)} %bitcast.6, f32[4]{0:T(128)} %slowness.1), custom_call_target="tpu_custom_call" | custom-call | flops 754974720 | bytes 2097152 | tf_op jit(solution)/shard_map/prepare/pallas_call | solution.py:118
  4.6 0.9 %copy-done.1 = f32[32,1024]{1,0:T(8,128)S(1)} copy-done((f32[32,1024]{1,0:T(8,128)S(1)}, f32[32,1024]{1,0:T(8,128)}, u32[]{:S(2)}) %copy-start.1) | copy-done | bytes 131096
  5.5 2.2 %shard_map.73.refs_0_.near = bf16[1024,1024]{1,0:T(8,128)(2,1)S(1)} custom-call(f32[32,1024]{1,0:T(8,128)S(1)} %copy-done.1, bf16[256,128]{1,0:T(8,128)(2,1)S(1)} %collective-permute-done.refs_0_.near_edge), custom_call_target="tpu_custom_call" | custom-call | flops 1006632960 | bytes 2097152 | tf_op jit(solution)/shard_map/pallas_call | solution.py:175
  7.7 3.0 %shard_map.74.refs_0_.mine = bf16[128,1024]{1,0:T(8,128)(2,1)S(1)} custom-call(bf16[256,128]{1,0:T(8,128)(2,1)S(1)} %collective-permute-done.refs_0_.near_edge, bf16[256,1024]{1,0:T(8,128)(2,1)S(1)} %copy-done.3, bf16[256,128]{1,0:T(8,128)(2,1)S(1)} %collective-permute-done.1.far_edge, f32[65,256]{1,0:T(8,128)S(1)} %bitcast.3, ...), custom_call_target="tpu_custom_call" | custom-call | flops 1509949440 | bytes 524288 | tf_op jit(solution)/shard_map/pallas_call | solution.py:214
  10.7 3.9 %collective-permute-start.2 = (bf16[128,1024]{1,0:T(8,128)(2,1)S(1)}, bf16[128,1024]{1,0:T(8,128)(2,1)S(1)}, u32[]{:S(2)}, u32[]{:S(2)}) collective-permute-start(bf16[128,1024]{1,0:T(8,128)(2,1)S(1)} %shard_map.74.refs_0_.mine), channel_id=1, source_target_pairs={{0,1},{1,0},{2,3},{3,2},{4,5},{5,4},{6,7},{7,6},{8,9},{9,8},{10,11... | collective-permute-start | bytes 786440 | tf_op jit(solution)/shard_map/ppermute | solution.py:42
  14.6 2.2 %shard_map.75.far.refs_0_ = bf16[1024,1024]{1,0:T(8,128)(2,1)S(1)} custom-call(f32[32,1024]{1,0:T(8,128)S(1)} %copy-done.2, bf16[128,1024]{1,0:T(8,128)(2,1)S(1)} %shard_map.74.refs_0_.mine), custom_call_target="tpu_custom_call" | custom-call | flops 1006632960 | bytes 2097152 | tf_op jit(solution)/shard_map/pallas_call | solution.py:175
  16.8 0.7 %mix.6.refs_0_.mine = bf16[128,1024]{1,0:T(8,128)(2,1)S(1)} custom-call(bf16[128,1024]{1,0:T(8,128)(2,1)S(1)} %shard_map.74.refs_0_.mine, bf16[128,1024]{1,0:T(8,128)(2,1)S(1)} %collective-permute-done.2.theirs, bf16[1024,1024]{1,0:T(8,128)(2,1)S(1)} %shard_map.73.refs_0_.near, bf16[1024,1024]{1,0:T(8,128)(2,1)S(1)} %shard_map.75.far.refs_0_, ...), custom_call_target="tpu_custom_call" | custom-call | flops 377487360 | bytes 4194304 | tf_op jit(solution)/shard_map/mix/pallas_call | solution.py:239
  17.5 3.0 %shard_map.76.mine.refs_0_ = bf16[128,1024]{1,0:T(8,128)(2,1)S(1)} custom-call(bf16[256,128]{1,0:T(8,128)(2,1)S(1)} %collective-permute-done.refs_0_.near_edge, bf16[256,1024]{1,0:T(8,128)(2,1)S(1)} %copy-done.3, bf16[256,128]{1,0:T(8,128)(2,1)S(1)} %collective-permute-done.1.far_edge, f32[65,256]{1,0:T(8,128)S(1)} %bitcast.4, ...), custom_call_target="tpu_custom_call" | custom-call | flops 1509949440 | bytes 524288 | tf_op jit(solution)/shard_map/pallas_call | solution.py:214
  20.6 2.5 %collective-permute-start.5 = (bf16[128,1024]{1,0:T(8,128)(2,1)S(1)}, bf16[128,1024]{1,0:T(8,128)(2,1)S(1)}, u32[]{:S(2)}, u32[]{:S(2)}) collective-permute-start(bf16[128,1024]{1,0:T(8,128)(2,1)S(1)} %mix.6.refs_0_.mine), channel_id=1, source_target_pairs={{0,2},{1,3},{2,0},{3,1},{4,6},{5,7},{6,4},{7,5},{8,10},{9,11},{10,... | collective-permute-start | bytes 786440 | tf_op jit(solution)/shard_map/ppermute | solution.py:42
  23.2 2.6 %collective-permute-start.8 = (bf16[256,1024]{1,0:T(8,128)(2,1)S(1)}, bf16[256,1024]{1,0:T(8,128)(2,1)S(1)}, u32[]{:S(2)}, u32[]{:S(2)}) collective-permute-start(bf16[256,1024]{1,0:T(8,128)(2,1)S(1)} %copy-done), channel_id=1, source_target_pairs={{0,8},{1,9},{2,10},{3,11},{4,12},{5,13},{6,14},{7,15},{8,0},{9,1},... | collective-permute-start | bytes 1572872 | tf_op jit(solution)/shard_map/ppermute | solution.py:42
  25.8 0.7 %mix.7.refs_0_.mine = bf16[128,1024]{1,0:T(8,128)(2,1)S(1)} custom-call(bf16[128,1024]{1,0:T(8,128)(2,1)S(1)} %shard_map.76.mine.refs_0_, bf16[128,1024]{1,0:T(8,128)(2,1)S(1)} %collective-permute-done.3.theirs, bf16[1024,1024]{1,0:T(8,128)(2,1)S(1)} %shard_map.73.refs_0_.near, bf16[1024,1024]{1,0:T(8,128)(2,1)S(1)} %shard_map.75.far.refs_0_, ...), custom_call_target="tpu_custom_call" | custom-call | flops 377487360 | bytes 4194304 | tf_op jit(solution)/shard_map/mix/pallas_call | solution.py:239
  26.5 0.6 %collective-permute-start.4 = (bf16[128,1024]{1,0:T(8,128)(2,1)S(1)}, bf16[128,1024]{1,0:T(8,128)(2,1)S(1)}, u32[]{:S(2)}, u32[]{:S(2)}) collective-permute-start(bf16[128,1024]{1,0:T(8,128)(2,1)S(1)} %mix.7.refs_0_.mine), channel_id=1, source_target_pairs={{0,2},{1,3},{2,0},{3,1},{4,6},{5,7},{6,4},{7,5},{8,10},{9,11},{10,... | collective-permute-start | bytes 786440 | tf_op jit(solution)/shard_map/ppermute | solution.py:42
  27.1 4.3 %shard_map.77 = (bf16[1024,1024]{1,0:T(8,128)(2,1)S(1)}, bf16[1024,1024]{1,0:T(8,128)(2,1)S(1)}) custom-call(f32[32,1024]{1,0:T(8,128)S(1)} %copy-done.2, bf16[128,1024]{1,0:T(8,128)(2,1)S(1)} %mix.7.refs_0_.mine), custom_call_target="tpu_custom_call" | custom-call | flops 2013265920 | bytes 4194304 | tf_op jit(solution)/shard_map/pallas_call | solution.py:175
  31.5 0.7 %mix.8.refs_0_.mine = bf16[128,1024]{1,0:T(8,128)(2,1)S(1)} custom-call(bf16[128,1024]{1,0:T(8,128)(2,1)S(1)} %mix.6.refs_0_.mine, bf16[128,1024]{1,0:T(8,128)(2,1)S(1)} %collective-permute-done.5.theirs, bf16[1024,1024]{1,0:T(8,128)(2,1)S(1)} %get-tuple-element.20.near.refs_0_, bf16[1024,1024]{1,0:T(8,128)(2,1)S(1)} %get-tuple-element.21.far, ...), custom_call_target="tpu_custom_call" | custom-call | flops 377487360 | bytes 4194304 | tf_op jit(solution)/shard_map/mix/pallas_call | solution.py:239
  32.2 1.6 %collective-permute-start.7 = (bf16[128,1024]{1,0:T(8,128)(2,1)S(1)}, bf16[128,1024]{1,0:T(8,128)(2,1)S(1)}, u32[]{:S(2)}, u32[]{:S(2)}) collective-permute-start(bf16[128,1024]{1,0:T(8,128)(2,1)S(1)} %mix.8.refs_0_.mine), channel_id=1, source_target_pairs={{0,4},{1,5},{2,6},{3,7},{4,0},{5,1},{6,2},{7,3},{8,12},{9,13},{10,... | collective-permute-start | bytes 786440 | tf_op jit(solution)/shard_map/ppermute | solution.py:42
  33.9 2.2 %shard_map.78.refs_0_.near = bf16[1024,1024]{1,0:T(8,128)(2,1)S(1)} custom-call(f32[32,1024]{1,0:T(8,128)S(1)} %copy-done.2, bf16[128,1024]{1,0:T(8,128)(2,1)S(1)} %mix.8.refs_0_.mine), custom_call_target="tpu_custom_call" | custom-call | flops 1006632960 | bytes 2097152 | tf_op jit(solution)/shard_map/pallas_call | solution.py:175
  36.1 0.7 %mix.9.refs_0_.mine = bf16[128,1024]{1,0:T(8,128)(2,1)S(1)} custom-call(bf16[128,1024]{1,0:T(8,128)(2,1)S(1)} %mix.7.refs_0_.mine, bf16[128,1024]{1,0:T(8,128)(2,1)S(1)} %collective-permute-done.4.theirs, bf16[1024,1024]{1,0:T(8,128)(2,1)S(1)} %get-tuple-element.20.near.refs_0_, bf16[1024,1024]{1,0:T(8,128)(2,1)S(1)} %get-tuple-element.21.far, ...), custom_call_target="tpu_custom_call" | custom-call | flops 377487360 | bytes 4194304 | tf_op jit(solution)/shard_map/mix/pallas_call | solution.py:239
  36.8 1.3 %collective-permute-start.6 = (bf16[128,1024]{1,0:T(8,128)(2,1)S(1)}, bf16[128,1024]{1,0:T(8,128)(2,1)S(1)}, u32[]{:S(2)}, u32[]{:S(2)}) collective-permute-start(bf16[128,1024]{1,0:T(8,128)(2,1)S(1)} %mix.9.refs_0_.mine), channel_id=1, source_target_pairs={{0,4},{1,5},{2,6},{3,7},{4,0},{5,1},{6,2},{7,3},{8,12},{9,13},{10,... | collective-permute-start | bytes 786440 | tf_op jit(solution)/shard_map/ppermute | solution.py:42
  38.1 2.2 %shard_map.79.refs_0_.far = bf16[1024,1024]{1,0:T(8,128)(2,1)S(1)} custom-call(f32[32,1024]{1,0:T(8,128)S(1)} %copy-done.2, bf16[128,1024]{1,0:T(8,128)(2,1)S(1)} %mix.9.refs_0_.mine), custom_call_target="tpu_custom_call" | custom-call | flops 1006632960 | bytes 2097152 | tf_op jit(solution)/shard_map/pallas_call | solution.py:175
  40.3 4.3 %shard_map.80 = (bf16[1024,1024]{1,0:T(8,128)(2,1)S(1)}, bf16[1024,1024]{1,0:T(8,128)(2,1)S(1)}) custom-call(f32[32,1024]{1,0:T(8,128)S(1)} %copy-done.2, bf16[1024,1024]{1,0:T(8,128)(2,1)S(1)} %shard_map.79.refs_0_.far), custom_call_target="tpu_custom_call" | custom-call | flops 2013265920 | bytes 4194304 | tf_op jit(solution)/shard_map/pallas_call | solution.py:175
  44.6 6.6 %collective-permute-done.7.theirs = bf16[128,1024]{1,0:T(8,128)(2,1)S(1)} collective-permute-done((bf16[128,1024]{1,0:T(8,128)(2,1)S(1)}, bf16[128,1024]{1,0:T(8,128)(2,1)S(1)}, u32[]{:S(2)}, u32[]{:S(2)}) %collective-permute-start.7) | collective-permute-done | bytes 262176 | tf_op jit(solution)/shard_map/ppermute | solution.py:42
  51.2 0.7 %mix.10.state = bf16[128,1024]{1,0:T(8,128)(2,1)S(1)} custom-call(bf16[128,1024]{1,0:T(8,128)(2,1)S(1)} %mix.8.refs_0_.mine, bf16[128,1024]{1,0:T(8,128)(2,1)S(1)} %collective-permute-done.7.theirs, bf16[1024,1024]{1,0:T(8,128)(2,1)S(1)} %shard_map.78.refs_0_.near, bf16[1024,1024]{1,0:T(8,128)(2,1)S(1)} %shard_map.79.refs_0_.far, ...), custom_call_target="tpu_custom_call" | custom-call | flops 377487360 | bytes 4194304 | tf_op jit(solution)/shard_map/mix/pallas_call | solution.py:239
  52.0 0.8 %shard_map.81 = (f32[1,1024]{1,0:T(1,128)S(1)}, f32[1,1024]{1,0:T(1,128)S(1)}) custom-call(bf16[128,1024]{1,0:T(8,128)(2,1)S(1)} %mix.10.state, f32[32,1024]{1,0:T(8,128)S(1)} %copy-done.2, bf16[1024,1024]{1,0:T(8,128)(2,1)S(1)} %get-tuple-element.22.refs_0_, bf16[1024,1024]{1,0:T(8,128)(2,1)S(1)} %get-tuple-element.23.refs_1_.refs_0_, ...), custom_call_target="tpu_custom_call" | custom-call | flops 402653184 | bytes 4194304 | tf_op jit(solution)/shard_map/pallas_call | solution.py:276
  52.8 2.9 %collective-permute-done.6.theirs = bf16[128,1024]{1,0:T(8,128)(2,1)S(1)} collective-permute-done((bf16[128,1024]{1,0:T(8,128)(2,1)S(1)}, bf16[128,1024]{1,0:T(8,128)(2,1)S(1)}, u32[]{:S(2)}, u32[]{:S(2)}) %collective-permute-start.6) | collective-permute-done | bytes 262176 | tf_op jit(solution)/shard_map/ppermute | solution.py:42
  55.6 0.7 %mix.11.state = bf16[128,1024]{1,0:T(8,128)(2,1)S(1)} custom-call(bf16[128,1024]{1,0:T(8,128)(2,1)S(1)} %mix.9.refs_0_.mine, bf16[128,1024]{1,0:T(8,128)(2,1)S(1)} %collective-permute-done.6.theirs, bf16[1024,1024]{1,0:T(8,128)(2,1)S(1)} %shard_map.78.refs_0_.near, bf16[1024,1024]{1,0:T(8,128)(2,1)S(1)} %shard_map.79.refs_0_.far, ...), custom_call_target="tpu_custom_call" | custom-call | flops 377487360 | bytes 4194304 | tf_op jit(solution)/shard_map/mix/pallas_call | solution.py:239
  56.4 0.5 shard_map.82.refs_3_
  57.0 0.5 shard_map.83
  57.5 3.9 %collective-permute-done.9 = f32[1,1024]{1,0:T(1,128)S(1)} collective-permute-done((f32[1,1024]{1,0:T(1,128)S(1)}, f32[1,1024]{1,0:T(1,128)S(1)}, u32[]{:S(2)}, u32[]{:S(2)}) %collective-permute-start.9) | collective-permute-done | bytes 4128 | tf_op jit(solution)/shard_map/ppermute | solution.py:42
  61.4 0.6 add.11
  (18 shorter events, 0.3 us)
Async XLA Ops:
  0.9 3.7 %collective-permute-start = (bf16[256,128]{1,0:T(8,128)(2,1)S(1)}, bf16[256,128]{1,0:T(8,128)(2,1)S(1)}, u32[]{:S(2)}, u32[]{:S(2)}) collective-permute-start(bf16[256,128]{1,0:T(8,128)(2,1)S(1)} %get-tuple-element.28), channel_id=1, source_target_pairs={{0,1},{1,0},{2,3},{3,2},{4,5},{5,4},{6,7},{7,6},{8,9},{9,8},{10,11... | collective-permute-start | bytes 196616 | tf_op jit(solution)/shard_map/ppermute | solution.py:42
  1.4 3.1 %collective-permute-start.1 = (bf16[256,128]{1,0:T(8,128)(2,1)S(1)}, bf16[256,128]{1,0:T(8,128)(2,1)S(1)}, u32[]{:S(2)}, u32[]{:S(2)}) collective-permute-start(bf16[256,128]{1,0:T(8,128)(2,1)S(1)} %get-tuple-element.27), channel_id=1, source_target_pairs={{1,2},{2,1},{3,4},{4,3},{5,6},{6,5},{7,8},{8,7},{9,10},{10,9},{11,... | collective-permute-start | bytes 196616 | tf_op jit(solution)/shard_map/ppermute | solution.py:38
  2.1 5.5 %copy-start.3 = (bf16[256,1024]{1,0:T(8,128)(2,1)S(1)}, bf16[256,1024]{1,0:T(8,128)(2,1)}, u32[]{:S(2)}) copy-start(bf16[256,1024]{1,0:T(8,128)(2,1)} %wave.3) | copy-start | bytes 1572868
  2.1 5.5 %copy-start.4 = (f32[256,65]{0,1:T(8,128)S(1)}, f32[256,65]{0,1:T(8,128)}, u32[]{:S(2)}) copy-start(f32[256,65]{0,1:T(8,128)} %param.8) | copy-start | bytes 199684
  4.6 0.9 %copy-start.1 = (f32[32,1024]{1,0:T(8,128)S(1)}, f32[32,1024]{1,0:T(8,128)}, u32[]{:S(2)}) copy-start(f32[32,1024]{1,0:T(8,128)} %get-tuple-element.19.coords) | copy-start | bytes 393220
  7.7 6.9 %copy-start.2 = (f32[32,1024]{1,0:T(8,128)S(1)}, f32[32,1024]{1,0:T(8,128)}, u32[]{:S(2)}) copy-start(f32[32,1024]{1,0:T(8,128)} %get-tuple-element.19.coords) | copy-start | bytes 393220
  10.7 6.1 %collective-permute-start.2 = (bf16[128,1024]{1,0:T(8,128)(2,1)S(1)}, bf16[128,1024]{1,0:T(8,128)(2,1)S(1)}, u32[]{:S(2)}, u32[]{:S(2)}) collective-permute-start(bf16[128,1024]{1,0:T(8,128)(2,1)S(1)} %shard_map.74.refs_0_.mine), channel_id=1, source_target_pairs={{0,1},{1,0},{2,3},{3,2},{4,5},{5,4},{6,7},{7,6},{8,9},{9,8},{10,11... | collective-permute-start | bytes 786440 | tf_op jit(solution)/shard_map/ppermute | solution.py:42
  17.5 5.6 %copy-start = (bf16[256,1024]{1,0:T(8,128)(2,1)S(1)}, bf16[256,1024]{1,0:T(8,128)(2,1)}, u32[]{:S(2)}) copy-start(bf16[256,1024]{1,0:T(8,128)(2,1)} %get-tuple-element.24.refs_2_.refs_1_) | copy-start | bytes 1572868
  20.5 5.2 %collective-permute-start.3 = (bf16[128,1024]{1,0:T(8,128)(2,1)S(1)}, bf16[128,1024]{1,0:T(8,128)(2,1)S(1)}, u32[]{:S(2)}, u32[]{:S(2)}) collective-permute-start(bf16[128,1024]{1,0:T(8,128)(2,1)S(1)} %shard_map.76.mine.refs_0_), channel_id=1, source_target_pairs={{0,1},{1,0},{2,3},{3,2},{4,5},{5,4},{6,7},{7,6},{8,9},{9,8},{10,11... | collective-permute-start | bytes 786440 | tf_op jit(solution)/shard_map/ppermute | solution.py:42
  20.6 10.9 %collective-permute-start.5 = (bf16[128,1024]{1,0:T(8,128)(2,1)S(1)}, bf16[128,1024]{1,0:T(8,128)(2,1)S(1)}, u32[]{:S(2)}, u32[]{:S(2)}) collective-permute-start(bf16[128,1024]{1,0:T(8,128)(2,1)S(1)} %mix.6.refs_0_.mine), channel_id=1, source_target_pairs={{0,2},{1,3},{2,0},{3,1},{4,6},{5,7},{6,4},{7,5},{8,10},{9,11},{10,... | collective-permute-start | bytes 786440 | tf_op jit(solution)/shard_map/ppermute | solution.py:42
  23.2 28.8 %collective-permute-start.8 = (bf16[256,1024]{1,0:T(8,128)(2,1)S(1)}, bf16[256,1024]{1,0:T(8,128)(2,1)S(1)}, u32[]{:S(2)}, u32[]{:S(2)}) collective-permute-start(bf16[256,1024]{1,0:T(8,128)(2,1)S(1)} %copy-done), channel_id=1, source_target_pairs={{0,8},{1,9},{2,10},{3,11},{4,12},{5,13},{6,14},{7,15},{8,0},{9,1},... | collective-permute-start | bytes 1572872 | tf_op jit(solution)/shard_map/ppermute | solution.py:42
  26.5 9.6 %collective-permute-start.4 = (bf16[128,1024]{1,0:T(8,128)(2,1)S(1)}, bf16[128,1024]{1,0:T(8,128)(2,1)S(1)}, u32[]{:S(2)}, u32[]{:S(2)}) collective-permute-start(bf16[128,1024]{1,0:T(8,128)(2,1)S(1)} %mix.7.refs_0_.mine), channel_id=1, source_target_pairs={{0,2},{1,3},{2,0},{3,1},{4,6},{5,7},{6,4},{7,5},{8,10},{9,11},{10,... | collective-permute-start | bytes 786440 | tf_op jit(solution)/shard_map/ppermute | solution.py:42
  32.2 19.0 %collective-permute-start.7 = (bf16[128,1024]{1,0:T(8,128)(2,1)S(1)}, bf16[128,1024]{1,0:T(8,128)(2,1)S(1)}, u32[]{:S(2)}, u32[]{:S(2)}) collective-permute-start(bf16[128,1024]{1,0:T(8,128)(2,1)S(1)} %mix.8.refs_0_.mine), channel_id=1, source_target_pairs={{0,4},{1,5},{2,6},{3,7},{4,0},{5,1},{6,2},{7,3},{8,12},{9,13},{10,... | collective-permute-start | bytes 786440 | tf_op jit(solution)/shard_map/ppermute | solution.py:42
  36.8 18.8 %collective-permute-start.6 = (bf16[128,1024]{1,0:T(8,128)(2,1)S(1)}, bf16[128,1024]{1,0:T(8,128)(2,1)S(1)}, u32[]{:S(2)}, u32[]{:S(2)}) collective-permute-start(bf16[128,1024]{1,0:T(8,128)(2,1)S(1)} %mix.9.refs_0_.mine), channel_id=1, source_target_pairs={{0,4},{1,5},{2,6},{3,7},{4,0},{5,1},{6,2},{7,3},{8,12},{9,13},{10,... | collective-permute-start | bytes 786440 | tf_op jit(solution)/shard_map/ppermute | solution.py:42
  56.8 4.6 %collective-permute-start.9 = (f32[1,1024]{1,0:T(1,128)S(1)}, f32[1,1024]{1,0:T(1,128)S(1)}, u32[]{:S(2)}, u32[]{:S(2)}) collective-permute-start(f32[1,1024]{1,0:T(1,128)S(1)} %shard_map.82.refs_3_), channel_id=1, source_target_pairs={{0,8},{1,9},{2,10},{3,11},{4,12},{5,13},{6,14},{7,15},{8,0},{9,1},... | collective-permute-start | bytes 12296 | tf_op jit(solution)/shard_map/ppermute | solution.py:42

commit v4 on v3

--- a/solution.py
+++ b/solution.py
@@ -307,7 +307,7 @@
     (near,) = tables(0, (0,), coords, near_edge)
     both, sums = (mask, masks), ()
     end = len(parts) - 1
-    states, theirs, far = [], [], None
+    states, theirs, second, far = [], [], [], None
     ahead = near
     for part in parts:
         state = redatum(blocks, part, near_edge, wavefield, far_edge, taps, ahead)
@@ -316,11 +316,14 @@
         if part == 0:
             (far,) = tables(0, (1,), coords, ahead)
             ahead = far
+        if part == end:
+            second += tables(1, (0,), coords, ahead)
+            ahead = second[0]
         states.append(mix(state, received, near, far, ahead))
         ahead = states[part]
         theirs.append(partner(ahead, "space", 1 + block_bits))
-    second = tables(1, (0, 1), coords, ahead)
-    ahead = second[0]
+    second += tables(1, (1,), coords, ahead)
+    ahead = second[-1]
     third = []
     for part in parts:
         states[part] = mix(states[part], theirs[part], *second, ahead)

time: 62.2 us -> 62.4 us (level)
  starting transfers between devices: 14.1 us -> 14.9 us
  waiting for transfers between devices: 13.4 us -> 12.6 us
    ppermute x9, waiting for transfers between devices: 13.4 us -> 12.6 us  [partner(): lax.ppermute(shard, axis, [(i, i ^ 1 << bit) for i in range(lax.axis_size...]
    ppermute x9, starting transfers between devices: 13.4 us -> 14.2 us  [partner(): lax.ppermute(shard, axis, [(i, i ^ 1 << bit) for i in range(lax.axis_size...]
    pallas_call x6 -> x7, Pallas kernels: 17.3 us -> 17.3 us  [tables(): pl.pallas_call(functools.partial(tables_kernel, jobs, step), out_shape=(s...]
  transfers between devices with their start and end apart: 10 -> 10, of which waited for: 3 -> 4; matrix products, arithmetic and copies ran while one was open for 0% -> 0% of each run, Pallas kernels for 35% -> 35%
where the time goes in v4:
time: 62.4 us; the launch traced here: 62.1 us
  Pallas kernels  31.8 us (51%)
  starting transfers between devices  14.9 us (24%)
  waiting for transfers between devices  12.6 us (20%)
  other arithmetic  1.48 us (2%)
  local copies, waits for them, and re-layouts  1.1 us (2%)
    pallas_call x7, Pallas kernels, tables(): pl.pallas_call(functools.partial(tables_kernel, jobs, step), out_shape=(s...  17.3 us
    ppermute x9, starting transfers between devices, partner(): lax.ppermute(shard, axis, [(i, i ^ 1 << bit) for i in range(lax.axis_size...  14.2 us
    ppermute x9, waiting for transfers between devices, partner(): lax.ppermute(shard, axis, [(i, i ^ 1 << bit) for i in range(lax.axis_size...  12.6 us
    pallas_call x2, Pallas kernels, redatum(): pl.pallas_call(functools.partial(redatum_kernel, reach, blocks, part), ou...  5.97 us
    pallas_call x6, Pallas kernels, mix(): pl.pallas_call(mix_kernel, out_shape=jax.ShapeDtypeStruct((count, width),...  4.37 us
    pallas_call x1, Pallas kernels, prepare(): pl.pallas_call(functools.partial(prepare_kernel, blocks, count, width), o...  2.42 us
    pallas_call x3, Pallas kernels, last(): pl.pallas_call(functools.partial(last_kernel, part, weights, len(sums)),...  1.74 us
  transfers between devices with their start and end apart: 10, of which 4 were waited for; matrix products, arithmetic and copies ran while one was open for 0% of the time, Pallas kernels for 35%

profile of v4, /device:TPU:0, one launch (start us, length us, event | category | flops | bytes accessed | tf_op | source)
XLA Modules:
  0.0 62.1 jit_solution(17844127986999274945)
XLA Ops:
  0.0 0.9 %broadcast_select_fusion = (bf16[256,128]{1,0:T(8,128)(2,1)S(1)}, bf16[256,128]{1,0:T(8,128)(2,1)S(1)}) fusion(pred[]{:T(512)S(6)} %eq.6, bf16[256,1024]{1,0:T(8,128)(2,1)} %wave.3), kind=kLoop, calls=%fused_computation | loop fusion | flops 65536 | bytes 262145 | tf_op jit(solution)/shard_map/jit(_where)/select_n | solution.py:296
  0.9 0.6 collective-permute-start
  1.4 0.7 %collective-permute-start.1 = (bf16[256,128]{1,0:T(8,128)(2,1)S(1)}, bf16[256,128]{1,0:T(8,128)(2,1)S(1)}, u32[]{:S(2)}, u32[]{:S(2)}) collective-permute-start(bf16[256,128]{1,0:T(8,128)(2,1)S(1)} %get-tuple-element.23), channel_id=1, source_target_pairs={{1,2},{2,1},{3,4},{4,3},{5,6},{6,5},{7,8},{8,7},{9,10},{10,9},{11,... | collective-permute-start | bytes 196616 | tf_op jit(solution)/shard_map/ppermute | solution.py:38
  2.1 2.4 %prepare.1 = (bf16[256,1024]{1,0:T(8,128)(2,1)}, f32[32,1024]{1,0:T(8,128)}) custom-call(s32[256,1024]{1,0:T(8,128)} %aperture.1, s32[5,16384]{1,0:T(8,128)} %cell_x.1, s32[128,128]{1,0:T(8,128)} %bitcast.5, f32[128,128]{1,0:T(8,128)} %bitcast.6, f32[4]{0:T(128)} %slowness.1), custom_call_target="tpu_custom_call" | custom-call | flops 754974720 | bytes 2097152 | tf_op jit(solution)/shard_map/prepare/pallas_call | solution.py:118
  4.6 0.9 %copy-done.1 = f32[32,1024]{1,0:T(8,128)S(1)} copy-done((f32[32,1024]{1,0:T(8,128)S(1)}, f32[32,1024]{1,0:T(8,128)}, u32[]{:S(2)}) %copy-start.1) | copy-done | bytes 131096
  5.5 2.2 %shard_map.73.refs_0_.near = bf16[1024,1024]{1,0:T(8,128)(2,1)S(1)} custom-call(f32[32,1024]{1,0:T(8,128)S(1)} %copy-done.1, bf16[256,128]{1,0:T(8,128)(2,1)S(1)} %collective-permute-done.refs_0_.near_edge), custom_call_target="tpu_custom_call" | custom-call | flops 1006632960 | bytes 2097152 | tf_op jit(solution)/shard_map/pallas_call | solution.py:175
  7.7 3.0 %shard_map.74.refs_0_.mine = bf16[128,1024]{1,0:T(8,128)(2,1)S(1)} custom-call(bf16[256,128]{1,0:T(8,128)(2,1)S(1)} %collective-permute-done.refs_0_.near_edge, bf16[256,1024]{1,0:T(8,128)(2,1)S(1)} %copy-done.3, bf16[256,128]{1,0:T(8,128)(2,1)S(1)} %collective-permute-done.1.far_edge, f32[65,256]{1,0:T(8,128)S(1)} %bitcast.3, ...), custom_call_target="tpu_custom_call" | custom-call | flops 1509949440 | bytes 524288 | tf_op jit(solution)/shard_map/pallas_call | solution.py:214
  10.7 3.9 %collective-permute-start.2 = (bf16[128,1024]{1,0:T(8,128)(2,1)S(1)}, bf16[128,1024]{1,0:T(8,128)(2,1)S(1)}, u32[]{:S(2)}, u32[]{:S(2)}) collective-permute-start(bf16[128,1024]{1,0:T(8,128)(2,1)S(1)} %shard_map.74.refs_0_.mine), channel_id=1, source_target_pairs={{0,1},{1,0},{2,3},{3,2},{4,5},{5,4},{6,7},{7,6},{8,9},{9,8},{10,11... | collective-permute-start | bytes 786440 | tf_op jit(solution)/shard_map/ppermute | solution.py:42
  14.6 2.2 %shard_map.75.far.refs_0_ = bf16[1024,1024]{1,0:T(8,128)(2,1)S(1)} custom-call(f32[32,1024]{1,0:T(8,128)S(1)} %copy-done.2, bf16[128,1024]{1,0:T(8,128)(2,1)S(1)} %shard_map.74.refs_0_.mine), custom_call_target="tpu_custom_call" | custom-call | flops 1006632960 | bytes 2097152 | tf_op jit(solution)/shard_map/pallas_call | solution.py:175
  16.8 0.7 %mix.6.refs_0_.mine = bf16[128,1024]{1,0:T(8,128)(2,1)S(1)} custom-call(bf16[128,1024]{1,0:T(8,128)(2,1)S(1)} %shard_map.74.refs_0_.mine, bf16[128,1024]{1,0:T(8,128)(2,1)S(1)} %collective-permute-done.2.theirs, bf16[1024,1024]{1,0:T(8,128)(2,1)S(1)} %shard_map.73.refs_0_.near, bf16[1024,1024]{1,0:T(8,128)(2,1)S(1)} %shard_map.75.far.refs_0_, ...), custom_call_target="tpu_custom_call" | custom-call | flops 377487360 | bytes 4194304 | tf_op jit(solution)/shard_map/mix/pallas_call | solution.py:239
  17.5 3.0 %shard_map.76.refs_0_.mine = bf16[128,1024]{1,0:T(8,128)(2,1)S(1)} custom-call(bf16[256,128]{1,0:T(8,128)(2,1)S(1)} %collective-permute-done.refs_0_.near_edge, bf16[256,1024]{1,0:T(8,128)(2,1)S(1)} %copy-done.3, bf16[256,128]{1,0:T(8,128)(2,1)S(1)} %collective-permute-done.1.far_edge, f32[65,256]{1,0:T(8,128)S(1)} %bitcast.4, ...), custom_call_target="tpu_custom_call" | custom-call | flops 1509949440 | bytes 524288 | tf_op jit(solution)/shard_map/pallas_call | solution.py:214
  20.6 2.5 %collective-permute-start.5 = (bf16[128,1024]{1,0:T(8,128)(2,1)S(1)}, bf16[128,1024]{1,0:T(8,128)(2,1)S(1)}, u32[]{:S(2)}, u32[]{:S(2)}) collective-permute-start(bf16[128,1024]{1,0:T(8,128)(2,1)S(1)} %mix.6.refs_0_.mine), channel_id=1, source_target_pairs={{0,2},{1,3},{2,0},{3,1},{4,6},{5,7},{6,4},{7,5},{8,10},{9,11},{10,... | collective-permute-start | bytes 786440 | tf_op jit(solution)/shard_map/ppermute | solution.py:42
  23.1 2.2 %shard_map.77.refs_0_.near = bf16[1024,1024]{1,0:T(8,128)(2,1)S(1)} custom-call(f32[32,1024]{1,0:T(8,128)S(1)} %copy-done.2, bf16[128,1024]{1,0:T(8,128)(2,1)S(1)} %shard_map.76.refs_0_.mine), custom_call_target="tpu_custom_call" | custom-call | flops 1006632960 | bytes 2097152 | tf_op jit(solution)/shard_map/pallas_call | solution.py:175
  25.3 0.7 %mix.7.refs_0_.mine = bf16[128,1024]{1,0:T(8,128)(2,1)S(1)} custom-call(bf16[128,1024]{1,0:T(8,128)(2,1)S(1)} %shard_map.76.refs_0_.mine, bf16[128,1024]{1,0:T(8,128)(2,1)S(1)} %collective-permute-done.3.theirs, bf16[1024,1024]{1,0:T(8,128)(2,1)S(1)} %shard_map.73.refs_0_.near, bf16[1024,1024]{1,0:T(8,128)(2,1)S(1)} %shard_map.75.far.refs_0_, ...), custom_call_target="tpu_custom_call" | custom-call | flops 377487360 | bytes 4194304 | tf_op jit(solution)/shard_map/mix/pallas_call | solution.py:239
  26.4 3.0 %collective-permute-start.8 = (bf16[256,1024]{1,0:T(8,128)(2,1)S(1)}, bf16[256,1024]{1,0:T(8,128)(2,1)S(1)}, u32[]{:S(2)}, u32[]{:S(2)}) collective-permute-start(bf16[256,1024]{1,0:T(8,128)(2,1)S(1)} %copy-done), channel_id=1, source_target_pairs={{0,8},{1,9},{2,10},{3,11},{4,12},{5,13},{6,14},{7,15},{8,0},{9,1},... | collective-permute-start | bytes 1572872 | tf_op jit(solution)/shard_map/ppermute | solution.py:42
  29.3 2.2 %shard_map.78.far.refs_0_ = bf16[1024,1024]{1,0:T(8,128)(2,1)S(1)} custom-call(f32[32,1024]{1,0:T(8,128)S(1)} %copy-done.2, bf16[128,1024]{1,0:T(8,128)(2,1)S(1)} %mix.7.refs_0_.mine), custom_call_target="tpu_custom_call" | custom-call | flops 1006632960 | bytes 2097152 | tf_op jit(solution)/shard_map/pallas_call | solution.py:175
  31.5 0.7 %mix.8.refs_0_.mine = bf16[128,1024]{1,0:T(8,128)(2,1)S(1)} custom-call(bf16[128,1024]{1,0:T(8,128)(2,1)S(1)} %mix.6.refs_0_.mine, bf16[128,1024]{1,0:T(8,128)(2,1)S(1)} %collective-permute-done.5.theirs, bf16[1024,1024]{1,0:T(8,128)(2,1)S(1)} %shard_map.77.refs_0_.near, bf16[1024,1024]{1,0:T(8,128)(2,1)S(1)} %shard_map.78.far.refs_0_, ...), custom_call_target="tpu_custom_call" | custom-call | flops 377487360 | bytes 4194304 | tf_op jit(solution)/shard_map/mix/pallas_call | solution.py:239
  32.2 1.6 %collective-permute-start.7 = (bf16[128,1024]{1,0:T(8,128)(2,1)S(1)}, bf16[128,1024]{1,0:T(8,128)(2,1)S(1)}, u32[]{:S(2)}, u32[]{:S(2)}) collective-permute-start(bf16[128,1024]{1,0:T(8,128)(2,1)S(1)} %mix.8.refs_0_.mine), channel_id=1, source_target_pairs={{0,4},{1,5},{2,6},{3,7},{4,0},{5,1},{6,2},{7,3},{8,12},{9,13},{10,... | collective-permute-start | bytes 786440 | tf_op jit(solution)/shard_map/ppermute | solution.py:42
  33.9 2.2 %shard_map.79.refs_0_.near = bf16[1024,1024]{1,0:T(8,128)(2,1)S(1)} custom-call(f32[32,1024]{1,0:T(8,128)S(1)} %copy-done.2, bf16[128,1024]{1,0:T(8,128)(2,1)S(1)} %mix.8.refs_0_.mine), custom_call_target="tpu_custom_call" | custom-call | flops 1006632960 | bytes 2097152 | tf_op jit(solution)/shard_map/pallas_call | solution.py:175
  36.1 0.7 %mix.9.refs_0_.mine = bf16[128,1024]{1,0:T(8,128)(2,1)S(1)} custom-call(bf16[128,1024]{1,0:T(8,128)(2,1)S(1)} %mix.7.refs_0_.mine, bf16[128,1024]{1,0:T(8,128)(2,1)S(1)} %collective-permute-done.4.theirs, bf16[1024,1024]{1,0:T(8,128)(2,1)S(1)} %shard_map.77.refs_0_.near, bf16[1024,1024]{1,0:T(8,128)(2,1)S(1)} %shard_map.78.far.refs_0_, ...), custom_call_target="tpu_custom_call" | custom-call | flops 377487360 | bytes 4194304 | tf_op jit(solution)/shard_map/mix/pallas_call | solution.py:239
  36.8 1.3 %collective-permute-start.6 = (bf16[128,1024]{1,0:T(8,128)(2,1)S(1)}, bf16[128,1024]{1,0:T(8,128)(2,1)S(1)}, u32[]{:S(2)}, u32[]{:S(2)}) collective-permute-start(bf16[128,1024]{1,0:T(8,128)(2,1)S(1)} %mix.9.refs_0_.mine), channel_id=1, source_target_pairs={{0,4},{1,5},{2,6},{3,7},{4,0},{5,1},{6,2},{7,3},{8,12},{9,13},{10,... | collective-permute-start | bytes 786440 | tf_op jit(solution)/shard_map/ppermute | solution.py:42
  38.1 2.2 %shard_map.80.refs_0_.far = bf16[1024,1024]{1,0:T(8,128)(2,1)S(1)} custom-call(f32[32,1024]{1,0:T(8,128)S(1)} %copy-done.2, bf16[128,1024]{1,0:T(8,128)(2,1)S(1)} %mix.9.refs_0_.mine), custom_call_target="tpu_custom_call" | custom-call | flops 1006632960 | bytes 2097152 | tf_op jit(solution)/shard_map/pallas_call | solution.py:175
  40.3 4.3 %shard_map.81 = (bf16[1024,1024]{1,0:T(8,128)(2,1)S(1)}, bf16[1024,1024]{1,0:T(8,128)(2,1)S(1)}) custom-call(f32[32,1024]{1,0:T(8,128)S(1)} %copy-done.2, bf16[1024,1024]{1,0:T(8,128)(2,1)S(1)} %shard_map.80.refs_0_.far), custom_call_target="tpu_custom_call" | custom-call | flops 2013265920 | bytes 4194304 | tf_op jit(solution)/shard_map/pallas_call | solution.py:175
  44.6 2.7 %collective-permute-done.7.theirs = bf16[128,1024]{1,0:T(8,128)(2,1)S(1)} collective-permute-done((bf16[128,1024]{1,0:T(8,128)(2,1)S(1)}, bf16[128,1024]{1,0:T(8,128)(2,1)S(1)}, u32[]{:S(2)}, u32[]{:S(2)}) %collective-permute-start.7) | collective-permute-done | bytes 262176 | tf_op jit(solution)/shard_map/ppermute | solution.py:42
  47.2 0.7 %mix.10.state = bf16[128,1024]{1,0:T(8,128)(2,1)S(1)} custom-call(bf16[128,1024]{1,0:T(8,128)(2,1)S(1)} %mix.8.refs_0_.mine, bf16[128,1024]{1,0:T(8,128)(2,1)S(1)} %collective-permute-done.7.theirs, bf16[1024,1024]{1,0:T(8,128)(2,1)S(1)} %shard_map.79.refs_0_.near, bf16[1024,1024]{1,0:T(8,128)(2,1)S(1)} %shard_map.80.refs_0_.far, ...), custom_call_target="tpu_custom_call" | custom-call | flops 377487360 | bytes 4194304 | tf_op jit(solution)/shard_map/mix/pallas_call | solution.py:239
  48.0 4.6 %collective-permute-done.8.refs_3_.refs_1_ = bf16[256,1024]{1,0:T(8,128)(2,1)S(1)} collective-permute-done((bf16[256,1024]{1,0:T(8,128)(2,1)S(1)}, bf16[256,1024]{1,0:T(8,128)(2,1)S(1)}, u32[]{:S(2)}, u32[]{:S(2)}) %collective-permute-start.8) | collective-permute-done | bytes 524320 | tf_op jit(solution)/shard_map/ppermute | solution.py:42
  52.6 0.8 %shard_map.82 = (f32[1,1024]{1,0:T(1,128)S(1)}, f32[1,1024]{1,0:T(1,128)S(1)}) custom-call(bf16[128,1024]{1,0:T(8,128)(2,1)S(1)} %mix.10.state, f32[32,1024]{1,0:T(8,128)S(1)} %copy-done.2, bf16[1024,1024]{1,0:T(8,128)(2,1)S(1)} %get-tuple-element.18.refs_0_, bf16[1024,1024]{1,0:T(8,128)(2,1)S(1)} %get-tuple-element.19.refs_1_.refs_0_, ...), custom_call_target="tpu_custom_call" | custom-call | flops 402653184 | bytes 4194304 | tf_op jit(solution)/shard_map/pallas_call | solution.py:276
  53.4 2.4 %collective-permute-done.6.theirs = bf16[128,1024]{1,0:T(8,128)(2,1)S(1)} collective-permute-done((bf16[128,1024]{1,0:T(8,128)(2,1)S(1)}, bf16[128,1024]{1,0:T(8,128)(2,1)S(1)}, u32[]{:S(2)}, u32[]{:S(2)}) %collective-permute-start.6) | collective-permute-done | bytes 262176 | tf_op jit(solution)/shard_map/ppermute | solution.py:42
  55.7 0.7 %mix.11.state = bf16[128,1024]{1,0:T(8,128)(2,1)S(1)} custom-call(bf16[128,1024]{1,0:T(8,128)(2,1)S(1)} %mix.9.refs_0_.mine, bf16[128,1024]{1,0:T(8,128)(2,1)S(1)} %collective-permute-done.6.theirs, bf16[1024,1024]{1,0:T(8,128)(2,1)S(1)} %shard_map.79.refs_0_.near, bf16[1024,1024]{1,0:T(8,128)(2,1)S(1)} %shard_map.80.refs_0_.far, ...), custom_call_target="tpu_custom_call" | custom-call | flops 377487360 | bytes 4194304 | tf_op jit(solution)/shard_map/mix/pallas_call | solution.py:239
  57.0 1.2 %collective-permute-start.9 = (f32[1,1024]{1,0:T(1,128)S(1)}, f32[1,1024]{1,0:T(1,128)S(1)}, u32[]{:S(2)}, u32[]{:S(2)}) collective-permute-start(f32[1,1024]{1,0:T(1,128)S(1)} %shard_map.83.refs_3_), channel_id=1, source_target_pairs={{0,8},{1,9},{2,10},{3,11},{4,12},{5,13},{6,14},{7,15},{8,0},{9,1},... | collective-permute-start | bytes 12296 | tf_op jit(solution)/shard_map/ppermute | solution.py:42
  58.6 2.9 %collective-permute-done.9 = f32[1,1024]{1,0:T(1,128)S(1)} collective-permute-done((f32[1,1024]{1,0:T(1,128)S(1)}, f32[1,1024]{1,0:T(1,128)S(1)}, u32[]{:S(2)}, u32[]{:S(2)}) %collective-permute-start.9) | collective-permute-done | bytes 4128 | tf_op jit(solution)/shard_map/ppermute | solution.py:42
  61.5 0.6 add.11
  (19 shorter events, 1.4 us)
Async XLA Ops:
  0.9 3.7 %collective-permute-start = (bf16[256,128]{1,0:T(8,128)(2,1)S(1)}, bf16[256,128]{1,0:T(8,128)(2,1)S(1)}, u32[]{:S(2)}, u32[]{:S(2)}) collective-permute-start(bf16[256,128]{1,0:T(8,128)(2,1)S(1)} %get-tuple-element.24), channel_id=1, source_target_pairs={{0,1},{1,0},{2,3},{3,2},{4,5},{5,4},{6,7},{7,6},{8,9},{9,8},{10,11... | collective-permute-start | bytes 196616 | tf_op jit(solution)/shard_map/ppermute | solution.py:42
  1.4 3.1 %collective-permute-start.1 = (bf16[256,128]{1,0:T(8,128)(2,1)S(1)}, bf16[256,128]{1,0:T(8,128)(2,1)S(1)}, u32[]{:S(2)}, u32[]{:S(2)}) collective-permute-start(bf16[256,128]{1,0:T(8,128)(2,1)S(1)} %get-tuple-element.23), channel_id=1, source_target_pairs={{1,2},{2,1},{3,4},{4,3},{5,6},{6,5},{7,8},{8,7},{9,10},{10,9},{11,... | collective-permute-start | bytes 196616 | tf_op jit(solution)/shard_map/ppermute | solution.py:38
  2.1 5.6 %copy-start.3 = (bf16[256,1024]{1,0:T(8,128)(2,1)S(1)}, bf16[256,1024]{1,0:T(8,128)(2,1)}, u32[]{:S(2)}) copy-start(bf16[256,1024]{1,0:T(8,128)(2,1)} %wave.3) | copy-start | bytes 1572868
  2.1 5.6 %copy-start.4 = (f32[256,65]{0,1:T(8,128)S(1)}, f32[256,65]{0,1:T(8,128)}, u32[]{:S(2)}) copy-start(f32[256,65]{0,1:T(8,128)} %param.8) | copy-start | bytes 199684
  4.6 0.9 %copy-start.1 = (f32[32,1024]{1,0:T(8,128)S(1)}, f32[32,1024]{1,0:T(8,128)}, u32[]{:S(2)}) copy-start(f32[32,1024]{1,0:T(8,128)} %get-tuple-element.17.coords) | copy-start | bytes 393220
  7.7 6.9 %copy-start.2 = (f32[32,1024]{1,0:T(8,128)S(1)}, f32[32,1024]{1,0:T(8,128)}, u32[]{:S(2)}) copy-start(f32[32,1024]{1,0:T(8,128)} %get-tuple-element.17.coords) | copy-start | bytes 393220
  10.7 6.1 %collective-permute-start.2 = (bf16[128,1024]{1,0:T(8,128)(2,1)S(1)}, bf16[128,1024]{1,0:T(8,128)(2,1)S(1)}, u32[]{:S(2)}, u32[]{:S(2)}) collective-permute-start(bf16[128,1024]{1,0:T(8,128)(2,1)S(1)} %shard_map.74.refs_0_.mine), channel_id=1, source_target_pairs={{0,1},{1,0},{2,3},{3,2},{4,5},{5,4},{6,7},{7,6},{8,9},{9,8},{10,11... | collective-permute-start | bytes 786440 | tf_op jit(solution)/shard_map/ppermute | solution.py:42
  20.5 4.8 %collective-permute-start.3 = (bf16[128,1024]{1,0:T(8,128)(2,1)S(1)}, bf16[128,1024]{1,0:T(8,128)(2,1)S(1)}, u32[]{:S(2)}, u32[]{:S(2)}) collective-permute-start(bf16[128,1024]{1,0:T(8,128)(2,1)S(1)} %shard_map.76.refs_0_.mine), channel_id=1, source_target_pairs={{0,1},{1,0},{2,3},{3,2},{4,5},{5,4},{6,7},{7,6},{8,9},{9,8},{10,11... | collective-permute-start | bytes 786440 | tf_op jit(solution)/shard_map/ppermute | solution.py:42
  20.6 10.9 %collective-permute-start.5 = (bf16[128,1024]{1,0:T(8,128)(2,1)S(1)}, bf16[128,1024]{1,0:T(8,128)(2,1)S(1)}, u32[]{:S(2)}, u32[]{:S(2)}) collective-permute-start(bf16[128,1024]{1,0:T(8,128)(2,1)S(1)} %mix.6.refs_0_.mine), channel_id=1, source_target_pairs={{0,2},{1,3},{2,0},{3,1},{4,6},{5,7},{6,4},{7,5},{8,10},{9,11},{10,... | collective-permute-start | bytes 786440 | tf_op jit(solution)/shard_map/ppermute | solution.py:42
  25.3 1.0 %copy-start = (bf16[256,1024]{1,0:T(8,128)(2,1)S(1)}, bf16[256,1024]{1,0:T(8,128)(2,1)}, u32[]{:S(2)}) copy-start(bf16[256,1024]{1,0:T(8,128)(2,1)} %get-tuple-element.20.refs_2_.refs_1_) | copy-start | bytes 1572868
  26.1 10.0 %collective-permute-start.4 = (bf16[128,1024]{1,0:T(8,128)(2,1)S(1)}, bf16[128,1024]{1,0:T(8,128)(2,1)S(1)}, u32[]{:S(2)}, u32[]{:S(2)}) collective-permute-start(bf16[128,1024]{1,0:T(8,128)(2,1)S(1)} %mix.7.refs_0_.mine), channel_id=1, source_target_pairs={{0,2},{1,3},{2,0},{3,1},{4,6},{5,7},{6,4},{7,5},{8,10},{9,11},{10,... | collective-permute-start | bytes 786440 | tf_op jit(solution)/shard_map/ppermute | solution.py:42
  26.4 26.2 %collective-permute-start.8 = (bf16[256,1024]{1,0:T(8,128)(2,1)S(1)}, bf16[256,1024]{1,0:T(8,128)(2,1)S(1)}, u32[]{:S(2)}, u32[]{:S(2)}) collective-permute-start(bf16[256,1024]{1,0:T(8,128)(2,1)S(1)} %copy-done), channel_id=1, source_target_pairs={{0,8},{1,9},{2,10},{3,11},{4,12},{5,13},{6,14},{7,15},{8,0},{9,1},... | collective-permute-start | bytes 1572872 | tf_op jit(solution)/shard_map/ppermute | solution.py:42
  32.2 15.0 %collective-permute-start.7 = (bf16[128,1024]{1,0:T(8,128)(2,1)S(1)}, bf16[128,1024]{1,0:T(8,128)(2,1)S(1)}, u32[]{:S(2)}, u32[]{:S(2)}) collective-permute-start(bf16[128,1024]{1,0:T(8,128)(2,1)S(1)} %mix.8.refs_0_.mine), channel_id=1, source_target_pairs={{0,4},{1,5},{2,6},{3,7},{4,0},{5,1},{6,2},{7,3},{8,12},{9,13},{10,... | collective-permute-start | bytes 786440 | tf_op jit(solution)/shard_map/ppermute | solution.py:42
  36.8 18.9 %collective-permute-start.6 = (bf16[128,1024]{1,0:T(8,128)(2,1)S(1)}, bf16[128,1024]{1,0:T(8,128)(2,1)S(1)}, u32[]{:S(2)}, u32[]{:S(2)}) collective-permute-start(bf16[128,1024]{1,0:T(8,128)(2,1)S(1)} %mix.9.refs_0_.mine), channel_id=1, source_target_pairs={{0,4},{1,5},{2,6},{3,7},{4,0},{5,1},{6,2},{7,3},{8,12},{9,13},{10,... | collective-permute-start | bytes 786440 | tf_op jit(solution)/shard_map/ppermute | solution.py:42
  57.0 4.6 %collective-permute-start.9 = (f32[1,1024]{1,0:T(1,128)S(1)}, f32[1,1024]{1,0:T(1,128)S(1)}, u32[]{:S(2)}, u32[]{:S(2)}) collective-permute-start(f32[1,1024]{1,0:T(1,128)S(1)} %shard_map.83.refs_3_), channel_id=1, source_target_pairs={{0,8},{1,9},{2,10},{3,11},{4,12},{5,13},{6,14},{7,15},{8,0},{9,1},... | collective-permute-start | bytes 12296 | tf_op jit(solution)/shard_map/ppermute | solution.py:42

commit v5 on v4

--- a/solution.py
+++ b/solution.py
@@ -149,7 +149,7 @@
     for (row, column, below), out in zip(jobs, outs):
         fill(0, row, 0)
 
-        @pl.loop(0, steps)
+        @pl.loop(0, steps, unroll=2)
         def _(i):
             at = pl.ds(pl.multiple_of(i * step, step), step)
             part = rows[i % 2]
@@ -324,17 +324,13 @@
         theirs.append(partner(ahead, "space", 1 + block_bits))
     second += tables(1, (1,), coords, ahead)
     ahead = second[-1]
-    third = []
     for part in parts:
         states[part] = mix(states[part], theirs[part], *second, ahead)
         ahead = states[part]
         theirs[part] = partner(ahead, "space", 2 + block_bits)
         if part == 0:
-            third += tables(2, (0,), coords, ahead)
-            ahead = third[-1]
-        if part == end:
-            third += tables(2, (1,), coords, ahead)
-            ahead = third[-1]
+            third = tables(2, (0, 1), coords, ahead)
+            ahead = third[0]
     later = tables(3, (0, 1), coords, ahead)
     ahead = later[0]
     for part in parts:

time: 62.4 us -> 62.1 us (level)
  waiting for transfers between devices: 12.6 us -> 14.3 us
  starting transfers between devices: 14.9 us -> 13.4 us
    ppermute x9, waiting for transfers between devices: 12.6 us -> 14.3 us  [partner(): lax.ppermute(shard, axis, [(i, i ^ 1 << bit) for i in range(lax.axis_size...]
    ppermute x9, starting transfers between devices: 14.2 us -> 12.7 us  [partner(): lax.ppermute(shard, axis, [(i, i ^ 1 << bit) for i in range(lax.axis_size...]
    pallas_call x7 -> x6, Pallas kernels: 17.3 us -> 17 us  [tables(): pl.pallas_call(functools.partial(tables_kernel, jobs, step), out_shape=(s...]
  transfers between devices with their start and end apart: 10 -> 10, of which waited for: 4 -> 3; matrix products, arithmetic and copies ran while one was open for 0% -> 0% of each run, Pallas kernels for 35% -> 35%
where the time goes in v5:
time: 62.1 us; the launch traced here: 61.9 us
  Pallas kernels  31.6 us (51%)
  waiting for transfers between devices  14.3 us (23%)
  starting transfers between devices  13.4 us (22%)
  other arithmetic  1.48 us (2%)
  local copies, waits for them, and re-layouts  0.92 us (1%)
    pallas_call x6, Pallas kernels, tables(): pl.pallas_call(functools.partial(tables_kernel, jobs, step), out_shape=(s...  17 us
    ppermute x9, waiting for transfers between devices, partner(): lax.ppermute(shard, axis, [(i, i ^ 1 << bit) for i in range(lax.axis_size...  14.3 us
    ppermute x9, starting transfers between devices, partner(): lax.ppermute(shard, axis, [(i, i ^ 1 << bit) for i in range(lax.axis_size...  12.7 us
    pallas_call x2, Pallas kernels, redatum(): pl.pallas_call(functools.partial(redatum_kernel, reach, blocks, part), ou...  5.97 us
    pallas_call x6, Pallas kernels, mix(): pl.pallas_call(mix_kernel, out_shape=jax.ShapeDtypeStruct((count, width),...  4.45 us
    pallas_call x1, Pallas kernels, prepare(): pl.pallas_call(functools.partial(prepare_kernel, blocks, count, width), o...  2.41 us
    pallas_call x3, Pallas kernels, last(): pl.pallas_call(functools.partial(last_kernel, part, weights, len(sums)),...  1.76 us
  transfers between devices with their start and end apart: 10, of which 3 were waited for; matrix products, arithmetic and copies ran while one was open for 0% of the time, Pallas kernels for 35%

profile of v5, /device:TPU:0, one launch (start us, length us, event | category | flops | bytes accessed | tf_op | source)
XLA Modules:
  0.0 61.9 jit_solution(9963608159633150026)
XLA Ops:
  0.0 0.9 %broadcast_select_fusion = (bf16[256,128]{1,0:T(8,128)(2,1)S(1)}, bf16[256,128]{1,0:T(8,128)(2,1)S(1)}) fusion(pred[]{:T(512)S(6)} %eq.6, bf16[256,1024]{1,0:T(8,128)(2,1)} %wave.3), kind=kLoop, calls=%fused_computation | loop fusion | flops 65536 | bytes 262145 | tf_op jit(solution)/shard_map/jit(_where)/select_n | solution.py:296
  0.9 0.6 collective-permute-start
  1.4 0.7 %collective-permute-start.1 = (bf16[256,128]{1,0:T(8,128)(2,1)S(1)}, bf16[256,128]{1,0:T(8,128)(2,1)S(1)}, u32[]{:S(2)}, u32[]{:S(2)}) collective-permute-start(bf16[256,128]{1,0:T(8,128)(2,1)S(1)} %get-tuple-element.27), channel_id=1, source_target_pairs={{1,2},{2,1},{3,4},{4,3},{5,6},{6,5},{7,8},{8,7},{9,10},{10,9},{11,... | collective-permute-start | bytes 196616 | tf_op jit(solution)/shard_map/ppermute | solution.py:38
  2.1 2.4 %prepare.1 = (bf16[256,1024]{1,0:T(8,128)(2,1)}, f32[32,1024]{1,0:T(8,128)}) custom-call(s32[256,1024]{1,0:T(8,128)} %aperture.1, s32[5,16384]{1,0:T(8,128)} %cell_x.1, s32[128,128]{1,0:T(8,128)} %bitcast.5, f32[128,128]{1,0:T(8,128)} %bitcast.6, f32[4]{0:T(128)} %slowness.1), custom_call_target="tpu_custom_call" | custom-call | flops 754974720 | bytes 2097152 | tf_op jit(solution)/shard_map/prepare/pallas_call | solution.py:118
  4.6 0.9 %copy-done.1 = f32[32,1024]{1,0:T(8,128)S(1)} copy-done((f32[32,1024]{1,0:T(8,128)S(1)}, f32[32,1024]{1,0:T(8,128)}, u32[]{:S(2)}) %copy-start.1) | copy-done | bytes 131096
  5.5 2.1 %shard_map.73.refs_0_.near = bf16[1024,1024]{1,0:T(8,128)(2,1)S(1)} custom-call(f32[32,1024]{1,0:T(8,128)S(1)} %copy-done.1, bf16[256,128]{1,0:T(8,128)(2,1)S(1)} %collective-permute-done.refs_0_.near_edge), custom_call_target="tpu_custom_call" | custom-call | flops 1006632960 | bytes 2097152 | tf_op jit(solution)/shard_map/pallas_call | solution.py:175
  7.7 3.0 %shard_map.74.refs_0_.mine = bf16[128,1024]{1,0:T(8,128)(2,1)S(1)} custom-call(bf16[256,128]{1,0:T(8,128)(2,1)S(1)} %collective-permute-done.refs_0_.near_edge, bf16[256,1024]{1,0:T(8,128)(2,1)S(1)} %copy-done.3, bf16[256,128]{1,0:T(8,128)(2,1)S(1)} %collective-permute-done.1.far_edge, f32[65,256]{1,0:T(8,128)S(1)} %bitcast.3, ...), custom_call_target="tpu_custom_call" | custom-call | flops 1509949440 | bytes 524288 | tf_op jit(solution)/shard_map/pallas_call | solution.py:214
  10.6 3.9 %collective-permute-start.2 = (bf16[128,1024]{1,0:T(8,128)(2,1)S(1)}, bf16[128,1024]{1,0:T(8,128)(2,1)S(1)}, u32[]{:S(2)}, u32[]{:S(2)}) collective-permute-start(bf16[128,1024]{1,0:T(8,128)(2,1)S(1)} %shard_map.74.refs_0_.mine), channel_id=1, source_target_pairs={{0,1},{1,0},{2,3},{3,2},{4,5},{5,4},{6,7},{7,6},{8,9},{9,8},{10,11... | collective-permute-start | bytes 786440 | tf_op jit(solution)/shard_map/ppermute | solution.py:42
  14.6 2.1 %shard_map.75.far.refs_0_ = bf16[1024,1024]{1,0:T(8,128)(2,1)S(1)} custom-call(f32[32,1024]{1,0:T(8,128)S(1)} %copy-done.2, bf16[128,1024]{1,0:T(8,128)(2,1)S(1)} %shard_map.74.refs_0_.mine), custom_call_target="tpu_custom_call" | custom-call | flops 1006632960 | bytes 2097152 | tf_op jit(solution)/shard_map/pallas_call | solution.py:175
  16.7 0.7 %mix.6.refs_0_.mine = bf16[128,1024]{1,0:T(8,128)(2,1)S(1)} custom-call(bf16[128,1024]{1,0:T(8,128)(2,1)S(1)} %shard_map.74.refs_0_.mine, bf16[128,1024]{1,0:T(8,128)(2,1)S(1)} %collective-permute-done.2.theirs, bf16[1024,1024]{1,0:T(8,128)(2,1)S(1)} %shard_map.73.refs_0_.near, bf16[1024,1024]{1,0:T(8,128)(2,1)S(1)} %shard_map.75.far.refs_0_, ...), custom_call_target="tpu_custom_call" | custom-call | flops 377487360 | bytes 4194304 | tf_op jit(solution)/shard_map/mix/pallas_call | solution.py:239
  17.5 3.0 %shard_map.76.refs_0_.mine = bf16[128,1024]{1,0:T(8,128)(2,1)S(1)} custom-call(bf16[256,128]{1,0:T(8,128)(2,1)S(1)} %collective-permute-done.refs_0_.near_edge, bf16[256,1024]{1,0:T(8,128)(2,1)S(1)} %copy-done.3, bf16[256,128]{1,0:T(8,128)(2,1)S(1)} %collective-permute-done.1.far_edge, f32[65,256]{1,0:T(8,128)S(1)} %bitcast.4, ...), custom_call_target="tpu_custom_call" | custom-call | flops 1509949440 | bytes 524288 | tf_op jit(solution)/shard_map/pallas_call | solution.py:214
  20.6 2.5 %collective-permute-start.5 = (bf16[128,1024]{1,0:T(8,128)(2,1)S(1)}, bf16[128,1024]{1,0:T(8,128)(2,1)S(1)}, u32[]{:S(2)}, u32[]{:S(2)}) collective-permute-start(bf16[128,1024]{1,0:T(8,128)(2,1)S(1)} %mix.6.refs_0_.mine), channel_id=1, source_target_pairs={{0,2},{1,3},{2,0},{3,1},{4,6},{5,7},{6,4},{7,5},{8,10},{9,11},{10,... | collective-permute-start | bytes 786440 | tf_op jit(solution)/shard_map/ppermute | solution.py:42
  23.1 2.6 %collective-permute-start.8 = (bf16[256,1024]{1,0:T(8,128)(2,1)S(1)}, bf16[256,1024]{1,0:T(8,128)(2,1)S(1)}, u32[]{:S(2)}, u32[]{:S(2)}) collective-permute-start(bf16[256,1024]{1,0:T(8,128)(2,1)S(1)} %copy-done), channel_id=1, source_target_pairs={{0,8},{1,9},{2,10},{3,11},{4,12},{5,13},{6,14},{7,15},{8,0},{9,1},... | collective-permute-start | bytes 1572872 | tf_op jit(solution)/shard_map/ppermute | solution.py:42
  25.7 2.1 %shard_map.77.refs_0_.near = bf16[1024,1024]{1,0:T(8,128)(2,1)S(1)} custom-call(f32[32,1024]{1,0:T(8,128)S(1)} %copy-done.2, bf16[128,1024]{1,0:T(8,128)(2,1)S(1)} %shard_map.76.refs_0_.mine), custom_call_target="tpu_custom_call" | custom-call | flops 1006632960 | bytes 2097152 | tf_op jit(solution)/shard_map/pallas_call | solution.py:175
  27.8 0.7 %mix.7.refs_0_.mine = bf16[128,1024]{1,0:T(8,128)(2,1)S(1)} custom-call(bf16[128,1024]{1,0:T(8,128)(2,1)S(1)} %shard_map.76.refs_0_.mine, bf16[128,1024]{1,0:T(8,128)(2,1)S(1)} %collective-permute-done.3.theirs, bf16[1024,1024]{1,0:T(8,128)(2,1)S(1)} %shard_map.73.refs_0_.near, bf16[1024,1024]{1,0:T(8,128)(2,1)S(1)} %shard_map.75.far.refs_0_, ...), custom_call_target="tpu_custom_call" | custom-call | flops 377487360 | bytes 4194304 | tf_op jit(solution)/shard_map/mix/pallas_call | solution.py:239
  28.6 0.6 %collective-permute-start.4 = (bf16[128,1024]{1,0:T(8,128)(2,1)S(1)}, bf16[128,1024]{1,0:T(8,128)(2,1)S(1)}, u32[]{:S(2)}, u32[]{:S(2)}) collective-permute-start(bf16[128,1024]{1,0:T(8,128)(2,1)S(1)} %mix.7.refs_0_.mine), channel_id=1, source_target_pairs={{0,2},{1,3},{2,0},{3,1},{4,6},{5,7},{6,4},{7,5},{8,10},{9,11},{10,... | collective-permute-start | bytes 786440 | tf_op jit(solution)/shard_map/ppermute | solution.py:42
  29.2 2.1 %shard_map.78.far.refs_0_ = bf16[1024,1024]{1,0:T(8,128)(2,1)S(1)} custom-call(f32[32,1024]{1,0:T(8,128)S(1)} %copy-done.2, bf16[128,1024]{1,0:T(8,128)(2,1)S(1)} %mix.7.refs_0_.mine), custom_call_target="tpu_custom_call" | custom-call | flops 1006632960 | bytes 2097152 | tf_op jit(solution)/shard_map/pallas_call | solution.py:175
  31.4 0.8 %mix.8.refs_0_.mine = bf16[128,1024]{1,0:T(8,128)(2,1)S(1)} custom-call(bf16[128,1024]{1,0:T(8,128)(2,1)S(1)} %mix.6.refs_0_.mine, bf16[128,1024]{1,0:T(8,128)(2,1)S(1)} %collective-permute-done.5.theirs, bf16[1024,1024]{1,0:T(8,128)(2,1)S(1)} %shard_map.77.refs_0_.near, bf16[1024,1024]{1,0:T(8,128)(2,1)S(1)} %shard_map.78.far.refs_0_, ...), custom_call_target="tpu_custom_call" | custom-call | flops 377487360 | bytes 4194304 | tf_op jit(solution)/shard_map/mix/pallas_call | solution.py:239
  32.1 1.6 %collective-permute-start.7 = (bf16[128,1024]{1,0:T(8,128)(2,1)S(1)}, bf16[128,1024]{1,0:T(8,128)(2,1)S(1)}, u32[]{:S(2)}, u32[]{:S(2)}) collective-permute-start(bf16[128,1024]{1,0:T(8,128)(2,1)S(1)} %mix.8.refs_0_.mine), channel_id=1, source_target_pairs={{0,4},{1,5},{2,6},{3,7},{4,0},{5,1},{6,2},{7,3},{8,12},{9,13},{10,... | collective-permute-start | bytes 786440 | tf_op jit(solution)/shard_map/ppermute | solution.py:42
  33.8 4.3 %shard_map.79 = (bf16[1024,1024]{1,0:T(8,128)(2,1)S(1)}, bf16[1024,1024]{1,0:T(8,128)(2,1)S(1)}) custom-call(f32[32,1024]{1,0:T(8,128)S(1)} %copy-done.2, bf16[128,1024]{1,0:T(8,128)(2,1)S(1)} %mix.8.refs_0_.mine), custom_call_target="tpu_custom_call" | custom-call | flops 2013265920 | bytes 4194304 | tf_op jit(solution)/shard_map/pallas_call | solution.py:175
  38.0 0.7 %mix.9.refs_0_.mine = bf16[128,1024]{1,0:T(8,128)(2,1)S(1)} custom-call(bf16[128,1024]{1,0:T(8,128)(2,1)S(1)} %mix.7.refs_0_.mine, bf16[128,1024]{1,0:T(8,128)(2,1)S(1)} %collective-permute-done.4.theirs, bf16[1024,1024]{1,0:T(8,128)(2,1)S(1)} %shard_map.77.refs_0_.near, bf16[1024,1024]{1,0:T(8,128)(2,1)S(1)} %shard_map.78.far.refs_0_, ...), custom_call_target="tpu_custom_call" | custom-call | flops 377487360 | bytes 4194304 | tf_op jit(solution)/shard_map/mix/pallas_call | solution.py:239
  38.8 0.5 collective-permute-start.6
  39.3 4.3 %shard_map.80 = (bf16[1024,1024]{1,0:T(8,128)(2,1)S(1)}, bf16[1024,1024]{1,0:T(8,128)(2,1)S(1)}) custom-call(f32[32,1024]{1,0:T(8,128)S(1)} %copy-done.2, bf16[128,1024]{1,0:T(8,128)(2,1)S(1)} %mix.9.refs_0_.mine), custom_call_target="tpu_custom_call" | custom-call | flops 2013265920 | bytes 4194304 | tf_op jit(solution)/shard_map/pallas_call | solution.py:175
  43.6 6.9 %collective-permute-done.7.theirs = bf16[128,1024]{1,0:T(8,128)(2,1)S(1)} collective-permute-done((bf16[128,1024]{1,0:T(8,128)(2,1)S(1)}, bf16[128,1024]{1,0:T(8,128)(2,1)S(1)}, u32[]{:S(2)}, u32[]{:S(2)}) %collective-permute-start.7) | collective-permute-done | bytes 262176 | tf_op jit(solution)/shard_map/ppermute | solution.py:42
  50.5 0.7 %mix.10.state = bf16[128,1024]{1,0:T(8,128)(2,1)S(1)} custom-call(bf16[128,1024]{1,0:T(8,128)(2,1)S(1)} %mix.8.refs_0_.mine, bf16[128,1024]{1,0:T(8,128)(2,1)S(1)} %collective-permute-done.7.theirs, bf16[1024,1024]{1,0:T(8,128)(2,1)S(1)} %get-tuple-element.20.refs_0_.near, bf16[1024,1024]{1,0:T(8,128)(2,1)S(1)} %get-tuple-element.21.far, ...), custom_call_target="tpu_custom_call" | custom-call | flops 377487360 | bytes 4194304 | tf_op jit(solution)/shard_map/mix/pallas_call | solution.py:239
  51.2 0.8 %shard_map.81 = (f32[1,1024]{1,0:T(1,128)S(1)}, f32[1,1024]{1,0:T(1,128)S(1)}) custom-call(bf16[128,1024]{1,0:T(8,128)(2,1)S(1)} %mix.10.state, f32[32,1024]{1,0:T(8,128)S(1)} %copy-done.2, bf16[1024,1024]{1,0:T(8,128)(2,1)S(1)} %get-tuple-element.22.refs_0_, bf16[1024,1024]{1,0:T(8,128)(2,1)S(1)} %get-tuple-element.23.refs_1_.refs_0_, ...), custom_call_target="tpu_custom_call" | custom-call | flops 402653184 | bytes 4194304 | tf_op jit(solution)/shard_map/pallas_call | solution.py:276
  52.0 3.5 %collective-permute-done.6.theirs = bf16[128,1024]{1,0:T(8,128)(2,1)S(1)} collective-permute-done((bf16[128,1024]{1,0:T(8,128)(2,1)S(1)}, bf16[128,1024]{1,0:T(8,128)(2,1)S(1)}, u32[]{:S(2)}, u32[]{:S(2)}) %collective-permute-start.6) | collective-permute-done | bytes 262176 | tf_op jit(solution)/shard_map/ppermute | solution.py:42
  55.5 0.7 %mix.11.state = bf16[128,1024]{1,0:T(8,128)(2,1)S(1)} custom-call(bf16[128,1024]{1,0:T(8,128)(2,1)S(1)} %mix.9.refs_0_.mine, bf16[128,1024]{1,0:T(8,128)(2,1)S(1)} %collective-permute-done.6.theirs, bf16[1024,1024]{1,0:T(8,128)(2,1)S(1)} %get-tuple-element.20.refs_0_.near, bf16[1024,1024]{1,0:T(8,128)(2,1)S(1)} %get-tuple-element.21.far, ...), custom_call_target="tpu_custom_call" | custom-call | flops 377487360 | bytes 4194304 | tf_op jit(solution)/shard_map/mix/pallas_call | solution.py:239
  56.3 0.5 shard_map.82.refs_3_
  57.0 0.5 shard_map.83
  57.5 3.9 %collective-permute-done.9 = f32[1,1024]{1,0:T(1,128)S(1)} collective-permute-done((f32[1,1024]{1,0:T(1,128)S(1)}, f32[1,1024]{1,0:T(1,128)S(1)}, u32[]{:S(2)}, u32[]{:S(2)}) %collective-permute-start.9) | collective-permute-done | bytes 4128 | tf_op jit(solution)/shard_map/ppermute | solution.py:42
  61.3 0.6 add.11
  (18 shorter events, 0.3 us)
Async XLA Ops:
  0.9 3.7 %collective-permute-start = (bf16[256,128]{1,0:T(8,128)(2,1)S(1)}, bf16[256,128]{1,0:T(8,128)(2,1)S(1)}, u32[]{:S(2)}, u32[]{:S(2)}) collective-permute-start(bf16[256,128]{1,0:T(8,128)(2,1)S(1)} %get-tuple-element.28), channel_id=1, source_target_pairs={{0,1},{1,0},{2,3},{3,2},{4,5},{5,4},{6,7},{7,6},{8,9},{9,8},{10,11... | collective-permute-start | bytes 196616 | tf_op jit(solution)/shard_map/ppermute | solution.py:42
  1.4 3.1 %collective-permute-start.1 = (bf16[256,128]{1,0:T(8,128)(2,1)S(1)}, bf16[256,128]{1,0:T(8,128)(2,1)S(1)}, u32[]{:S(2)}, u32[]{:S(2)}) collective-permute-start(bf16[256,128]{1,0:T(8,128)(2,1)S(1)} %get-tuple-element.27), channel_id=1, source_target_pairs={{1,2},{2,1},{3,4},{4,3},{5,6},{6,5},{7,8},{8,7},{9,10},{10,9},{11,... | collective-permute-start | bytes 196616 | tf_op jit(solution)/shard_map/ppermute | solution.py:38
  2.1 5.5 %copy-start.3 = (bf16[256,1024]{1,0:T(8,128)(2,1)S(1)}, bf16[256,1024]{1,0:T(8,128)(2,1)}, u32[]{:S(2)}) copy-start(bf16[256,1024]{1,0:T(8,128)(2,1)} %wave.3) | copy-start | bytes 1572868
  2.1 5.5 %copy-start.4 = (f32[256,65]{0,1:T(8,128)S(1)}, f32[256,65]{0,1:T(8,128)}, u32[]{:S(2)}) copy-start(f32[256,65]{0,1:T(8,128)} %param.8) | copy-start | bytes 199684
  4.6 0.9 %copy-start.1 = (f32[32,1024]{1,0:T(8,128)S(1)}, f32[32,1024]{1,0:T(8,128)}, u32[]{:S(2)}) copy-start(f32[32,1024]{1,0:T(8,128)} %get-tuple-element.19.coords) | copy-start | bytes 393220
  7.6 6.9 %copy-start.2 = (f32[32,1024]{1,0:T(8,128)S(1)}, f32[32,1024]{1,0:T(8,128)}, u32[]{:S(2)}) copy-start(f32[32,1024]{1,0:T(8,128)} %get-tuple-element.19.coords) | copy-start | bytes 393220
  10.6 6.1 %collective-permute-start.2 = (bf16[128,1024]{1,0:T(8,128)(2,1)S(1)}, bf16[128,1024]{1,0:T(8,128)(2,1)S(1)}, u32[]{:S(2)}, u32[]{:S(2)}) collective-permute-start(bf16[128,1024]{1,0:T(8,128)(2,1)S(1)} %shard_map.74.refs_0_.mine), channel_id=1, source_target_pairs={{0,1},{1,0},{2,3},{3,2},{4,5},{5,4},{6,7},{7,6},{8,9},{9,8},{10,11... | collective-permute-start | bytes 786440 | tf_op jit(solution)/shard_map/ppermute | solution.py:42
  17.5 5.6 %copy-start = (bf16[256,1024]{1,0:T(8,128)(2,1)S(1)}, bf16[256,1024]{1,0:T(8,128)(2,1)}, u32[]{:S(2)}) copy-start(bf16[256,1024]{1,0:T(8,128)(2,1)} %get-tuple-element.24.refs_2_.refs_1_) | copy-start | bytes 1572868
  20.5 7.3 %collective-permute-start.3 = (bf16[128,1024]{1,0:T(8,128)(2,1)S(1)}, bf16[128,1024]{1,0:T(8,128)(2,1)S(1)}, u32[]{:S(2)}, u32[]{:S(2)}) collective-permute-start(bf16[128,1024]{1,0:T(8,128)(2,1)S(1)} %shard_map.76.refs_0_.mine), channel_id=1, source_target_pairs={{0,1},{1,0},{2,3},{3,2},{4,5},{5,4},{6,7},{7,6},{8,9},{9,8},{10,11... | collective-permute-start | bytes 786440 | tf_op jit(solution)/shard_map/ppermute | solution.py:42
  20.6 10.8 %collective-permute-start.5 = (bf16[128,1024]{1,0:T(8,128)(2,1)S(1)}, bf16[128,1024]{1,0:T(8,128)(2,1)S(1)}, u32[]{:S(2)}, u32[]{:S(2)}) collective-permute-start(bf16[128,1024]{1,0:T(8,128)(2,1)S(1)} %mix.6.refs_0_.mine), channel_id=1, source_target_pairs={{0,2},{1,3},{2,0},{3,1},{4,6},{5,7},{6,4},{7,5},{8,10},{9,11},{10,... | collective-permute-start | bytes 786440 | tf_op jit(solution)/shard_map/ppermute | solution.py:42
  23.1 28.1 %collective-permute-start.8 = (bf16[256,1024]{1,0:T(8,128)(2,1)S(1)}, bf16[256,1024]{1,0:T(8,128)(2,1)S(1)}, u32[]{:S(2)}, u32[]{:S(2)}) collective-permute-start(bf16[256,1024]{1,0:T(8,128)(2,1)S(1)} %copy-done), channel_id=1, source_target_pairs={{0,8},{1,9},{2,10},{3,11},{4,12},{5,13},{6,14},{7,15},{8,0},{9,1},... | collective-permute-start | bytes 1572872 | tf_op jit(solution)/shard_map/ppermute | solution.py:42
  28.6 9.5 %collective-permute-start.4 = (bf16[128,1024]{1,0:T(8,128)(2,1)S(1)}, bf16[128,1024]{1,0:T(8,128)(2,1)S(1)}, u32[]{:S(2)}, u32[]{:S(2)}) collective-permute-start(bf16[128,1024]{1,0:T(8,128)(2,1)S(1)} %mix.7.refs_0_.mine), channel_id=1, source_target_pairs={{0,2},{1,3},{2,0},{3,1},{4,6},{5,7},{6,4},{7,5},{8,10},{9,11},{10,... | collective-permute-start | bytes 786440 | tf_op jit(solution)/shard_map/ppermute | solution.py:42
  32.1 18.3 %collective-permute-start.7 = (bf16[128,1024]{1,0:T(8,128)(2,1)S(1)}, bf16[128,1024]{1,0:T(8,128)(2,1)S(1)}, u32[]{:S(2)}, u32[]{:S(2)}) collective-permute-start(bf16[128,1024]{1,0:T(8,128)(2,1)S(1)} %mix.8.refs_0_.mine), channel_id=1, source_target_pairs={{0,4},{1,5},{2,6},{3,7},{4,0},{5,1},{6,2},{7,3},{8,12},{9,13},{10,... | collective-permute-start | bytes 786440 | tf_op jit(solution)/shard_map/ppermute | solution.py:42
  38.8 16.7 %collective-permute-start.6 = (bf16[128,1024]{1,0:T(8,128)(2,1)S(1)}, bf16[128,1024]{1,0:T(8,128)(2,1)S(1)}, u32[]{:S(2)}, u32[]{:S(2)}) collective-permute-start(bf16[128,1024]{1,0:T(8,128)(2,1)S(1)} %mix.9.refs_0_.mine), channel_id=1, source_target_pairs={{0,4},{1,5},{2,6},{3,7},{4,0},{5,1},{6,2},{7,3},{8,12},{9,13},{10,... | collective-permute-start | bytes 786440 | tf_op jit(solution)/shard_map/ppermute | solution.py:42
  56.8 4.6 %collective-permute-start.9 = (f32[1,1024]{1,0:T(1,128)S(1)}, f32[1,1024]{1,0:T(1,128)S(1)}, u32[]{:S(2)}, u32[]{:S(2)}) collective-permute-start(f32[1,1024]{1,0:T(1,128)S(1)} %shard_map.82.refs_3_), channel_id=1, source_target_pairs={{0,8},{1,9},{2,10},{3,11},{4,12},{5,13},{6,14},{7,15},{8,0},{9,1},... | collective-permute-start | bytes 12296 | tf_op jit(solution)/shard_map/ppermute | solution.py:42
